TPU v7x, 32 devices: a whole 2x2x4 slice. The times are simulated.
32 devices in a mesh: cells: 16 (over z, y, x), faces: 2 (over core).
Axes of the slice: x: 2, y: 2, z: 4, core: 2. Of those that a mesh axis runs over, the one named last changes fastest.
Arguments:
- flow_state: float32 [4, 131072], P(None, 'cells'), may hold values from -6 to 6
- source_term: float32 [4, 131072], P(None, 'cells'), may hold values from -24 to 24
- volume_rate: float32 [131072], P('cells'), may hold values from 0.5 to 4
- face_normal: float32 [3, 393216], P(None, ('cells', 'faces')), may hold values from -3 to 3
- face_owner: int32 [393216], P(('cells', 'faces')), may hold values from 0 to 8191, as said below
- face_neighbour: int32 [393216], P(('cells', 'faces')), may hold values from 0 to 9727, as said below
- face_count: int32 [32], P(('cells', 'faces')), may hold values from 1536 to 12288, as said below
- send_list: int32 [96, 256], P('cells'), may hold values from 0 to 8191
- halo_count: int32 [96], P('cells'), may hold values from 64 to 256, as said below
Outputs:
- solution_field: float32 [4, 131072], P(None, 'cells')
- residual: float32 [4, 131072], P(None, 'cells')
Inputs may be any that keep to these rules, and one draw needn't show every extreme that they name: `face_owner`: A local cell of the slot's partition; with s = g mod 12288 and t = s // 192, it lies in 128 * t to 128 * t + 127. `face_neighbour`: with s and t as for face_owner: below 8192 a local cell (128 * t + d) mod 8192 with d in 0 to 255; otherwise 8192 plus a halo slot of the slot's partition in (t mod (6)) * 256 to that plus 256 - 1. Live slots of a block are its first face_count slots; in every draw some block has all 12288 slots live. `send_list`: entries at or past the list's count are unused. `halo_count`: every partition has one list with exactly 256 entries.
All inputs are finite; a program needn't handle non-finite values.
Results may differ from a plain program's by a relative error of at most 0.0003.
Values sent between devices are 32-bit elements; how exact they have to be, the bound alone decides.
No kernel may reach another device: no remote copies, remote signals or barrier semaphores. Data moves between devices by JAX's collectives and lax.ppermute only.
A program may use at most 64 MiB of HBM per device.

v0:
```python
import jax
import jax.numpy as jnp
import numpy as np
from jax import lax
from jax.sharding import PartitionSpec as P

ITERS = 2


def passed_along(block, axis, distance):
    devices = range(lax.axis_size(axis))
    route = [((i - distance) % len(devices), i) for i in devices]
    return lax.ppermute(block, axis, route)


def offsets(count):
    return [which + 1 for which in range(count)] + [-(which + 1) for which in range(count)]


def body(
    flow_state,
    source_term,
    volume_rate,
    face_normal,
    face_owner,
    face_neighbour,
    face_count,
    send_list,
    halo_count,
):
    highest = lax.Precision.HIGHEST
    cells_here = flow_state.shape[1]
    list_total, slot_width = send_list.shape
    shift_list = offsets(list_total // 2)
    slot_ids = lax.broadcasted_iota(jnp.int32, (list_total, slot_width), 1)
    keep_mask = (slot_ids < halo_count[:, None]).astype(jnp.float32)
    tiles = cells_here // 128
    slot_total = face_owner.shape[0]
    per_tile = slot_total // tiles
    halo_total = list_total * slot_width
    window = max(slot_width, halo_total // tiles)
    window_count = halo_total // window
    window_pick = np.arange(tiles) % window_count
    tile_ids = lax.broadcasted_iota(jnp.int32, (tiles, per_tile), 0)
    owner_tiled = face_owner.reshape(tiles, per_tile)
    neighbour_tiled = face_neighbour.reshape(tiles, per_tile)
    is_local_tiled = neighbour_tiled < cells_here
    owner_column = owner_tiled - tile_ids * 128
    local_column = jnp.where(is_local_tiled, (neighbour_tiled - tile_ids * 128) % cells_here, -1)
    halo_column = jnp.where(
        is_local_tiled, -1, neighbour_tiled - cells_here - tile_ids % window_count * window
    )
    owner_hot = (
        owner_column[:, :, None] == lax.broadcasted_iota(jnp.int32, (1, 1, 128), 2)
    ).astype(jnp.float32)
    local_hot = (
        local_column[:, :, None] == lax.broadcasted_iota(jnp.int32, (1, 1, 256), 2)
    ).astype(jnp.float32)
    halo_hot = (
        halo_column[:, :, None] == lax.broadcasted_iota(jnp.int32, (1, 1, window), 2)
    ).astype(jnp.float32)
    is_live = (
        lax.broadcasted_iota(jnp.int32, (tiles, per_tile), 0) * per_tile
        + lax.broadcasted_iota(jnp.int32, (tiles, per_tile), 1)
        < face_count[0]
    ).astype(jnp.float32)
    local_weight = is_local_tiled.astype(jnp.float32)
    normal_tiled = face_normal.reshape(3, tiles, per_tile)

    def ghosts(vector_in):
        outgoing = (
            jnp.stack(
                [jnp.take(vector_in, send_list[which], axis=1) for which in range(list_total)]
            )
            * keep_mask[:, None, :]
        )
        incoming = jnp.stack(
            [
                passed_along(outgoing[which], "cells", shift_list[which])
                for which in range(list_total)
            ]
        )
        return jnp.transpose(incoming, (1, 0, 2)).reshape(vector_in.shape[0], halo_total)

    def to_faces(vector_in):
        rows = vector_in.shape[0]
        blocks = vector_in.reshape(rows, tiles, 128)
        paired = jnp.concatenate([blocks, jnp.roll(blocks, -1, axis=1)], axis=2)
        halo_cells = ghosts(vector_in)
        halo_windows = halo_cells.reshape(rows, window_count, window)[:, window_pick]
        left_side = jnp.einsum("tfc,btc->btf", owner_hot, blocks, precision=highest)
        right_side = jnp.einsum("tfc,btc->btf", local_hot, paired, precision=highest)
        right_side = right_side + jnp.einsum(
            "tfc,btc->btf", halo_hot, halo_windows, precision=highest
        )
        return (left_side, right_side)

    def to_cells(owner_values, neighbour_values):
        rows = owner_values.shape[0]
        owned = jnp.einsum("tfc,btf->btc", owner_hot, owner_values, precision=highest)
        beside = jnp.einsum("tfc,btf->btc", local_hot, neighbour_values, precision=highest)
        summed = owned + beside[:, :, :128] + jnp.roll(beside[:, :, 128:], 1, axis=1)
        return summed.reshape(rows, cells_here)

    left_state, right_state = to_faces(flow_state)
    normal_speed = 0.5 * jnp.sum(normal_tiled * (left_state[:3] + right_state[:3]), axis=0)
    normal_size = jnp.sqrt(jnp.sum(normal_tiled * normal_tiled, axis=0))
    wave_speed = jnp.abs(normal_speed) + 2.0 * normal_size
    owner_terms = (
        0.5
        * jnp.concatenate([normal_speed[None], normal_tiled, wave_speed[None]], axis=0)
        * is_live
    )
    neighbour_terms = jnp.concatenate(
        [-0.5 * normal_speed[None], -0.5 * normal_tiled, 0.5 * wave_speed[None]], axis=0
    ) * (is_live * local_weight)
    block_terms = lax.psum(to_cells(owner_terms, neighbour_terms), "faces")
    velocity_diag = volume_rate + block_terms[0] + block_terms[4]
    pressure_diag = volume_rate + block_terms[4]
    coupling = block_terms[1:4]
    schur = pressure_diag - jnp.sum(coupling * coupling, axis=0) / velocity_diag

    def precondition(vector_in):
        pressure = (
            vector_in[3] - jnp.sum(coupling * vector_in[:3], axis=0) / velocity_diag
        ) / schur
        velocity = (vector_in[:3] - coupling * pressure) / velocity_diag
        return jnp.concatenate([velocity, pressure[None]], axis=0)

    def apply_matrix(vector_in):
        left_side, right_side = to_faces(vector_in)
        face_sum = left_side + right_side
        central = jnp.concatenate(
            [
                normal_speed * face_sum[:3] + normal_tiled * face_sum[3],
                jnp.sum(normal_tiled * face_sum[:3], axis=0)[None],
            ],
            axis=0,
        )
        face_flux = (0.5 * central - 0.5 * wave_speed * (right_side - left_side)) * is_live
        partial_value = to_cells(face_flux, -face_flux * local_weight)
        return volume_rate * vector_in + lax.psum(partial_value, "faces")

    solution_field = jnp.zeros_like(source_term)
    residual = source_term
    direction = source_term
    rho_now = lax.psum(jnp.sum(source_term * residual), "cells")
    for iteration in range(ITERS):
        pre_dir = precondition(direction)
        image = apply_matrix(pre_dir)
        step_alpha = rho_now / lax.psum(jnp.sum(source_term * image), "cells")
        middle = residual - step_alpha * image
        pre_mid = precondition(middle)
        second = apply_matrix(pre_mid)
        second_mid, second_sq, shadow_mid, shadow_second = lax.psum(
            (
                jnp.sum(second * middle),
                jnp.sum(second * second),
                jnp.sum(source_term * middle),
                jnp.sum(source_term * second),
            ),
            "cells",
        )
        step_omega = second_mid / second_sq
        solution_field = solution_field + step_alpha * pre_dir + step_omega * pre_mid
        residual = middle - step_omega * second
        rho_next = shadow_mid - step_omega * shadow_second
        if iteration + 1 < ITERS:
            ratio_beta = rho_next / rho_now * (step_alpha / step_omega)
            direction = residual + ratio_beta * (direction - step_omega * image)
            rho_now = rho_next
    return (solution_field, residual)


def solution(mesh):
    in_specs = (
        P(None, "cells"),
        P(None, "cells"),
        P("cells"),
        P(None, ("cells", "faces")),
        P(("cells", "faces")),
        P(("cells", "faces")),
        P(("cells", "faces")),
        P("cells", None),
        P("cells"),
    )
    out_specs = (P(None, "cells"), P(None, "cells"))
    return jax.shard_map(body, mesh=mesh, in_specs=in_specs, out_specs=out_specs, check_vma=False)
```

profile of v0, /device:TPU:0, one launch (start us, length us, event | category | flops | bytes accessed | tf_op | source)
XLA Modules:
  0.0 638.8 jit_solution(4085861947890233693)
XLA Ops:
  42.0 6.4 fusion.61
  54.7 6.8 %fusion.4 = f32[64,4,192]{2,1,0:T(4,128)S(1)} fusion(s32[64,192]{1,0:T(8,128)S(1)} %get-tuple-element.48, f32[64,4,256]{2,1,0:T(4,128)S(1)} %gather_fusion), kind=kOutput, calls=%fused_computation.40 | convolution fusion | flops 154140672 | bytes 507904 | tf_op jit(solution)/shard_map/tfc,btc->btf/dot_general | solution.py:93
  61.5 6.9 %fusion.56 = f32[4,64,192]{2,0,1:T(4,128)S(1)} fusion(f32[64,4,192]{2,1,0:T(4,128)S(1)} %fusion.4, s32[64,192]{1,0:T(8,128)S(1)} %get-tuple-element.47, f32[4,1,128]{2,0,1:T(4,128)S(1)} %slice.454, f32[4,63,128]{2,0,1:T(4,128)S(1)} %slice.453, f32[4,64,128]{2,0,1:T(4,128)S(1)} %bitcast.444), kind=kOutput, calls=%fused_computation.94 | convolution fusion | flops 154320896 | bytes 704512 | tf_op jit(solution)/shard_map/tfc,btc->btf/dot_general | solution.py:92
  68.8 6.9 %fusion.50 = f32[5,64,256]{2,0,1:T(8,128)S(1)} fusion(s32[64,192]{1,0:T(8,128)S(1)} %get-tuple-element.47, f32[5,64,192]{2,1,0:T(8,128)S(1)} %maximum_multiply_fusion.1), kind=kOutput, calls=%fused_computation.88 | convolution fusion | flops 191889408 | bytes 622592 | tf_op jit(solution)/shard_map/tfc,btf->btc/dot_general | solution.py:101
  75.7 5.4 fusion.54
  81.3 18.1 %all-reduce.9.cloned.1.call-done = f32[5,8192]{1,0:T(8,128)} async-done(((f32[5,8192]{1,0:T(8,128)}), f32[5,8192]{1,0:T(8,128)}) %all-reduce.9.cloned.1.call-update) | async-done | bytes 163856 | tf_op jit(solution)/shard_map/psum | solution.py:117
  122.9 6.4 fusion.37
  145.3 6.8 %fusion.3 = f32[64,4,192]{2,1,0:T(4,128)S(1)} fusion(s32[64,192]{1,0:T(8,128)S(1)} %get-tuple-element.48, f32[64,4,256]{2,1,0:T(4,128)S(1)} %gather_fusion.1), kind=kOutput, calls=%fused_computation.39 | convolution fusion | flops 154140672 | bytes 507904 | tf_op jit(solution)/shard_map/tfc,btc->btf/dot_general | solution.py:93
  152.1 6.9 %fusion.57 = f32[64,4,192]{2,1,0:T(4,128)S(1)} fusion(f32[64,4,192]{2,1,0:T(4,128)S(1)} %fusion.3, s32[64,192]{1,0:T(8,128)S(1)} %get-tuple-element.47, f32[4,1,128]{2,0,1:T(4,128)S(1)} %fusion.167, f32[4,63,128]{2,0,1:T(4,128)S(1)} %fusion.154, f32[1,64,128]{2,0,1:T(1,128)S(1)} %bitcast.425, f32[3,64,128]{2,0,1:T(4,128)S(1)} %bitcast.399), kind=kOutput, calls=%fused_computation.95 | convolution fusion | flops 154386432 | bytes 704512 | tf_op jit(solution)/shard_map/tfc,btc->btf/dot_general | solution.py:92
  165.1 5.4 fusion.81
  170.6 17.9 %all-reduce.11.cloned.1.call-done = f32[4,8192]{1,0:T(4,128)} async-done(((f32[4,8192]{1,0:T(4,128)}), f32[4,8192]{1,0:T(4,128)}) %all-reduce.11.cloned.1.call-update) | async-done | bytes 131088 | tf_op jit(solution)/shard_map/psum | solution.py:142
  190.2 42.6 %all-reduce.2 = (f32[]{:T(128)}, f32[]{:T(128)}) all-reduce(f32[]{:T(128)} %get-tuple-element.16, f32[]{:T(128)} %get-tuple-element.15), channel_id=1, replica_groups=mesh['cells'=16,'faces'=2] {'cells'}, use_global_device_ids=true, to_apply=%region_1.2 | all-reduce | flops 2 | bytes 16 | tf_op jit(solution)/shard_map/psum | solution.py:147
  254.6 6.4 fusion.35
  262.4 5.6 collective-permute-start.15
  275.2 6.8 %fusion.2 = f32[64,4,192]{2,1,0:T(4,128)S(1)} fusion(s32[64,192]{1,0:T(8,128)S(1)} %get-tuple-element.48, f32[64,4,256]{2,1,0:T(4,128)S(1)} %gather_fusion.2), kind=kOutput, calls=%fused_computation.38 | convolution fusion | flops 154140672 | bytes 507904 | tf_op jit(solution)/shard_map/tfc,btc->btf/dot_general | solution.py:93
  282.0 6.9 %fusion.58 = f32[64,4,192]{2,1,0:T(4,128)S(1)} fusion(f32[64,4,192]{2,1,0:T(4,128)S(1)} %fusion.2, s32[64,192]{1,0:T(8,128)S(1)} %get-tuple-element.47, f32[4,1,128]{2,0,1:T(4,128)S(1)} %fusion.166, f32[4,63,128]{2,0,1:T(4,128)S(1)} %fusion.153, f32[1,64,128]{2,0,1:T(1,128)S(1)} %bitcast.432, f32[3,64,128]{2,0,1:T(4,128)S(1)} %bitcast.403), kind=kOutput, calls=%fused_computation.96 | convolution fusion | flops 154386432 | bytes 704512 | tf_op jit(solution)/shard_map/tfc,btc->btf/dot_general | solution.py:92
  295.0 5.4 fusion.78
  300.5 18.5 %all-reduce.13.cloned.1.call-done = f32[4,8192]{1,0:T(4,128)} async-done(((f32[4,8192]{1,0:T(4,128)}), f32[4,8192]{1,0:T(4,128)}) %all-reduce.13.cloned.1.call-update) | async-done | bytes 131088 | tf_op jit(solution)/shard_map/psum | solution.py:142
  320.7 42.9 %all-reduce.1 = (f32[]{:T(128)}, f32[]{:T(128)}, f32[]{:T(128)}, f32[]{:T(128)}) all-reduce(f32[]{:T(128)} %get-tuple-element.14, f32[]{:T(128)} %get-tuple-element.13, f32[]{:T(128)} %get-tuple-element.12, f32[]{:T(128)} %get-tuple-element.11), channel_id=1, replica_groups=mesh['cells'=16,'faces'=2] {'cells'}, use_global_device_ids=true, to_apply=%region_19.21 | all-reduce | flops 4 | bytes 32 | tf_op jit(solution)/shard_map/psum | solution.py:155
  389.9 6.4 fusion.33
  397.7 5.6 collective-permute-start.21
  410.5 6.8 %fusion.1 = f32[64,4,192]{2,1,0:T(4,128)S(1)} fusion(s32[64,192]{1,0:T(8,128)S(1)} %get-tuple-element.48, f32[64,4,256]{2,1,0:T(4,128)S(1)} %gather_fusion.3), kind=kOutput, calls=%fused_computation.37 | convolution fusion | flops 154140672 | bytes 507904 | tf_op jit(solution)/shard_map/tfc,btc->btf/dot_general | solution.py:93
  417.3 6.9 %fusion.59 = f32[64,4,192]{2,1,0:T(4,128)S(1)} fusion(f32[64,4,192]{2,1,0:T(4,128)S(1)} %fusion.1, s32[64,192]{1,0:T(8,128)S(1)} %get-tuple-element.47, f32[4,1,128]{2,0,1:T(4,128)S(1)} %fusion.165, f32[4,63,128]{2,0,1:T(4,128)S(1)} %fusion.152, f32[1,64,128]{2,0,1:T(1,128)S(1)} %bitcast.417, f32[3,64,128]{2,0,1:T(4,128)S(1)} %bitcast.395), kind=kOutput, calls=%fused_computation.97 | convolution fusion | flops 154386432 | bytes 704512 | tf_op jit(solution)/shard_map/tfc,btc->btf/dot_general | solution.py:92
  430.3 5.4 fusion.75
  435.8 18.5 %all-reduce.15.cloned.1.call-done = f32[4,8192]{1,0:T(4,128)} async-done(((f32[4,8192]{1,0:T(4,128)}), f32[4,8192]{1,0:T(4,128)}) %all-reduce.15.cloned.1.call-update) | async-done | bytes 131088 | tf_op jit(solution)/shard_map/psum | solution.py:142
  455.9 42.6 %psum.108 = f32[]{:T(128)} all-reduce(f32[]{:T(128)} %multiply_reduce_fusion.4), channel_id=1, replica_groups=mesh['cells'=16,'faces'=2] {'cells'}, use_global_device_ids=true, to_apply=%region_26.28 | all-reduce | flops 1 | bytes 8 | tf_op jit(solution)/shard_map/psum | solution.py:151
  520.7 6.4 fusion.31
  528.5 5.6 collective-permute-start.27
  541.3 6.8 %fusion = f32[64,4,192]{2,1,0:T(4,128)S(1)} fusion(s32[64,192]{1,0:T(8,128)S(1)} %get-tuple-element.48, f32[64,4,256]{2,1,0:T(4,128)S(1)} %gather_fusion.4), kind=kOutput, calls=%fused_computation.36 | convolution fusion | flops 154140672 | bytes 507904 | tf_op jit(solution)/shard_map/tfc,btc->btf/dot_general | solution.py:93
  548.1 6.9 %fusion.60 = f32[64,4,192]{2,1,0:T(4,128)S(1)} fusion(f32[64,4,192]{2,1,0:T(4,128)S(1)} %fusion, s32[64,192]{1,0:T(8,128)S(1)} %get-tuple-element.47, f32[4,1,128]{2,0,1:T(4,128)S(1)} %fusion.164, f32[4,63,128]{2,0,1:T(4,128)S(1)} %fusion.151, f32[1,64,128]{2,0,1:T(1,128)S(1)} %bitcast.439, f32[3,64,128]{2,0,1:T(4,128)S(1)} %bitcast.407), kind=kOutput, calls=%fused_computation.98 | convolution fusion | flops 154386432 | bytes 704512 | tf_op jit(solution)/shard_map/tfc,btc->btf/dot_general | solution.py:92
  566.5 18.6 %all-reduce.17.cloned.1.call-done = f32[4,8192]{1,0:T(4,128)} async-done(((f32[4,8192]{1,0:T(4,128)}), f32[4,8192]{1,0:T(4,128)}) %all-reduce.17.cloned.1.call-update) | async-done | bytes 131088 | tf_op jit(solution)/shard_map/psum | solution.py:142
  586.7 42.6 %all-reduce = (f32[]{:T(128)}, f32[]{:T(128)}) all-reduce(f32[]{:T(128)} %get-tuple-element.10, f32[]{:T(128)} %get-tuple-element.9), channel_id=1, replica_groups=mesh['cells'=16,'faces'=2] {'cells'}, use_global_device_ids=true, to_apply=%region_31.33 | all-reduce | flops 2 | bytes 16 | tf_op jit(solution)/shard_map/psum | solution.py:155
  (373 shorter events, 206.0 us)
Async XLA Ops:
  7.2 92.2 %all-reduce.9.cloned.1.call-start = ((), (), s32[]{:S(2)}) async-start(), calls=%async_computation | async-start | bytes 524288 | tf_op jit(solution)/shard_map/psum | solution.py:117
  30.6 18.8 %collective-permute-start = (f32[4,256]{1,0:T(4,128)S(1)}, f32[4,256]{1,0:T(4,128)S(1)}, u32[]{:S(2)}, u32[]{:S(2)}) collective-permute-start(f32[4,256]{1,0:T(4,128)S(1)} %get-tuple-element.78), channel_id=1, source_target_pairs={{30,0},{0,2},{2,4},{4,6},{6,8},{8,10},{10,12},{12,14},{14,16},{16,... | collective-permute-start | bytes 12296 | tf_op jit(solution)/shard_map/ppermute | solution.py:13
  33.7 17.1 %collective-permute-start.1 = (f32[4,256]{1,0:T(4,128)S(1)}, f32[4,256]{1,0:T(4,128)S(1)}, u32[]{:S(2)}, u32[]{:S(2)}) collective-permute-start(f32[4,256]{1,0:T(4,128)S(1)} %get-tuple-element.77), channel_id=1, source_target_pairs={{28,0},{30,2},{0,4},{2,6},{4,8},{6,10},{8,12},{10,14},{12,16},{14,... | collective-permute-start | bytes 12296 | tf_op jit(solution)/shard_map/ppermute | solution.py:13
  35.2 15.6 %collective-permute-start.2 = (f32[4,256]{1,0:T(4,128)S(1)}, f32[4,256]{1,0:T(4,128)S(1)}, u32[]{:S(2)}, u32[]{:S(2)}) collective-permute-start(f32[4,256]{1,0:T(4,128)S(1)} %get-tuple-element.76), channel_id=1, source_target_pairs={{26,0},{28,2},{30,4},{0,6},{2,8},{4,10},{6,12},{8,14},{10,16},{12,... | collective-permute-start | bytes 12296 | tf_op jit(solution)/shard_map/ppermute | solution.py:13
  37.6 13.2 %collective-permute-start.3 = (f32[4,256]{1,0:T(4,128)S(1)}, f32[4,256]{1,0:T(4,128)S(1)}, u32[]{:S(2)}, u32[]{:S(2)}) collective-permute-start(f32[4,256]{1,0:T(4,128)S(1)} %get-tuple-element.75), channel_id=1, source_target_pairs={{2,0},{4,2},{6,4},{8,6},{10,8},{12,10},{14,12},{16,14},{18,16},{20... | collective-permute-start | bytes 12296 | tf_op jit(solution)/shard_map/ppermute | solution.py:13
  40.9 10.0 %collective-permute-start.4 = (f32[4,256]{1,0:T(4,128)S(1)}, f32[4,256]{1,0:T(4,128)S(1)}, u32[]{:S(2)}, u32[]{:S(2)}) collective-permute-start(f32[4,256]{1,0:T(4,128)S(1)} %get-tuple-element.74), channel_id=1, source_target_pairs={{4,0},{6,2},{8,4},{10,6},{12,8},{14,10},{16,12},{18,14},{20,16},{2... | collective-permute-start | bytes 12296 | tf_op jit(solution)/shard_map/ppermute | solution.py:13
  49.4 4.6 collective-permute-start.5
  81.2 107.4 %all-reduce.11.cloned.1.call-start = ((), (), s32[]{:S(2)}) async-start(), calls=%async_computation.1 | async-start | bytes 262144 | tf_op jit(solution)/shard_map/psum | solution.py:142
  130.6 9.5 %collective-permute-start.6 = (f32[4,256]{1,0:T(4,128)S(1)}, f32[4,256]{1,0:T(4,128)S(1)}, u32[]{:S(2)}, u32[]{:S(2)}) collective-permute-start(f32[4,256]{1,0:T(4,128)S(1)} %get-tuple-element.72), channel_id=1, source_target_pairs={{30,0},{0,2},{2,4},{4,6},{6,8},{8,10},{10,12},{12,14},{14,16},{16,... | collective-permute-start | bytes 12296 | tf_op jit(solution)/shard_map/ppermute | solution.py:13
  132.4 8.8 %collective-permute-start.7 = (f32[4,256]{1,0:T(4,128)S(1)}, f32[4,256]{1,0:T(4,128)S(1)}, u32[]{:S(2)}, u32[]{:S(2)}) collective-permute-start(f32[4,256]{1,0:T(4,128)S(1)} %get-tuple-element.71), channel_id=1, source_target_pairs={{28,0},{30,2},{0,4},{2,6},{4,8},{6,10},{8,12},{10,14},{12,16},{14,... | collective-permute-start | bytes 12296 | tf_op jit(solution)/shard_map/ppermute | solution.py:13
  133.9 7.3 %collective-permute-start.8 = (f32[4,256]{1,0:T(4,128)S(1)}, f32[4,256]{1,0:T(4,128)S(1)}, u32[]{:S(2)}, u32[]{:S(2)}) collective-permute-start(f32[4,256]{1,0:T(4,128)S(1)} %get-tuple-element.70), channel_id=1, source_target_pairs={{26,0},{28,2},{30,4},{0,6},{2,8},{4,10},{6,12},{8,14},{10,16},{12,... | collective-permute-start | bytes 12296 | tf_op jit(solution)/shard_map/ppermute | solution.py:13
  136.3 5.0 collective-permute-start.9
  140.1 4.5 collective-permute-start.11
  170.5 148.4 %all-reduce.13.cloned.1.call-start = ((), (), s32[]{:S(2)}) async-start(), calls=%async_computation.2 | async-start | bytes 262144 | tf_op jit(solution)/shard_map/psum | solution.py:142
  262.2 7.7 %collective-permute-start.12 = (f32[4,256]{1,0:T(4,128)S(1)}, f32[4,256]{1,0:T(4,128)S(1)}, u32[]{:S(2)}, u32[]{:S(2)}) collective-permute-start(f32[4,256]{1,0:T(4,128)S(1)} %get-tuple-element.66), channel_id=1, source_target_pairs={{30,0},{0,2},{2,4},{4,6},{6,8},{8,10},{10,12},{12,14},{14,16},{16,... | collective-permute-start | bytes 12296 | tf_op jit(solution)/shard_map/ppermute | solution.py:13
  262.3 10.6 %collective-permute-start.13 = (f32[4,256]{1,0:T(4,128)S(1)}, f32[4,256]{1,0:T(4,128)S(1)}, u32[]{:S(2)}, u32[]{:S(2)}) collective-permute-start(f32[4,256]{1,0:T(4,128)S(1)} %get-tuple-element.65), channel_id=1, source_target_pairs={{28,0},{30,2},{0,4},{2,6},{4,8},{6,10},{8,12},{10,14},{12,16},{14,... | collective-permute-start | bytes 12296 | tf_op jit(solution)/shard_map/ppermute | solution.py:13
  262.4 10.5 %collective-permute-start.14 = (f32[4,256]{1,0:T(4,128)S(1)}, f32[4,256]{1,0:T(4,128)S(1)}, u32[]{:S(2)}, u32[]{:S(2)}) collective-permute-start(f32[4,256]{1,0:T(4,128)S(1)} %get-tuple-element.64), channel_id=1, source_target_pairs={{26,0},{28,2},{30,4},{0,6},{2,8},{4,10},{6,12},{8,14},{10,16},{12,... | collective-permute-start | bytes 12296 | tf_op jit(solution)/shard_map/ppermute | solution.py:13
  262.4 10.5 %collective-permute-start.15 = (f32[4,256]{1,0:T(4,128)S(1)}, f32[4,256]{1,0:T(4,128)S(1)}, u32[]{:S(2)}, u32[]{:S(2)}) collective-permute-start(f32[4,256]{1,0:T(4,128)S(1)} %get-tuple-element.63), channel_id=1, source_target_pairs={{2,0},{4,2},{6,4},{8,6},{10,8},{12,10},{14,12},{16,14},{18,16},{20... | collective-permute-start | bytes 12296 | tf_op jit(solution)/shard_map/ppermute | solution.py:13
  268.0 4.9 collective-permute-start.16
  300.4 153.9 %all-reduce.15.cloned.1.call-start = ((), (), s32[]{:S(2)}) async-start(), calls=%async_computation.3 | async-start | bytes 262144 | tf_op jit(solution)/shard_map/psum | solution.py:142
  397.5 7.7 %collective-permute-start.18 = (f32[4,256]{1,0:T(4,128)S(1)}, f32[4,256]{1,0:T(4,128)S(1)}, u32[]{:S(2)}, u32[]{:S(2)}) collective-permute-start(f32[4,256]{1,0:T(4,128)S(1)} %get-tuple-element.60), channel_id=1, source_target_pairs={{30,0},{0,2},{2,4},{4,6},{6,8},{8,10},{10,12},{12,14},{14,16},{16,... | collective-permute-start | bytes 12296 | tf_op jit(solution)/shard_map/ppermute | solution.py:13
  397.6 10.6 %collective-permute-start.19 = (f32[4,256]{1,0:T(4,128)S(1)}, f32[4,256]{1,0:T(4,128)S(1)}, u32[]{:S(2)}, u32[]{:S(2)}) collective-permute-start(f32[4,256]{1,0:T(4,128)S(1)} %get-tuple-element.59), channel_id=1, source_target_pairs={{28,0},{30,2},{0,4},{2,6},{4,8},{6,10},{8,12},{10,14},{12,16},{14,... | collective-permute-start | bytes 12296 | tf_op jit(solution)/shard_map/ppermute | solution.py:13
  397.7 10.5 %collective-permute-start.20 = (f32[4,256]{1,0:T(4,128)S(1)}, f32[4,256]{1,0:T(4,128)S(1)}, u32[]{:S(2)}, u32[]{:S(2)}) collective-permute-start(f32[4,256]{1,0:T(4,128)S(1)} %get-tuple-element.58), channel_id=1, source_target_pairs={{26,0},{28,2},{30,4},{0,6},{2,8},{4,10},{6,12},{8,14},{10,16},{12,... | collective-permute-start | bytes 12296 | tf_op jit(solution)/shard_map/ppermute | solution.py:13
  397.7 10.5 %collective-permute-start.21 = (f32[4,256]{1,0:T(4,128)S(1)}, f32[4,256]{1,0:T(4,128)S(1)}, u32[]{:S(2)}, u32[]{:S(2)}) collective-permute-start(f32[4,256]{1,0:T(4,128)S(1)} %get-tuple-element.57), channel_id=1, source_target_pairs={{2,0},{4,2},{6,4},{8,6},{10,8},{12,10},{14,12},{16,14},{18,16},{20... | collective-permute-start | bytes 12296 | tf_op jit(solution)/shard_map/ppermute | solution.py:13
  403.3 4.9 collective-permute-start.22
  435.7 149.3 %all-reduce.17.cloned.1.call-start = ((), (), s32[]{:S(2)}) async-start(), calls=%async_computation.4 | async-start | bytes 262144 | tf_op jit(solution)/shard_map/psum | solution.py:142
  528.3 7.7 %collective-permute-start.24 = (f32[4,256]{1,0:T(4,128)S(1)}, f32[4,256]{1,0:T(4,128)S(1)}, u32[]{:S(2)}, u32[]{:S(2)}) collective-permute-start(f32[4,256]{1,0:T(4,128)S(1)} %get-tuple-element.54), channel_id=1, source_target_pairs={{30,0},{0,2},{2,4},{4,6},{6,8},{8,10},{10,12},{12,14},{14,16},{16,... | collective-permute-start | bytes 12296 | tf_op jit(solution)/shard_map/ppermute | solution.py:13
  528.4 10.6 %collective-permute-start.25 = (f32[4,256]{1,0:T(4,128)S(1)}, f32[4,256]{1,0:T(4,128)S(1)}, u32[]{:S(2)}, u32[]{:S(2)}) collective-permute-start(f32[4,256]{1,0:T(4,128)S(1)} %get-tuple-element.53), channel_id=1, source_target_pairs={{28,0},{30,2},{0,4},{2,6},{4,8},{6,10},{8,12},{10,14},{12,16},{14,... | collective-permute-start | bytes 12296 | tf_op jit(solution)/shard_map/ppermute | solution.py:13
  528.5 10.5 %collective-permute-start.26 = (f32[4,256]{1,0:T(4,128)S(1)}, f32[4,256]{1,0:T(4,128)S(1)}, u32[]{:S(2)}, u32[]{:S(2)}) collective-permute-start(f32[4,256]{1,0:T(4,128)S(1)} %get-tuple-element.52), channel_id=1, source_target_pairs={{26,0},{28,2},{30,4},{0,6},{2,8},{4,10},{6,12},{8,14},{10,16},{12,... | collective-permute-start | bytes 12296 | tf_op jit(solution)/shard_map/ppermute | solution.py:13
  528.5 10.5 %collective-permute-start.27 = (f32[4,256]{1,0:T(4,128)S(1)}, f32[4,256]{1,0:T(4,128)S(1)}, u32[]{:S(2)}, u32[]{:S(2)}) collective-permute-start(f32[4,256]{1,0:T(4,128)S(1)} %get-tuple-element.51), channel_id=1, source_target_pairs={{2,0},{4,2},{6,4},{8,6},{10,8},{12,10},{14,12},{16,14},{18,16},{20... | collective-permute-start | bytes 12296 | tf_op jit(solution)/shard_map/ppermute | solution.py:13
  534.1 4.9 collective-permute-start.28
  536.0 4.5 collective-permute-start.29
  (12 other events, 352.0 us)
Sparse Core Ops, SparseCore 0:
  81.3 18.0 all-reduce.8
  170.7 17.8 all-reduce.10
  300.5 18.3 all-reduce.12
  435.8 18.3 all-reduce.14
  566.6 18.3 all-reduce.16
where the time goes:
time: 640 us; the launch traced here: 639 us
  blocking collectives  171 us (27%)
  matrix products  155 us (24%)
  local copies, waits for them, and re-layouts  111 us (17%)
  waiting for transfers between devices  103 us (16%)
  starting transfers between devices  54.7 us (9%)
  between operations  24.9 us (4%)
  other arithmetic  19.9 us (3%)
    gather x30, local copies, waits for them, and re-layouts, ghosts(): jnp.take(vector_in, send_list[which], axis=1)  87.3 us
    psum x2, blocking collectives, body(): lax.psum((jnp.sum(second * middle), jnp.sum(second * second), jnp.sum(sou...  85.5 us
    psum x4, waiting for transfers between devices, apply_matrix(): return volume_rate * vector_in + lax.psum(partial_value, 'faces')  73.5 us
    ppermute x30, starting transfers between devices, passed_along(): return lax.ppermute(block, axis, route)  54.5 us
    psum x1, blocking collectives, body(): rho_now = lax.psum(jnp.sum(source_term * residual), 'cells')  42.6 us
    psum x1, blocking collectives, body(): step_alpha = rho_now / lax.psum(jnp.sum(source_term * image), 'cells')  42.6 us
    dot_general x5, matrix products, to_faces(): jnp.einsum('tfc,btc->btf', local_hot, paired, precision=highest)  34.4 us
    dot_general x5, matrix products, to_faces(): jnp.einsum('tfc,btc->btf', halo_hot, halo_windows, precision=highest)  34 us
  transfers between devices with their start and end apart: 35, of which 11 were waited for; matrix products, arithmetic and copies ran while one was open for 1% of the time, Pallas kernels for 0%

commit v1 on v0

v1 whole, which is shorter than its diff:
```python
import functools

import jax
import jax.numpy as jnp
from jax import lax
from jax.experimental import pallas as pl
from jax.experimental.pallas import tpu as pltpu
from jax.sharding import PartitionSpec as P

F32 = jnp.float32
I32 = jnp.int32
LANES = 128
SUB = 8
BLOCK = 4


def offsets(count):
    return [which + 1 for which in range(count)] + [-(which + 1) for which in range(count)]


def pick(values, index):
    return jnp.take_along_axis(values, index, axis=1, mode="promise_in_bounds")


def lane_ids(shape=(SUB, LANES)):
    return lax.broadcasted_iota(I32, shape, 1)


def sub_ids(shape=(SUB, LANES)):
    return lax.broadcasted_iota(I32, shape, 0)


def ring_place(distance, count):
    here = lax.axis_index("cells")
    return lax.rem(here + distance + count, count)


def in_groups(tiles):
    return range(tiles // SUB)


def rows8(g):
    return slice(g * SUB, g * SUB + SUB)


def listed(cell_ref, send_ref):
    tiles = cell_ref.shape[1]
    halves = send_ref.shape[0] // 2
    row_at = [send_ref[h] for h in range(halves)]
    lane_at = [send_ref[halves + h] for h in range(halves)]
    found = [[jnp.zeros((SUB, LANES), F32) for _ in range(halves)] for _ in range(BLOCK)]
    for t in range(tiles):
        here = [row_at[h] == t for h in range(halves)]
        for c in range(BLOCK):
            row = jnp.broadcast_to(cell_ref[c, t : t + 1, :], (SUB, LANES))
            for h in range(halves):
                found[c][h] = jnp.where(here[h], pick(row, lane_at[h]), found[c][h])
    return found


def send_halo(found, stage_ref, out_ref, shifts):
    count = out_ref.shape[0]
    halves = len(found[0])
    for c in range(BLOCK):
        for h in range(halves):
            at = (c * halves + h) * SUB
            stage_ref[at : at + SUB, :] = found[c][h]
    for which, shift in enumerate(shifts):
        place = ring_place(shift, count)
        out_ref[place, 0:SUB, :] = stage_ref[pl.ds(which, SUB, stride=SUB), :]


def got_halo(in_ref, shifts):
    count = in_ref.shape[0]
    return [in_ref[ring_place(-shift, count), 0:SUB, :] for shift in shifts]


def lay_halo(lists, halo_ref):
    total = len(lists)
    span = halo_ref.shape[0] // SUB
    for j in range(total + SUB - 1):
        halo_ref[pl.ds(j, SUB, stride=span), :] = lists[j % total]


def send_sums(sums, out_ref):
    rows = jnp.zeros((SUB, LANES), F32)
    sub = sub_ids()
    for i, acc in enumerate(sums):
        row = jnp.sum(acc, axis=0, keepdims=True)
        rows = jnp.where(sub == i, jnp.broadcast_to(row, (SUB, LANES)), rows)
    first = out_ref.shape[1] - SUB
    for d in range(out_ref.shape[0]):
        out_ref[d, first : first + SUB, :] = rows


def got_sums(in_ref):
    first = in_ref.shape[1] - SUB
    parts = [in_ref[d, first : first + SUB, :] for d in range(in_ref.shape[0])]
    while len(parts) > 1:
        parts = [a + b for a, b in zip(parts[::2], parts[1::2])] + parts[len(parts) & ~1 :]
    return jnp.sum(parts[0], axis=1, keepdims=True)


def spread(column, i):
    return jnp.broadcast_to(column[i : i + 1, :], (SUB, LANES))


def row_of(ref, i):
    return jnp.broadcast_to(ref[i : i + 1, :], (SUB, LANES))


def prefix_matrix():
    shape = (3 * LANES, LANES)
    upto = (lax.broadcasted_iota(I32, shape, 0) % LANES) <= lax.broadcasted_iota(I32, shape, 1)
    return jnp.where(upto, 1.0, 0.0).astype(jnp.bfloat16)


def prefix_sums(blocks, matrix):
    values = jnp.concatenate(blocks, axis=0)
    high = values.astype(jnp.bfloat16)
    rest = values - high.astype(F32)
    middle = rest.astype(jnp.bfloat16)
    low = (rest - middle.astype(F32)).astype(jnp.bfloat16)
    split = jnp.concatenate([high, middle, low], axis=1)
    sums = jnp.dot(split, matrix, preferred_element_type=F32)
    return [sums[i * SUB : (i + 1) * SUB, :] for i in range(len(blocks))]


def to_cells(fluxes, tables, g, matrix, signs):
    rows, parts = len(fluxes), len(fluxes[0])
    order_ref, last_ref = tables
    blocks = []
    for side in range(2):
        for r in range(rows):
            order = order_ref[side, r, rows8(g), :]
            blocks += [pick(fluxes[r][c], order) for c in range(parts)]
    sums = prefix_sums(blocks, matrix)
    totals = []
    for side, of in ((0, 0), (1, 1), (1, 2)):
        acc = None
        for r in range(rows):
            last = last_ref[of, r, rows8(g), :]
            some = last >= 0
            at = jnp.maximum(last, 0)
            got = [
                jnp.where(some, pick(sums[(side * rows + r) * parts + c], at), 0.0)
                for c in range(parts)
            ]
            acc = got if acc is None else [a + b for a, b in zip(acc, got)]
        totals.append(acc)
    lane = lane_ids()
    here, beside = [], []
    for c in range(parts):
        owned, near, far = totals[0][c], totals[1][c], totals[2][c]
        both = owned + near if signs[c] > 0 else owned - near
        here.append(both - jnp.where(lane == 0, 0.0, pltpu.roll(both, 1, 1)))
        before = pltpu.roll(jnp.where(lane == LANES - 1, near, far), 1, 1)
        beside.append(far - before)
    return here, beside


def face_values(wide_ref, halo_ref, owner, code, g, lists, parts):
    span = halo_ref.shape[0] // SUB
    halves = SUB // BLOCK
    at = code & (LANES - 1)
    source = code >> 7
    first = (g * SUB) % lists
    left, right = [], []
    for c in range(parts):
        own = wide_ref[c, rows8(g), :]
        left.append(pick(own, owner))
        got = pick(own, at)
        got = jnp.where(source == 1, pick(wide_ref[c, g * SUB + 1 : g * SUB + 1 + SUB, :], at), got)
        for h in range(halves):
            base = (c * halves + h) * span + first
            got = jnp.where(source == 2 + h, pick(halo_ref[base : base + SUB, :], at), got)
        right.append(got)
    return left, right


def widen(wide_ref, tiles):
    for c in range(BLOCK):
        wide_ref[c, tiles : tiles + 1, :] = wide_ref[c, 0:1, :]


def wrap_beside(beside_ref, tiles):
    for c in range(beside_ref.shape[0]):
        beside_ref[c, 0:1, :] = beside_ref[c, tiles : tiles + 1, :]


def face_part(wide_ref, halo_ref, face_ref, link_ref, tables, here_ref, beside_ref, lists):
    tiles = here_ref.shape[1]
    rows = face_ref.shape[1]
    matrix = prefix_matrix()
    for g in in_groups(tiles):
        fluxes = []
        for r in range(rows):
            owner, code = link_ref[0, r, rows8(g), :], link_ref[1, r, rows8(g), :]
            left, right = face_values(wide_ref, halo_ref, owner, code, g, lists, BLOCK)
            speed, n0, n1, n2, wave = [face_ref[i, r, rows8(g), :] for i in range(5)]
            both = [a + b for a, b in zip(left, right)]
            gap = [a - b for a, b in zip(left, right)]
            normal = (n0, n1, n2)
            flux = [speed * both[i] + normal[i] * both[3] + wave * gap[i] for i in range(3)]
            flux.append(n0 * both[0] + n1 * both[1] + n2 * both[2] + wave * gap[3])
            fluxes.append(flux)
        here, beside = to_cells(fluxes, tables, g, matrix, (-1,) * BLOCK)
        for c in range(BLOCK):
            here_ref[c, rows8(g), :] = here[c]
            beside_ref[c, g * SUB + 1 : g * SUB + 1 + SUB, :] = beside[c]
    wrap_beside(beside_ref, tiles)


def precondition(vector, diag_ref, g):
    inverse, n0, n1, n2, schur = [diag_ref[i, rows8(g), :] for i in range(5)]
    coupled = n0 * vector[0] + n1 * vector[1] + n2 * vector[2]
    pressure = (vector[3] - coupled * inverse) * schur
    return [(vector[i] - n * pressure) * inverse for i, n in enumerate((n0, n1, n2))] + [pressure]


def applied(g, volume_ref, wide_ref, here_ref, beside_ref):
    volume = volume_ref[rows8(g), :]
    return [
        volume * wide_ref[c, rows8(g), :] + (here_ref[c, rows8(g), :] - beside_ref[c, rows8(g), :])
        for c in range(BLOCK)
    ]


def cell(ref, g):
    return [ref[c, rows8(g), :] for c in range(BLOCK)]


def put(ref, g, vector):
    for c in range(BLOCK):
        ref[c, rows8(g), :] = vector[c]


def added(acc, a, b):
    for x, y in zip(a, b):
        acc = acc + x * y
    return acc


def zero():
    return jnp.zeros((SUB, LANES), F32)


def start_kernel(
    count_ref, used_ref, normal_ref, owner_ref, neighbour_ref, flow_ref, list_ref,
    pack_ref, out_ref, flow_out, send_ref,
    stage_ref, *, shifts, cells_here,
):
    lists, width = list_ref.shape
    halves = width // LANES
    tiles = cells_here // LANES
    pairs = tiles // 2
    shape = (pairs, LANES)
    pair, lane = sub_ids(shape), lane_ids(shape)
    for i in range(3 * pairs):
        for c in range(3):
            at = (i % 3) * pairs + i // 3
            pack_ref[c, at : at + 1, :] = normal_ref[c : c + 1, i * LANES : (i + 1) * LANES]
    for q in range(3):
        at = slice(q * pairs, (q + 1) * pairs)
        tile = 2 * pair + (0, jnp.where(lane >= LANES // 2, 1, 0), 1)[q]
        live = (3 * pair + q) * LANES + lane < count_ref[0]
        owner = owner_ref[pl.ds(q, pairs, stride=3), :] - tile * LANES
        neighbour = neighbour_ref[pl.ds(q, pairs, stride=3), :]
        near = (neighbour - tile * LANES) & (cells_here - 1)
        far = neighbour - cells_here - lax.rem(tile, lists) * width + 2 * LANES
        code = jnp.where(neighbour < cells_here, near, far)
        pack_ref[3, at, :] = (owner * 512 + code).astype(F32)
        for c in range(3):
            pack_ref[c, at, :] = jnp.where(live, pack_ref[c, at, :], 0.0)
    for t in range(tiles):
        for c in range(BLOCK):
            flow_out[c, t : t + 1, :] = flow_ref[c : c + 1, t * LANES : (t + 1) * LANES]
    sub = sub_ids()
    used = jnp.zeros((SUB, LANES), I32)
    for k in range(lists):
        used = jnp.where(sub == k, used_ref[k], used)
    for h in range(halves):
        for k in range(lists):
            stage_ref[k : k + 1, :] = list_ref[k : k + 1, h * LANES : (h + 1) * LANES].astype(F32)
        listed_cell = stage_ref[0:SUB, :].astype(I32)
        alive = (lane_ids() + h * LANES < used) & (sub < lists)
        send_ref[h] = jnp.where(alive, listed_cell >> 7, -1)
        send_ref[halves + h] = jnp.where(alive, listed_cell & (LANES - 1), 0)
    send_halo(listed(flow_out, send_ref), stage_ref, out_ref, shifts)


def sorted_columns(x):
    sub = sub_ids()
    for k in range(1, 8):
        flip = None
        if 4 <= k <= 6:
            flip = ((sub >> (k - 4)) & 1) == 1
            x = [jnp.where(flip, -a, a) for a in x]
        for j in range(k - 1, -1, -1):
            if j < 4:
                new = list(x)
                for v in range(16):
                    w = v | (1 << j)
                    if w != v:
                        low, high = jnp.minimum(x[v], x[w]), jnp.maximum(x[v], x[w])
                        down = k < 4 and (v >> k) & 1
                        new[v], new[w] = (high, low) if down else (low, high)
                x = new
            else:
                d = 1 << (j - 4)
                first = ((sub >> (j - 4)) & 1) == 0
                x = [
                    jnp.where(
                        first,
                        jnp.minimum(a, pltpu.roll(a, SUB - d, 0)),
                        jnp.maximum(a, pltpu.roll(a, d, 0)),
                    )
                    for a in x
                ]
        if flip is not None:
            x = [jnp.where(flip, -a, a) for a in x]
    return x


def sort_rows(key_ref):
    lane = lane_ids()
    back = 8 * (lane & 15) + (lane >> 4)
    for b in range(key_ref.shape[0] // LANES):
        at = slice(b * LANES, (b + 1) * LANES)
        turned = jnp.transpose(key_ref[at, :])
        x = sorted_columns([turned[v * SUB : (v + 1) * SUB, :] for v in range(16)])
        turned = jnp.transpose(jnp.concatenate(x, axis=0))
        for v in range(16):
            row = b * LANES + v * SUB
            key_ref[row : row + SUB, :] = pick(turned[v * SUB : (v + 1) * SUB, :], back)


def last_below(keys, bound):
    at = jnp.zeros((SUB, LANES), I32)
    for step in (64, 32, 16, 8, 4, 2, 1):
        at = jnp.where(pick(keys, at + (step - 1)) < bound, at + step, at)
    return jnp.where(pick(keys, at) < bound, at, at - 1)


def setup_kernel(
    mine_ref, peer_ref, in_ref, flow_ref, source_ref, volume_ref, send_ref,
    face_ref, link_ref, order_ref, last_ref, diag_ref, source_out, pre_ref, out_ref,
    stage_ref, halo_ref, wide_ref, key_ref, here_ref, beside_ref, tile_ref, *, shifts,
):
    lists = len(shifts)
    tiles = volume_ref.shape[0]
    pairs = tiles // 2
    for t in range(tiles):
        for c in range(BLOCK):
            source_out[c, t : t + 1, :] = source_ref[c : c + 1, t * LANES : (t + 1) * LANES]
    swapped = lax.axis_index("faces") == 1
    lane = lane_ids((pairs, LANES))
    half = LANES // 2
    for i in range(4):
        part = []
        for q in range(3):
            mine = mine_ref[i, q * pairs : (q + 1) * pairs, :]
            peer = peer_ref[i, q * pairs : (q + 1) * pairs, :]
            part.append((jnp.where(swapped, peer, mine), jnp.where(swapped, mine, peer)))
        (a0, b0), (a1, b1), (a2, b2) = part
        even = (a0, b0, jnp.where(lane < half, a1, pltpu.roll(b1, half, 1)))
        odd = (a2, b2, jnp.where(lane < half, pltpu.roll(a1, half, 1), b1))
        for r in range(3):
            tile_ref[i * 3 + r, pl.ds(0, pairs, stride=2), :] = even[r]
            tile_ref[i * 3 + r, pl.ds(1, pairs, stride=2), :] = odd[r]
    lane = lane_ids()
    for r in range(3):
        for g in in_groups(tiles):
            joint = tile_ref[9 + r, rows8(g), :].astype(I32)
            owner, code = joint >> 9, joint & 511
            link_ref[0, r, rows8(g), :] = owner
            link_ref[1, r, rows8(g), :] = code
            at = r * tiles + g * SUB
            key_ref[at : at + SUB, :] = (owner * LANES + lane).astype(F32)
            at += 3 * tiles
            key_ref[at : at + SUB, :] = (jnp.minimum(code, 256) * LANES + lane).astype(F32)
    sort_rows(key_ref)
    for r in range(3):
        for g in in_groups(tiles):
            at = r * tiles + g * SUB
            owned = key_ref[at : at + SUB, :]
            near = key_ref[at + 3 * tiles : at + 3 * tiles + SUB, :]
            order_ref[0, r, rows8(g), :] = owned.astype(I32) & (LANES - 1)
            order_ref[1, r, rows8(g), :] = near.astype(I32) & (LANES - 1)
            bound = ((lane + 1) * LANES).astype(F32)
            last_ref[0, r, rows8(g), :] = last_below(owned, bound)
            last_ref[1, r, rows8(g), :] = last_below(near, bound)
            last_ref[2, r, rows8(g), :] = last_below(near, bound + float(LANES * LANES))
    for g in in_groups(tiles):
        put(wide_ref, g, cell(flow_ref, g))
    widen(wide_ref, tiles)
    lay_halo(got_halo(in_ref, shifts), halo_ref)
    matrix = prefix_matrix()
    for g in in_groups(tiles):
        terms = []
        for r in range(3):
            owner, code = link_ref[0, r, rows8(g), :], link_ref[1, r, rows8(g), :]
            left, right = face_values(wide_ref, halo_ref, owner, code, g, lists, 3)
            normal = [tile_ref[i * 3 + r, rows8(g), :] for i in range(3)]
            speed = zero()
            size = zero()
            for i in range(3):
                speed = speed + normal[i] * (left[i] + right[i])
                size = size + normal[i] * normal[i]
            speed = 0.5 * speed
            wave = jnp.abs(speed) + 2.0 * jnp.sqrt(size)
            term = [0.5 * speed] + [0.5 * n for n in normal] + [0.5 * wave]
            for i in range(5):
                face_ref[i, r, rows8(g), :] = term[i]
            terms.append(term)
        here, beside = to_cells(terms, (order_ref, last_ref), g, matrix, (-1, -1, -1, -1, 1))
        for i in range(5):
            here_ref[i, rows8(g), :] = here[i]
            beside_ref[i, g * SUB + 1 : g * SUB + 1 + SUB, :] = beside[i]
    wrap_beside(beside_ref, tiles)
    for g in in_groups(tiles):
        volume = volume_ref[rows8(g), :]
        own = [here_ref[i, rows8(g), :] for i in range(5)]
        other = [beside_ref[i, rows8(g), :] for i in range(5)]
        speed, n0, n1, n2 = [own[i] - other[i] for i in range(4)]
        pressure_diag = volume + (own[4] + other[4])
        inverse = 1.0 / (pressure_diag + speed)
        schur = pressure_diag - (n0 * n0 + n1 * n1 + n2 * n2) * inverse
        for i, value in enumerate((inverse, n0, n1, n2, 1.0 / schur)):
            diag_ref[i, rows8(g), :] = value
        put(pre_ref, g, precondition(cell(source_out, g), diag_ref, g))
    send_halo(listed(pre_ref, send_ref), stage_ref, out_ref, shifts)


def combine(scales, vectors):
    out = []
    for parts in zip(*vectors):
        acc = None
        for scale, part in zip(scales, parts):
            term = part if scale is None else scale * part
            acc = term if acc is None else acc + term
        out.append(acc)
    return out


def first_kernel(
    in_ref, pre_ref, source_ref, volume_ref, face_ref, link_ref, order_ref, last_ref, diag_ref, send_ref,
    image_ref, mimage_ref, out_ref,
    stage_ref, halo_ref, wide_ref, here_ref, beside_ref, *, shifts,
):
    tiles = volume_ref.shape[0]
    groups = in_groups(tiles)
    for g in groups:
        put(wide_ref, g, cell(pre_ref, g))
    widen(wide_ref, tiles)
    lay_halo(got_halo(in_ref, shifts), halo_ref)
    face_part(wide_ref, halo_ref, face_ref, link_ref, (order_ref, last_ref), here_ref, beside_ref, len(shifts))
    product, rho = zero(), zero()
    for g in groups:
        image = applied(g, volume_ref, wide_ref, here_ref, beside_ref)
        source = cell(source_ref, g)
        product = added(product, source, image)
        rho = added(rho, source, source)
        put(image_ref, g, image)
        put(mimage_ref, g, precondition(image, diag_ref, g))
    send_sums((product, rho), out_ref)
    send_halo(listed(mimage_ref, send_ref), stage_ref, out_ref, shifts)


def second_kernel(
    in1_ref, in2_ref, pre_ref, mimage_ref, image_ref, source_ref,
    volume_ref, face_ref, link_ref, order_ref, last_ref, diag_ref, send_ref,
    middle_ref, premid_ref, second_ref, msecond_ref, scale_ref, out_ref,
    stage_ref, halo_ref, wide_ref, here_ref, beside_ref, *, shifts,
):
    tiles = volume_ref.shape[0]
    groups = in_groups(tiles)
    sums = got_sums(in2_ref)
    rho = spread(sums, 1)
    alpha = rho / spread(sums, 0)
    scale_ref[0:1, :] = alpha[0:1, :]
    scale_ref[1:2, :] = rho[0:1, :]
    for g in groups:
        premid = combine((None, -alpha), (cell(pre_ref, g), cell(mimage_ref, g)))
        put(wide_ref, g, premid)
        put(premid_ref, g, premid)
    widen(wide_ref, tiles)
    lay_halo(combine((None, -alpha), (got_halo(in1_ref, shifts), got_halo(in2_ref, shifts))), halo_ref)
    face_part(wide_ref, halo_ref, face_ref, link_ref, (order_ref, last_ref), here_ref, beside_ref, len(shifts))
    products = [zero() for _ in range(4)]
    for g in groups:
        second = applied(g, volume_ref, wide_ref, here_ref, beside_ref)
        source = cell(source_ref, g)
        middle = combine((None, -alpha), (source, cell(image_ref, g)))
        put(middle_ref, g, middle)
        put(second_ref, g, second)
        put(msecond_ref, g, precondition(second, diag_ref, g))
        for i, (a, b) in enumerate(((second, middle), (second, second), (source, middle), (source, second))):
            products[i] = added(products[i], a, b)
    send_sums(products, out_ref)
    send_halo(listed(msecond_ref, send_ref), stage_ref, out_ref, shifts)


def third_kernel(
    in1_ref, in2_ref, in3_ref, scale_ref, pre_ref, mimage_ref, premid_ref, msecond_ref, middle_ref, second_ref, source_ref,
    volume_ref, face_ref, link_ref, order_ref, last_ref, diag_ref, send_ref,
    field_ref, residual_ref, preres_ref, predir_ref, image_ref, mimage_out, scale_out, ghost_ref, out_ref,
    stage_ref, halo_ref, wide_ref, here_ref, beside_ref, *, shifts,
):
    tiles = volume_ref.shape[0]
    groups = in_groups(tiles)
    sums = got_sums(in3_ref)
    alpha, rho = row_of(scale_ref, 0), row_of(scale_ref, 1)
    omega = spread(sums, 0) / spread(sums, 1)
    rho_next = spread(sums, 2) - omega * spread(sums, 3)
    beta = rho_next / rho * (alpha / omega)
    scale_out[0:1, :] = rho_next[0:1, :]
    drop = -beta * omega
    for g in groups:
        predir, mimage, premid = cell(pre_ref, g), cell(mimage_ref, g), cell(premid_ref, g)
        put(field_ref, g, combine((alpha, omega), (predir, premid)))
        put(residual_ref, g, combine((None, -omega), (cell(middle_ref, g), cell(second_ref, g))))
        preres = combine((None, -omega), (premid, cell(msecond_ref, g)))
        put(preres_ref, g, preres)
        predir = combine((None, beta, drop), (preres, predir, mimage))
        put(predir_ref, g, predir)
        put(wide_ref, g, predir)
    widen(wide_ref, tiles)
    ghost1, ghost2, ghost3 = [got_halo(ref, shifts) for ref in (in1_ref, in2_ref, in3_ref)]
    preres = combine((None, -alpha, -omega), (ghost1, ghost2, ghost3))
    for k in range(len(shifts)):
        ghost_ref[k] = preres[k]
    lay_halo(combine((None, beta, drop), (preres, ghost1, ghost2)), halo_ref)
    face_part(wide_ref, halo_ref, face_ref, link_ref, (order_ref, last_ref), here_ref, beside_ref, len(shifts))
    product = zero()
    for g in groups:
        image = applied(g, volume_ref, wide_ref, here_ref, beside_ref)
        product = added(product, cell(source_ref, g), image)
        put(image_ref, g, image)
        put(mimage_out, g, precondition(image, diag_ref, g))
    send_sums((product,), out_ref)
    send_halo(listed(mimage_out, send_ref), stage_ref, out_ref, shifts)


def fourth_kernel(
    in4_ref, scale_ref, ghost_ref, field_ref, residual_ref, preres_ref, predir_ref, image_ref, mimage_ref,
    volume_ref, face_ref, link_ref, order_ref, last_ref,
    field_out, premid_ref, middle_ref, second_ref, out_ref,
    halo_ref, wide_ref, here_ref, beside_ref, *, shifts,
):
    tiles = volume_ref.shape[0]
    groups = in_groups(tiles)
    alpha = row_of(scale_ref, 0) / spread(got_sums(in4_ref), 0)
    for g in groups:
        premid = combine((None, -alpha), (cell(preres_ref, g), cell(mimage_ref, g)))
        put(wide_ref, g, premid)
        put(premid_ref, g, premid)
        put(field_out, g, combine((None, alpha), (cell(field_ref, g), cell(predir_ref, g))))
        put(middle_ref, g, combine((None, -alpha), (cell(residual_ref, g), cell(image_ref, g))))
    widen(wide_ref, tiles)
    ghosts = [ghost_ref[k] for k in range(len(shifts))]
    lay_halo(combine((None, -alpha), (ghosts, got_halo(in4_ref, shifts))), halo_ref)
    face_part(wide_ref, halo_ref, face_ref, link_ref, (order_ref, last_ref), here_ref, beside_ref, len(shifts))
    cross, square = zero(), zero()
    for g in groups:
        second = applied(g, volume_ref, wide_ref, here_ref, beside_ref)
        put(second_ref, g, second)
        cross = added(cross, second, cell(middle_ref, g))
        square = added(square, second, second)
    send_sums((cross, square), out_ref)


def last_kernel(in_ref, field_ref, premid_ref, middle_ref, second_ref, field_out, residual_out, stage_ref):
    tiles = field_ref.shape[1]
    sums = got_sums(in_ref)
    omega = spread(sums, 0) / spread(sums, 1)
    for g in in_groups(tiles):
        field = combine((None, omega), (cell(field_ref, g), cell(premid_ref, g)))
        residual = combine((None, -omega), (cell(middle_ref, g), cell(second_ref, g)))
        put(stage_ref.at[0], g, field)
        put(stage_ref.at[1], g, residual)
        for i, out in enumerate((field_out, residual_out)):
            for t in range(g * SUB, g * SUB + SUB):
                for c in range(BLOCK):
                    out[c : c + 1, t * LANES : (t + 1) * LANES] = stage_ref[i, c, t : t + 1, :]


def run(kernel, outs, scratch, args, scalars=0):
    vmem = pl.BlockSpec(memory_space=pltpu.VMEM)
    smem = pl.BlockSpec(memory_space=pltpu.SMEM)
    return pl.pallas_call(
        kernel,
        out_shape=[jax.ShapeDtypeStruct(shape, dtype) for shape, dtype in outs],
        in_specs=[smem] * scalars + [vmem] * (len(args) - scalars),
        out_specs=[vmem] * len(outs),
        scratch_shapes=[pltpu.VMEM(shape, F32) for shape in scratch],
        compiler_params=pltpu.CompilerParams(vmem_limit_bytes=24 << 20),
    )(*args)


def exchange(block):
    return lax.all_to_all(block, "cells", 0, 0)


def body(
    flow_state,
    source_term,
    volume_rate,
    face_normal,
    face_owner,
    face_neighbour,
    face_count,
    send_list,
    halo_count,
):
    count = lax.axis_size("cells")
    cells_here = flow_state.shape[1]
    lists, width = send_list.shape
    tiles = cells_here // LANES
    per_tile = face_owner.shape[0] // tiles
    shifts = offsets(lists // 2)
    halves = width // LANES
    assert per_tile * 2 == 3 * LANES and lax.axis_size("faces") == 2
    assert width == 2 * LANES and count > lists and lists <= SUB
    assert tiles % SUB == 0 and cells_here & (cells_here - 1) == 0
    rows = 3
    span = -(-(lists + SUB - 1) // SUB) * SUB
    vector = (BLOCK, tiles, LANES)
    vec = (vector, F32)
    faces = (rows, tiles, LANES)
    scale = ((SUB, LANES), F32)
    halo_block = ((count, SUB, LANES), F32)
    full_block = ((count, 2 * SUB, LANES), F32)
    wide = (BLOCK, tiles + SUB, LANES)
    stage = (SUB * SUB, LANES)
    halo = (SUB * span, LANES)
    flat = face_owner.shape[0] // LANES
    volume = volume_rate.reshape(tiles, LANES)

    pack, out0, flow, send = run(
        functools.partial(start_kernel, shifts=shifts, cells_here=cells_here),
        [((4, flat, LANES), F32), halo_block, vec, ((2 * halves, SUB, LANES), I32)],
        [stage],
        (
            face_count, halo_count, face_normal, face_owner.reshape(flat, LANES),
            face_neighbour.reshape(flat, LANES), flow_state, send_list,
        ),
        scalars=2,
    )
    peer = lax.ppermute(pack, "faces", [(0, 1), (1, 0)])
    in0 = exchange(out0)
    face, link, order, last, diag, source, predir, out1 = run(
        functools.partial(setup_kernel, shifts=shifts),
        [
            ((5,) + faces, F32), ((2,) + faces, I32), ((2,) + faces, I32), ((3,) + faces, I32),
            ((5, tiles, LANES), F32), vec, vec, halo_block,
        ],
        [stage, halo, wide, (6 * tiles, LANES), (5, tiles, LANES), (5, tiles + SUB, LANES), (12, tiles, LANES)],
        (pack, peer, in0, flow, source_term, volume, send),
    )
    in1 = exchange(out1)
    work = [stage, halo, wide, vector, wide]
    fixed = (volume, face, link, order, last, diag, send)
    image, mimage, out2 = run(
        functools.partial(first_kernel, shifts=shifts), [vec, vec, full_block], work, (in1, predir, source) + fixed
    )
    in2 = exchange(out2)
    middle, premid, second, msecond, scales, out3 = run(
        functools.partial(second_kernel, shifts=shifts),
        [vec, vec, vec, vec, scale, full_block],
        work,
        (in1, in2, predir, mimage, image, source) + fixed,
    )
    in3 = exchange(out3)
    field, residual, preres, predir, image, mimage, scales, ghosts, out4 = run(
        functools.partial(third_kernel, shifts=shifts),
        [vec, vec, vec, vec, vec, vec, scale, ((lists, SUB, LANES), F32), full_block],
        work,
        (in1, in2, in3, scales, predir, mimage, premid, msecond, middle, second, source) + fixed,
    )
    in4 = exchange(out4)
    field, premid, middle, second, out5 = run(
        functools.partial(fourth_kernel, shifts=shifts),
        [vec, vec, vec, vec, halo_block],
        work[1:],
        (in4, scales, ghosts, field, residual, preres, predir, image, mimage) + fixed[:5],
    )
    in5 = exchange(out5)
    out = (flow_state.shape, F32)
    field, residual = run(last_kernel, [out, out], [(2,) + vector], (in5, field, premid, middle, second))
    return (field, residual)


def solution(mesh):
    in_specs = (
        P(None, "cells"),
        P(None, "cells"),
        P("cells"),
        P(None, ("cells", "faces")),
        P(("cells", "faces")),
        P(("cells", "faces")),
        P(("cells", "faces")),
        P("cells", None),
        P("cells"),
    )
    out_specs = (P(None, "cells"), P(None, "cells"))
    return jax.shard_map(body, mesh=mesh, in_specs=in_specs, out_specs=out_specs, check_vma=False)
```

time: 640 us -> 107 us (0.17)
  matrix products: 155 us -> 0 us
  local copies, waits for them, and re-layouts: 111 us -> 4.78 us
  blocking collectives: 171 us -> 66.6 us
  waiting for transfers between devices: 103 us -> 0.01 us
  starting transfers between devices: 54.7 us -> 0.56 us
  Pallas kernels: 0 us -> 33.4 us
  between operations: 24.9 us -> 1.34 us
  other arithmetic: 19.9 us -> 0 us
    psum x4 -> x0, blocking collectives: 171 us -> none  [the longest x2 85.5 us: body(): lax.psum((jnp.sum(second * middle), jnp.sum(second * second), jnp.sum(sou...]
    dot_general x25 -> x0, matrix products: 155 us -> none  [the longest x5 34.4 us: to_faces(): jnp.einsum('tfc,btc->btf', local_hot, paired, precision=highest)]
    psum x5 -> x0, waiting for transfers between devices: 91.6 us -> none  [the longest x4 73.5 us: apply_matrix(): return volume_rate * vector_in + lax.psum(partial_value, 'faces')]
    gather x35 -> x0, local copies, waits for them, and re-layouts: 90.9 us -> none  [the longest x30 87.3 us: ghosts(): jnp.take(vector_in, send_list[which], axis=1)]
    all_to_all x0 -> x6, blocking collectives: none -> 66.6 us  [exchange(): return lax.all_to_all(block, 'cells', 0, 0)]
    ppermute x30 -> x1, starting transfers between devices: 54.5 us -> 0.56 us  [body(): peer = lax.ppermute(pack, 'faces', [(0, 1), (1, 0)])]
    pallas_call x0 -> x7, Pallas kernels: none -> 33.4 us  [run(): pl.pallas_call(kernel, out_shape=[jax.ShapeDtypeStruct(shape, dtype) for...]
    ppermute x30 -> x1, waiting for transfers between devices: 11 us -> 0.01 us  [body(): peer = lax.ppermute(pack, 'faces', [(0, 1), (1, 0)])]
  transfers between devices with their start and end apart: 35 -> 1, of which waited for: 11 -> 0; matrix products, arithmetic and copies ran while one was open for 1% -> 0% of each run, Pallas kernels for 0% -> 0%
where the time goes in v1:
time: 107 us
  blocking collectives  66.6 us (62%)
  Pallas kernels  33.4 us (31%)
  local copies, waits for them, and re-layouts  4.78 us (4%)
  between operations  1.34 us (1%)
    all_to_all x6, blocking collectives, exchange(): return lax.all_to_all(block, 'cells', 0, 0)  66.6 us
    pallas_call x7, Pallas kernels, run(): pl.pallas_call(kernel, out_shape=[jax.ShapeDtypeStruct(shape, dtype) for...  33.4 us
    unnamed x16, local copies, waits for them, and re-layouts  4.78 us
  transfers between devices with their start and end apart: 1, of which 0 were waited for; matrix products, arithmetic and copies ran while one was open for 0% of the time, Pallas kernels for 0%

profile of v1, /device:TPU:0, one launch (start us, length us, event | category | flops | bytes accessed | tf_op | source)
XLA Modules:
  0.0 106.7 jit_solution(17860630433761814829)
XLA Ops:
  1.3 0.0 copy-start.7
  1.3 0.6 copy-done.7
  1.9 0.0 copy-start.1
  1.9 0.9 copy-done.1
  2.9 0.0 copy-start.2
  2.9 0.9 copy-done.2
  3.8 0.0 copy-start.4
  3.8 0.8 copy-done.4
  4.6 0.0 copy-start.5
  4.6 0.8 copy-done.5
  5.4 0.0 copy-start.6
  5.4 0.7 copy-done.6
  6.1 0.0 copy-start.3
  6.1 1.3 %shard_map.104 = (f32[4,96,128]{2,1,0:T(8,128)S(1)}, f32[16,8,128]{2,1,0:T(8,128)S(1)}, f32[4,64,128]{2,1,0:T(8,128)S(1)}, s32[4,8,128]{2,1,0:T(8,128)S(1)}) custom-call(s32[1]{0:T(128)S(6)} %copy.11.count_ref, s32[6]{0:T(128)S(1)} %copy-done.7, f32[3,12288]{1,0:T(4,128)S(1)} %copy-done.1, s32[96,128]{1,0:T(8,128)S(1)} %bitcast.8, s32[96,128]{1,0:T(8,128)S(1)} %bitcast.9, ...), custom_call_target="tpu_custom_call" | custom-call | tf_op jit(solution)/shard_map/pallas_call | solution.py:591
  7.4 0.6 collective-permute-start
  8.0 0.0 copy-start
  8.0 15.2 %all_to_all.30.in_ref = f32[16,8,128]{2,1,0:T(8,128)S(1)} all-to-all(f32[16,8,128]{2,1,0:T(8,128)S(1)} %get-tuple-element.38), channel_id=1, replica_groups=mesh['cells'=16,'faces'=2] {'cells'}, dimensions={0} | all-to-all | bytes 131072 | tf_op jit(solution)/shard_map/all_to_all | solution.py:602
  23.2 0.0 collective-permute-done.peer_ref
  23.2 0.0 copy-done.3
  23.2 0.0 copy-done
  23.2 13.3 %shard_map.105 = (f32[5,3,64,128]{3,2,1,0:T(8,128)S(1)}, s32[2,3,64,128]{3,2,1,0:T(8,128)S(1)}, s32[2,3,64,128]{3,2,1,0:T(8,128)S(1)}, s32[3,3,64,128]{3,2,1,0:T...) custom-call(f32[4,96,128]{2,1,0:T(8,128)S(1)} %get-tuple-element.37., ...), custom_call_target="tpu_custom_call" | custom-call | tf_op jit(solution)/shard_map/pallas_call | solution.py:591
  36.5 10.1 %all_to_all.31.in_ref.in1_ref = f32[16,8,128]{2,1,0:T(8,128)S(1)} all-to-all(f32[16,8,128]{2,1,0:T(8,128)S(1)} %get-tuple-element.41), channel_id=1, replica_groups=mesh['cells'=16,'faces'=2] {'cells'}, dimensions={0} | all-to-all | bytes 131072 | tf_op jit(solution)/shard_map/all_to_all | solution.py:602
  46.7 4.8 %shard_map.106 = (f32[4,64,128]{2,1,0:T(8,128)S(1)}, f32[4,64,128]{2,1,0:T(8,128)S(1)}, f32[16,16,128]{2,1,0:T(8,128)S(1)}) custom-call(f32[16,8,128]{2,1,0:T(8,128)S(1)} %all_to_all.31.in_ref.in1_ref, f32[4,64,128]{2,1,0:T(8,128)S(1)} %get-tuple-element.42.pre_ref, f32[4,64,128]{2,1,0:T(8,128)S(1)} %get-tuple-element.43.source_ref, f32[64,128]{1,0:T(8,128)S(1)} %bitcast.4, ...), custom_call_target="tpu_custom_call" | custom-call | tf_op jit(solution)/shard_map/pallas_call | solution.py:591
  51.5 10.4 %all_to_all.32.in2_ref = f32[16,16,128]{2,1,0:T(8,128)S(1)} all-to-all(f32[16,16,128]{2,1,0:T(8,128)S(1)} %get-tuple-element.49), channel_id=1, replica_groups=mesh['cells'=16,'faces'=2] {'cells'}, dimensions={0} | all-to-all | bytes 262144 | tf_op jit(solution)/shard_map/all_to_all | solution.py:602
  61.9 4.7 %shard_map.107 = (f32[4,64,128]{2,1,0:T(8,128)S(1)}, f32[4,64,128]{2,1,0:T(8,128)S(1)}, f32[4,64,128]{2,1,0:T(8,128)S(1)}, f32[4,64,128]{2,1,0:T(8,128)S(1)}, f3...) custom-call(f32[16,8,128]{2,1,0:T(8,128)S(1)} %all_to_all.31.in_ref.in1_ref, f32[16,16,128]{2,1,0:T(8,128)S(1)} %all_to_all.32.in2_ref, ...), custom_call_target="tpu_custom_call" | custom-call | tf_op jit(solution)/shard_map/pallas_call | solution.py:591
  66.6 10.4 %all_to_all.33.in3_ref = f32[16,16,128]{2,1,0:T(8,128)S(1)} all-to-all(f32[16,16,128]{2,1,0:T(8,128)S(1)} %get-tuple-element.52), channel_id=1, replica_groups=mesh['cells'=16,'faces'=2] {'cells'}, dimensions={0} | all-to-all | bytes 262144 | tf_op jit(solution)/shard_map/all_to_all | solution.py:602
  77.0 4.8 %shard_map.108 = (f32[4,64,128]{2,1,0:T(8,128)S(1)}, f32[4,64,128]{2,1,0:T(8,128)S(1)}, f32[4,64,128]{2,1,0:T(8,128)S(1)}, f32[4,64,128]{2,1,0:T(8,128)S(1)}, f3...) custom-call(f32[16,8,128]{2,1,0:T(8,128)S(1)} %all_to_all.31.in_ref., ...), custom_call_target="tpu_custom_call" | custom-call | tf_op jit(solution)/shard_map/pallas_call | solution.py:591
  81.8 10.4 %all_to_all.34.in4_ref = f32[16,16,128]{2,1,0:T(8,128)S(1)} all-to-all(f32[16,16,128]{2,1,0:T(8,128)S(1)} %get-tuple-element.58), channel_id=1, replica_groups=mesh['cells'=16,'faces'=2] {'cells'}, dimensions={0} | all-to-all | bytes 262144 | tf_op jit(solution)/shard_map/all_to_all | solution.py:602
  92.2 3.4 %shard_map.109 = (f32[4,64,128]{2,1,0:T(8,128)S(1)}, f32[4,64,128]{2,1,0:T(8,128)S(1)}, f32[4,64,128]{2,1,0:T(8,128)S(1)}, f32[4,64,128]{2,1,0:T(8,128)S(1)}, f32[16,8,128]{2,1,0:T(8,128)S(1)}) custom-call(f32[16,16,128]{2,1,0:T(8,128)S(1)} %all_to_all.34.in4_ref, f32[8,128]{1,0:T(8,128)S(1)} %get-tuple-element.59.scale_ref, ...), custom_call_target="tpu_custom_call" | custom-call | tf_op jit(solution)/shard_map/pallas_call | solution.py:591
  95.6 10.1 %all_to_all.35.in_ref = f32[16,8,128]{2,1,0:T(8,128)S(1)} all-to-all(f32[16,8,128]{2,1,0:T(8,128)S(1)} %get-tuple-element.67), channel_id=1, replica_groups=mesh['cells'=16,'faces'=2] {'cells'}, dimensions={0} | all-to-all | bytes 131072 | tf_op jit(solution)/shard_map/all_to_all | solution.py:602
  105.7 1.0 shard_map.110
Async XLA Ops:
  1.3 0.7 copy-start.7
  1.9 0.9 copy-start.1
  2.9 0.9 copy-start.2
  3.8 0.8 copy-start.4
  4.6 0.8 copy-start.5
  5.4 0.7 copy-start.6
  6.1 17.1 %copy-start.3 = (f32[4,8192]{1,0:T(4,128)S(1)}, f32[4,8192]{1,0:T(4,128)}, u32[]{:S(2)}) copy-start(f32[4,8192]{1,0:T(4,128)} %source_ref.1) | copy-start | bytes 393220
  7.4 15.8 %collective-permute-start = (f32[4,96,128]{2,1,0:T(8,128)S(1)}, f32[4,96,128]{2,1,0:T(8,128)S(1)}, u32[]{:S(2)}, u32[]{:S(2)}) collective-permute-start(f32[4,96,128]{2,1,0:T(8,128)S(1)} %get-tuple-element.37.mine_ref), channel_id=1, source_target_pairs={{0,1},{1,0},{2,3},{3,2},{4,5},{5,4},{6,7},{7,6},{8,9},{9,8},{10,11... | collective-permute-start | bytes 589832 | tf_op jit(solution)/shard_map/ppermute | solution.py:650
  8.0 15.2 %copy-start = (f32[8192]{0:T(1024)S(1)}, f32[8192]{0:T(1024)}, u32[]{:S(2)}) copy-start(f32[8192]{0:T(1024)} %param.11) | copy-start | bytes 98308

commit v2 on v1

--- a/solution.py
+++ b/solution.py
@@ -18,8 +18,31 @@
     return [which + 1 for which in range(count)] + [-(which + 1) for which in range(count)]
 
 
+ALONG_LANES = lax.GatherDimensionNumbers(
+    offset_dims=(),
+    collapsed_slice_dims=(1,),
+    start_index_map=(1,),
+    operand_batching_dims=(0,),
+    start_indices_batching_dims=(0,),
+)
+
+ALONG_ROWS = lax.GatherDimensionNumbers(
+    offset_dims=(),
+    collapsed_slice_dims=(0,),
+    start_index_map=(0,),
+    operand_batching_dims=(1,),
+    start_indices_batching_dims=(1,),
+)
+
+
 def pick(values, index):
-    return jnp.take_along_axis(values, index, axis=1, mode="promise_in_bounds")
+    mode = lax.GatherScatterMode.PROMISE_IN_BOUNDS
+    return lax.gather(values, index[..., None], ALONG_LANES, slice_sizes=(1, 1), mode=mode)
+
+
+def pick_row(values, index):
+    mode = lax.GatherScatterMode.PROMISE_IN_BOUNDS
+    return lax.gather(values, index[..., None], ALONG_ROWS, slice_sizes=(1, 1), mode=mode)
 
 
 def lane_ids(shape=(SUB, LANES)):
@@ -30,9 +53,8 @@
     return lax.broadcasted_iota(I32, shape, 0)
 
 
-def ring_place(distance, count):
-    here = lax.axis_index("cells")
-    return lax.rem(here + distance + count, count)
+def partition(distance, count):
+    return lax.rem(lax.axis_index("cells") + distance + count, count)
 
 
 def in_groups(tiles):
@@ -44,35 +66,36 @@
 
 
 def listed(cell_ref, send_ref):
-    tiles = cell_ref.shape[1]
-    halves = send_ref.shape[0] // 2
-    row_at = [send_ref[h] for h in range(halves)]
-    lane_at = [send_ref[halves + h] for h in range(halves)]
-    found = [[jnp.zeros((SUB, LANES), F32) for _ in range(halves)] for _ in range(BLOCK)]
-    for t in range(tiles):
-        here = [row_at[h] == t for h in range(halves)]
+    row_at, lane_at = send_ref[0], send_ref[1]
+    found = [jnp.zeros((SUB, LANES), F32) for _ in range(BLOCK)]
+    for t in range(cell_ref.shape[1]):
+        here = row_at == t
         for c in range(BLOCK):
             row = jnp.broadcast_to(cell_ref[c, t : t + 1, :], (SUB, LANES))
-            for h in range(halves):
-                found[c][h] = jnp.where(here[h], pick(row, lane_at[h]), found[c][h])
+            found[c] = jnp.where(here, pick(row, lane_at), found[c])
     return found
 
 
-def send_halo(found, stage_ref, out_ref, shifts):
-    count = out_ref.shape[0]
-    halves = len(found[0])
+def send_halo(found, stage_ref, out_ref, each):
+    cores = lax.axis_size("faces")
+    count = out_ref.shape[0] // cores
+    halves = SUB // BLOCK
     for c in range(BLOCK):
+        stage_ref[c * SUB : (c + 1) * SUB, :] = found[c]
+    sign = 1 - 2 * lax.axis_index("faces")
+    for j in range(each):
+        place = partition(sign * (j + 1), count)
         for h in range(halves):
-            at = (c * halves + h) * SUB
-            stage_ref[at : at + SUB, :] = found[c][h]
-    for which, shift in enumerate(shifts):
-        place = ring_place(shift, count)
-        out_ref[place, 0:SUB, :] = stage_ref[pl.ds(which, SUB, stride=SUB), :]
+            rows = stage_ref[pl.ds(j * halves + h, BLOCK, stride=SUB), :]
+            for core in range(cores):
+                out_ref[place * cores + core, h * BLOCK : (h + 1) * BLOCK, :] = rows
 
 
 def got_halo(in_ref, shifts):
-    count = in_ref.shape[0]
-    return [in_ref[ring_place(-shift, count), 0:SUB, :] for shift in shifts]
+    cores = lax.axis_size("faces")
+    count = in_ref.shape[0] // cores
+    each = len(shifts) // cores
+    return [in_ref[partition(-shift, count) * cores + k // each] for k, shift in enumerate(shifts)]
 
 
 def lay_halo(lists, halo_ref):
@@ -88,19 +111,27 @@
     for i, acc in enumerate(sums):
         row = jnp.sum(acc, axis=0, keepdims=True)
         rows = jnp.where(sub == i, jnp.broadcast_to(row, (SUB, LANES)), rows)
-    first = out_ref.shape[1] - SUB
     for d in range(out_ref.shape[0]):
-        out_ref[d, first : first + SUB, :] = rows
-
-
-def got_sums(in_ref):
-    first = in_ref.shape[1] - SUB
-    parts = [in_ref[d, first : first + SUB, :] for d in range(in_ref.shape[0])]
+        out_ref[d] = rows
+
+
+def total_of(parts):
     while len(parts) > 1:
         parts = [a + b for a, b in zip(parts[::2], parts[1::2])] + parts[len(parts) & ~1 :]
     return jnp.sum(parts[0], axis=1, keepdims=True)
 
 
+def got_sums(in_ref, each):
+    cores = lax.axis_size("faces")
+    count = in_ref.shape[0] // cores
+    parts = []
+    for q in range(count):
+        ahead = partition(-q, count)
+        core = jnp.where((ahead >= 1) & (ahead <= each), 1, 0)
+        parts.append(in_ref[q * cores + core])
+    return total_of(parts)
+
+
 def spread(column, i):
     return jnp.broadcast_to(column[i : i + 1, :], (SUB, LANES))
 
@@ -110,53 +141,66 @@
 
 
 def prefix_matrix():
-    shape = (3 * LANES, LANES)
-    upto = (lax.broadcasted_iota(I32, shape, 0) % LANES) <= lax.broadcasted_iota(I32, shape, 1)
+    shape = (2 * LANES, LANES)
+    upto = (lax.broadcasted_iota(I32, shape, 0) & (LANES - 1)) <= lax.broadcasted_iota(I32, shape, 1)
     return jnp.where(upto, 1.0, 0.0).astype(jnp.bfloat16)
 
 
-def prefix_sums(blocks, matrix):
-    values = jnp.concatenate(blocks, axis=0)
+def prefix_sums(values, matrix):
     high = values.astype(jnp.bfloat16)
-    rest = values - high.astype(F32)
-    middle = rest.astype(jnp.bfloat16)
-    low = (rest - middle.astype(F32)).astype(jnp.bfloat16)
-    split = jnp.concatenate([high, middle, low], axis=1)
-    sums = jnp.dot(split, matrix, preferred_element_type=F32)
-    return [sums[i * SUB : (i + 1) * SUB, :] for i in range(len(blocks))]
-
-
-def to_cells(fluxes, tables, g, matrix, signs):
-    rows, parts = len(fluxes), len(fluxes[0])
-    order_ref, last_ref = tables
-    blocks = []
-    for side in range(2):
-        for r in range(rows):
-            order = order_ref[side, r, rows8(g), :]
-            blocks += [pick(fluxes[r][c], order) for c in range(parts)]
-    sums = prefix_sums(blocks, matrix)
-    totals = []
-    for side, of in ((0, 0), (1, 1), (1, 2)):
-        acc = None
-        for r in range(rows):
-            last = last_ref[of, r, rows8(g), :]
-            some = last >= 0
-            at = jnp.maximum(last, 0)
-            got = [
-                jnp.where(some, pick(sums[(side * rows + r) * parts + c], at), 0.0)
-                for c in range(parts)
-            ]
-            acc = got if acc is None else [a + b for a, b in zip(acc, got)]
-        totals.append(acc)
+    low = (values - high.astype(F32)).astype(jnp.bfloat16)
+    return jnp.dot(jnp.concatenate([high, low], axis=1), matrix, preferred_element_type=F32)
+
+
+def block_at(i):
+    return slice(i * SUB, i * SUB + SUB)
+
+
+def to_cells(flux_ref, order_ref, last_ref, here_ref, beside_ref, sort_ref, signs):
+    parts = len(signs)
+    tiles = here_ref.shape[1]
+    rows = order_ref.shape[1]
+    each = rows * parts
+    matrix = prefix_matrix()
+    for g in in_groups(tiles):
+        for side in range(2):
+            for r in range(rows):
+                order = order_ref[side, r, rows8(g), :]
+                for c in range(parts):
+                    source = flux_ref[block_at(g * each + r * parts + c), :]
+                    sort_ref[block_at((g * 2 + side) * each + r * parts + c), :] = pick(source, order)
+    for g in in_groups(tiles):
+        at = slice(g * 2 * each * SUB, (g + 1) * 2 * each * SUB)
+        sort_ref[at, :] = prefix_sums(sort_ref[at, :], matrix)
     lane = lane_ids()
-    here, beside = [], []
+    for g in in_groups(tiles):
+        totals = []
+        for side, of in ((0, 0), (1, 1), (1, 2)):
+            acc = None
+            for r in range(rows):
+                last = last_ref[of, r, rows8(g), :]
+                some = last >= 0
+                at = last & (LANES - 1)
+                got = [
+                    jnp.where(some, pick(sort_ref[block_at((g * 2 + side) * each + r * parts + c), :], at), 0.0)
+                    for c in range(parts)
+                ]
+                acc = got if acc is None else [a + b for a, b in zip(acc, got)]
+            totals.append(acc)
+        for c in range(parts):
+            owned, near, far = totals[0][c], totals[1][c], totals[2][c]
+            here_ref[c, rows8(g), :] = owned + near if signs[c] > 0 else owned - near
+            beside_ref[c, g * SUB + 1 : g * SUB + 1 + SUB, :] = jnp.where(lane == LANES - 1, near, far)
+            sort_ref[block_at(g * 2 * each + c), :] = far
+    for g in in_groups(tiles):
+        for c in range(parts):
+            both = here_ref[c, rows8(g), :]
+            here_ref[c, rows8(g), :] = both - jnp.where(lane == 0, 0.0, pltpu.roll(both, 1, 1))
+            at = slice(g * SUB + 1, g * SUB + 1 + SUB)
+            before = pltpu.roll(beside_ref[c, at, :], 1, 1)
+            beside_ref[c, at, :] = sort_ref[block_at(g * 2 * each + c), :] - before
     for c in range(parts):
-        owned, near, far = totals[0][c], totals[1][c], totals[2][c]
-        both = owned + near if signs[c] > 0 else owned - near
-        here.append(both - jnp.where(lane == 0, 0.0, pltpu.roll(both, 1, 1)))
-        before = pltpu.roll(jnp.where(lane == LANES - 1, near, far), 1, 1)
-        beside.append(far - before)
-    return here, beside
+        beside_ref[c, 0:1, :] = beside_ref[c, tiles : tiles + 1, :]
 
 
 def face_values(wide_ref, halo_ref, owner, code, g, lists, parts):
@@ -165,16 +209,17 @@
     at = code & (LANES - 1)
     source = code >> 7
     first = (g * SUB) % lists
-    left, right = [], []
+    own = [wide_ref[c, rows8(g), :] for c in range(parts)]
+    left = [pick(v, owner) for v in own]
+    right = [pick(v, at) for v in own]
+    masks = [source == i for i in range(1, 2 + halves)]
     for c in range(parts):
-        own = wide_ref[c, rows8(g), :]
-        left.append(pick(own, owner))
-        got = pick(own, at)
-        got = jnp.where(source == 1, pick(wide_ref[c, g * SUB + 1 : g * SUB + 1 + SUB, :], at), got)
+        others = [wide_ref[c, g * SUB + 1 : g * SUB + 1 + SUB, :]]
         for h in range(halves):
-            base = (c * halves + h) * span + first
-            got = jnp.where(source == 2 + h, pick(halo_ref[base : base + SUB, :], at), got)
-        right.append(got)
+            base = (h * BLOCK + c) * span + first
+            others.append(halo_ref[base : base + SUB, :])
+        for mask, other in zip(masks, others):
+            right[c] = jnp.where(mask, pick(other, at), right[c])
     return left, right
 
 
@@ -183,17 +228,10 @@
         wide_ref[c, tiles : tiles + 1, :] = wide_ref[c, 0:1, :]
 
 
-def wrap_beside(beside_ref, tiles):
-    for c in range(beside_ref.shape[0]):
-        beside_ref[c, 0:1, :] = beside_ref[c, tiles : tiles + 1, :]
-
-
-def face_part(wide_ref, halo_ref, face_ref, link_ref, tables, here_ref, beside_ref, lists):
+def face_part(wide_ref, halo_ref, face_ref, link_ref, tables, here_ref, beside_ref, flux_ref, sort_ref, lists):
     tiles = here_ref.shape[1]
     rows = face_ref.shape[1]
-    matrix = prefix_matrix()
-    for g in in_groups(tiles):
-        fluxes = []
+    for g in in_groups(tiles):
         for r in range(rows):
             owner, code = link_ref[0, r, rows8(g), :], link_ref[1, r, rows8(g), :]
             left, right = face_values(wide_ref, halo_ref, owner, code, g, lists, BLOCK)
@@ -203,12 +241,9 @@
             normal = (n0, n1, n2)
             flux = [speed * both[i] + normal[i] * both[3] + wave * gap[i] for i in range(3)]
             flux.append(n0 * both[0] + n1 * both[1] + n2 * both[2] + wave * gap[3])
-            fluxes.append(flux)
-        here, beside = to_cells(fluxes, tables, g, matrix, (-1,) * BLOCK)
-        for c in range(BLOCK):
-            here_ref[c, rows8(g), :] = here[c]
-            beside_ref[c, g * SUB + 1 : g * SUB + 1 + SUB, :] = beside[c]
-    wrap_beside(beside_ref, tiles)
+            for c in range(BLOCK):
+                flux_ref[block_at((g * rows + r) * BLOCK + c), :] = flux[c]
+    to_cells(flux_ref, *tables, here_ref, beside_ref, sort_ref, (-1,) * BLOCK)
 
 
 def precondition(vector, diag_ref, g):
@@ -248,9 +283,10 @@
 def start_kernel(
     count_ref, used_ref, normal_ref, owner_ref, neighbour_ref, flow_ref, list_ref,
     pack_ref, out_ref, flow_out, send_ref,
-    stage_ref, *, shifts, cells_here,
+    stage_ref, *, cells_here,
 ):
     lists, width = list_ref.shape
+    each = lists // 2
     halves = width // LANES
     tiles = cells_here // LANES
     pairs = tiles // 2
@@ -276,17 +312,19 @@
         for c in range(BLOCK):
             flow_out[c, t : t + 1, :] = flow_ref[c : c + 1, t * LANES : (t + 1) * LANES]
     sub = sub_ids()
+    core = lax.axis_index("faces")
     used = jnp.zeros((SUB, LANES), I32)
-    for k in range(lists):
-        used = jnp.where(sub == k, used_ref[k], used)
-    for h in range(halves):
-        for k in range(lists):
-            stage_ref[k : k + 1, :] = list_ref[k : k + 1, h * LANES : (h + 1) * LANES].astype(F32)
-        listed_cell = stage_ref[0:SUB, :].astype(I32)
-        alive = (lane_ids() + h * LANES < used) & (sub < lists)
-        send_ref[h] = jnp.where(alive, listed_cell >> 7, -1)
-        send_ref[halves + h] = jnp.where(alive, listed_cell & (LANES - 1), 0)
-    send_halo(listed(flow_out, send_ref), stage_ref, out_ref, shifts)
+    for j in range(each):
+        for h in range(halves):
+            i = j * halves + h
+            rows = [list_ref[k : k + 1, h * LANES : (h + 1) * LANES] for k in (j, each + j)]
+            stage_ref[i : i + 1, :] = jnp.where(core == 0, *rows).astype(F32)
+            used = jnp.where(sub == i, used_ref[core * each + j] - h * LANES, used)
+    cells = stage_ref[0:SUB, :].astype(I32)
+    alive = (lane_ids() < used) & (sub < each * halves)
+    send_ref[0] = jnp.where(alive, cells >> 7, -1)
+    send_ref[1] = jnp.where(alive, cells & (LANES - 1), 0)
+    send_halo(listed(flow_out, send_ref), stage_ref, out_ref, each)
 
 
 def sorted_columns(x):
@@ -322,9 +360,27 @@
     return x
 
 
-def sort_rows(key_ref):
+def counts_below(x, first):
+    sub = sub_ids()
+    rows = []
+    heads = [jnp.broadcast_to(x[15][s : s + 1, :], (SUB, LANES)) for s in range(SUB)]
+    for w in range(LANES // SUB):
+        bound = ((sub + (first + w * SUB + 1)) * LANES).astype(F32)
+        block = jnp.zeros((SUB, LANES), I32)
+        for s in range(SUB):
+            block = jnp.where(heads[s] < bound, s + 1, block)
+        at = jnp.minimum(block, SUB - 1)
+        inside = jnp.zeros((SUB, LANES), I32)
+        for v in range(15):
+            inside = jnp.where(pick_row(x[v], at) < bound, v + 1, inside)
+        rows.append((block * 16 + jnp.where(block < SUB, inside, 0)).astype(F32))
+    return rows
+
+
+def sort_rows(key_ref, lower_ref, upper_ref):
     lane = lane_ids()
     back = 8 * (lane & 15) + (lane >> 4)
+    skip = lower_ref.shape[0] - upper_ref.shape[0]
     for b in range(key_ref.shape[0] // LANES):
         at = slice(b * LANES, (b + 1) * LANES)
         turned = jnp.transpose(key_ref[at, :])
@@ -333,19 +389,16 @@
         for v in range(16):
             row = b * LANES + v * SUB
             key_ref[row : row + SUB, :] = pick(turned[v * SUB : (v + 1) * SUB, :], back)
-
-
-def last_below(keys, bound):
-    at = jnp.zeros((SUB, LANES), I32)
-    for step in (64, 32, 16, 8, 4, 2, 1):
-        at = jnp.where(pick(keys, at + (step - 1)) < bound, at + step, at)
-    return jnp.where(pick(keys, at) < bound, at, at - 1)
+        lower_ref[at, :] = jnp.transpose(jnp.concatenate(counts_below(x, 0), axis=0))
+        if b * LANES >= skip:
+            at = slice(b * LANES - skip, (b + 1) * LANES - skip)
+            upper_ref[at, :] = jnp.transpose(jnp.concatenate(counts_below(x, LANES), axis=0))
 
 
 def setup_kernel(
     mine_ref, peer_ref, in_ref, flow_ref, source_ref, volume_ref, send_ref,
     face_ref, link_ref, order_ref, last_ref, diag_ref, source_out, pre_ref, out_ref,
-    stage_ref, halo_ref, wide_ref, key_ref, here_ref, beside_ref, tile_ref, *, shifts,
+    stage_ref, halo_ref, wide_ref, key_ref, here_ref, beside_ref, tile_ref, flux_ref, sort_ref, lower_ref, upper_ref, *, shifts,
 ):
     lists = len(shifts)
     tiles = volume_ref.shape[0]
@@ -379,7 +432,8 @@
             key_ref[at : at + SUB, :] = (owner * LANES + lane).astype(F32)
             at += 3 * tiles
             key_ref[at : at + SUB, :] = (jnp.minimum(code, 256) * LANES + lane).astype(F32)
-    sort_rows(key_ref)
+    sort_rows(key_ref, lower_ref, upper_ref)
+    skip = lower_ref.shape[0] - upper_ref.shape[0]
     for r in range(3):
         for g in in_groups(tiles):
             at = r * tiles + g * SUB
@@ -387,17 +441,16 @@
             near = key_ref[at + 3 * tiles : at + 3 * tiles + SUB, :]
             order_ref[0, r, rows8(g), :] = owned.astype(I32) & (LANES - 1)
             order_ref[1, r, rows8(g), :] = near.astype(I32) & (LANES - 1)
-            bound = ((lane + 1) * LANES).astype(F32)
-            last_ref[0, r, rows8(g), :] = last_below(owned, bound)
-            last_ref[1, r, rows8(g), :] = last_below(near, bound)
-            last_ref[2, r, rows8(g), :] = last_below(near, bound + float(LANES * LANES))
+            near = at + 3 * tiles
+            for i, count in enumerate(
+                (lower_ref[at : at + SUB, :], lower_ref[near : near + SUB, :], upper_ref[near - skip : near - skip + SUB, :])
+            ):
+                last_ref[i, r, rows8(g), :] = count.astype(I32) - 1
     for g in in_groups(tiles):
         put(wide_ref, g, cell(flow_ref, g))
     widen(wide_ref, tiles)
     lay_halo(got_halo(in_ref, shifts), halo_ref)
-    matrix = prefix_matrix()
-    for g in in_groups(tiles):
-        terms = []
+    for g in in_groups(tiles):
         for r in range(3):
             owner, code = link_ref[0, r, rows8(g), :], link_ref[1, r, rows8(g), :]
             left, right = face_values(wide_ref, halo_ref, owner, code, g, lists, 3)
@@ -412,12 +465,8 @@
             term = [0.5 * speed] + [0.5 * n for n in normal] + [0.5 * wave]
             for i in range(5):
                 face_ref[i, r, rows8(g), :] = term[i]
-            terms.append(term)
-        here, beside = to_cells(terms, (order_ref, last_ref), g, matrix, (-1, -1, -1, -1, 1))
-        for i in range(5):
-            here_ref[i, rows8(g), :] = here[i]
-            beside_ref[i, g * SUB + 1 : g * SUB + 1 + SUB, :] = beside[i]
-    wrap_beside(beside_ref, tiles)
+                flux_ref[block_at((g * 3 + r) * 5 + i), :] = term[i]
+    to_cells(flux_ref, order_ref, last_ref, here_ref, beside_ref, sort_ref, (-1, -1, -1, -1, 1))
     for g in in_groups(tiles):
         volume = volume_ref[rows8(g), :]
         own = [here_ref[i, rows8(g), :] for i in range(5)]
@@ -429,7 +478,7 @@
         for i, value in enumerate((inverse, n0, n1, n2, 1.0 / schur)):
             diag_ref[i, rows8(g), :] = value
         put(pre_ref, g, precondition(cell(source_out, g), diag_ref, g))
-    send_halo(listed(pre_ref, send_ref), stage_ref, out_ref, shifts)
+    send_halo(listed(pre_ref, send_ref), stage_ref, out_ref, len(shifts) // 2)
 
 
 def combine(scales, vectors):
@@ -446,7 +495,7 @@
 def first_kernel(
     in_ref, pre_ref, source_ref, volume_ref, face_ref, link_ref, order_ref, last_ref, diag_ref, send_ref,
     image_ref, mimage_ref, out_ref,
-    stage_ref, halo_ref, wide_ref, here_ref, beside_ref, *, shifts,
+    stage_ref, halo_ref, wide_ref, here_ref, beside_ref, flux_ref, sort_ref, *, shifts,
 ):
     tiles = volume_ref.shape[0]
     groups = in_groups(tiles)
@@ -454,7 +503,7 @@
         put(wide_ref, g, cell(pre_ref, g))
     widen(wide_ref, tiles)
     lay_halo(got_halo(in_ref, shifts), halo_ref)
-    face_part(wide_ref, halo_ref, face_ref, link_ref, (order_ref, last_ref), here_ref, beside_ref, len(shifts))
+    face_part(wide_ref, halo_ref, face_ref, link_ref, (order_ref, last_ref), here_ref, beside_ref, flux_ref, sort_ref, len(shifts))
     product, rho = zero(), zero()
     for g in groups:
         image = applied(g, volume_ref, wide_ref, here_ref, beside_ref)
@@ -464,18 +513,18 @@
         put(image_ref, g, image)
         put(mimage_ref, g, precondition(image, diag_ref, g))
     send_sums((product, rho), out_ref)
-    send_halo(listed(mimage_ref, send_ref), stage_ref, out_ref, shifts)
+    send_halo(listed(mimage_ref, send_ref), stage_ref, out_ref, len(shifts) // 2)
 
 
 def second_kernel(
     in1_ref, in2_ref, pre_ref, mimage_ref, image_ref, source_ref,
     volume_ref, face_ref, link_ref, order_ref, last_ref, diag_ref, send_ref,
     middle_ref, premid_ref, second_ref, msecond_ref, scale_ref, out_ref,
-    stage_ref, halo_ref, wide_ref, here_ref, beside_ref, *, shifts,
+    stage_ref, halo_ref, wide_ref, here_ref, beside_ref, flux_ref, sort_ref, *, shifts,
 ):
     tiles = volume_ref.shape[0]
     groups = in_groups(tiles)
-    sums = got_sums(in2_ref)
+    sums = got_sums(in2_ref, len(shifts) // 2)
     rho = spread(sums, 1)
     alpha = rho / spread(sums, 0)
     scale_ref[0:1, :] = alpha[0:1, :]
@@ -486,7 +535,7 @@
         put(premid_ref, g, premid)
     widen(wide_ref, tiles)
     lay_halo(combine((None, -alpha), (got_halo(in1_ref, shifts), got_halo(in2_ref, shifts))), halo_ref)
-    face_part(wide_ref, halo_ref, face_ref, link_ref, (order_ref, last_ref), here_ref, beside_ref, len(shifts))
+    face_part(wide_ref, halo_ref, face_ref, link_ref, (order_ref, last_ref), here_ref, beside_ref, flux_ref, sort_ref, len(shifts))
     products = [zero() for _ in range(4)]
     for g in groups:
         second = applied(g, volume_ref, wide_ref, here_ref, beside_ref)
@@ -498,18 +547,18 @@
         for i, (a, b) in enumerate(((second, middle), (second, second), (source, middle), (source, second))):
             products[i] = added(products[i], a, b)
     send_sums(products, out_ref)
-    send_halo(listed(msecond_ref, send_ref), stage_ref, out_ref, shifts)
+    send_halo(listed(msecond_ref, send_ref), stage_ref, out_ref, len(shifts) // 2)
 
 
 def third_kernel(
     in1_ref, in2_ref, in3_ref, scale_ref, pre_ref, mimage_ref, premid_ref, msecond_ref, middle_ref, second_ref, source_ref,
     volume_ref, face_ref, link_ref, order_ref, last_ref, diag_ref, send_ref,
     field_ref, residual_ref, preres_ref, predir_ref, image_ref, mimage_out, scale_out, ghost_ref, out_ref,
-    stage_ref, halo_ref, wide_ref, here_ref, beside_ref, *, shifts,
+    stage_ref, halo_ref, wide_ref, here_ref, beside_ref, flux_ref, sort_ref, *, shifts,
 ):
     tiles = volume_ref.shape[0]
     groups = in_groups(tiles)
-    sums = got_sums(in3_ref)
+    sums = got_sums(in3_ref, len(shifts) // 2)
     alpha, rho = row_of(scale_ref, 0), row_of(scale_ref, 1)
     omega = spread(sums, 0) / spread(sums, 1)
     rho_next = spread(sums, 2) - omega * spread(sums, 3)
@@ -531,7 +580,7 @@
     for k in range(len(shifts)):
         ghost_ref[k] = preres[k]
     lay_halo(combine((None, beta, drop), (preres, ghost1, ghost2)), halo_ref)
-    face_part(wide_ref, halo_ref, face_ref, link_ref, (order_ref, last_ref), here_ref, beside_ref, len(shifts))
+    face_part(wide_ref, halo_ref, face_ref, link_ref, (order_ref, last_ref), here_ref, beside_ref, flux_ref, sort_ref, len(shifts))
     product = zero()
     for g in groups:
         image = applied(g, volume_ref, wide_ref, here_ref, beside_ref)
@@ -539,18 +588,18 @@
         put(image_ref, g, image)
         put(mimage_out, g, precondition(image, diag_ref, g))
     send_sums((product,), out_ref)
-    send_halo(listed(mimage_out, send_ref), stage_ref, out_ref, shifts)
+    send_halo(listed(mimage_out, send_ref), stage_ref, out_ref, len(shifts) // 2)
 
 
 def fourth_kernel(
     in4_ref, scale_ref, ghost_ref, field_ref, residual_ref, preres_ref, predir_ref, image_ref, mimage_ref,
     volume_ref, face_ref, link_ref, order_ref, last_ref,
     field_out, premid_ref, middle_ref, second_ref, out_ref,
-    halo_ref, wide_ref, here_ref, beside_ref, *, shifts,
+    halo_ref, wide_ref, here_ref, beside_ref, flux_ref, sort_ref, *, shifts,
 ):
     tiles = volume_ref.shape[0]
     groups = in_groups(tiles)
-    alpha = row_of(scale_ref, 0) / spread(got_sums(in4_ref), 0)
+    alpha = row_of(scale_ref, 0) / spread(got_sums(in4_ref, len(shifts) // 2), 0)
     for g in groups:
         premid = combine((None, -alpha), (cell(preres_ref, g), cell(mimage_ref, g)))
         put(wide_ref, g, premid)
@@ -560,7 +609,7 @@
     widen(wide_ref, tiles)
     ghosts = [ghost_ref[k] for k in range(len(shifts))]
     lay_halo(combine((None, -alpha), (ghosts, got_halo(in4_ref, shifts))), halo_ref)
-    face_part(wide_ref, halo_ref, face_ref, link_ref, (order_ref, last_ref), here_ref, beside_ref, len(shifts))
+    face_part(wide_ref, halo_ref, face_ref, link_ref, (order_ref, last_ref), here_ref, beside_ref, flux_ref, sort_ref, len(shifts))
     cross, square = zero(), zero()
     for g in groups:
         second = applied(g, volume_ref, wide_ref, here_ref, beside_ref)
@@ -572,7 +621,7 @@
 
 def last_kernel(in_ref, field_ref, premid_ref, middle_ref, second_ref, field_out, residual_out, stage_ref):
     tiles = field_ref.shape[1]
-    sums = got_sums(in_ref)
+    sums = total_of([in_ref[d] for d in range(in_ref.shape[0])])
     omega = spread(sums, 0) / spread(sums, 1)
     for g in in_groups(tiles):
         field = combine((None, omega), (cell(field_ref, g), cell(premid_ref, g)))
@@ -599,7 +648,7 @@
 
 
 def exchange(block):
-    return lax.all_to_all(block, "cells", 0, 0)
+    return lax.all_to_all(block, ("cells", "faces"), 0, 0)
 
 
 def body(
@@ -619,9 +668,8 @@
     tiles = cells_here // LANES
     per_tile = face_owner.shape[0] // tiles
     shifts = offsets(lists // 2)
-    halves = width // LANES
     assert per_tile * 2 == 3 * LANES and lax.axis_size("faces") == 2
-    assert width == 2 * LANES and count > lists and lists <= SUB
+    assert width == 2 * LANES and count > lists and lists % 2 == 0 and lists <= SUB
     assert tiles % SUB == 0 and cells_here & (cells_here - 1) == 0
     rows = 3
     span = -(-(lists + SUB - 1) // SUB) * SUB
@@ -629,8 +677,8 @@
     vec = (vector, F32)
     faces = (rows, tiles, LANES)
     scale = ((SUB, LANES), F32)
-    halo_block = ((count, SUB, LANES), F32)
-    full_block = ((count, 2 * SUB, LANES), F32)
+    sum_block = ((count, SUB, LANES), F32)
+    full_block = ((2 * count, SUB, LANES), F32)
     wide = (BLOCK, tiles + SUB, LANES)
     stage = (SUB * SUB, LANES)
     halo = (SUB * span, LANES)
@@ -638,8 +686,8 @@
     volume = volume_rate.reshape(tiles, LANES)
 
     pack, out0, flow, send = run(
-        functools.partial(start_kernel, shifts=shifts, cells_here=cells_here),
-        [((4, flat, LANES), F32), halo_block, vec, ((2 * halves, SUB, LANES), I32)],
+        functools.partial(start_kernel, cells_here=cells_here),
+        [((4, flat, LANES), F32), full_block, vec, ((2, SUB, LANES), I32)],
         [stage],
         (
             face_count, halo_count, face_normal, face_owner.reshape(flat, LANES),
@@ -653,13 +701,13 @@
         functools.partial(setup_kernel, shifts=shifts),
         [
             ((5,) + faces, F32), ((2,) + faces, I32), ((2,) + faces, I32), ((3,) + faces, I32),
-            ((5, tiles, LANES), F32), vec, vec, halo_block,
+            ((5, tiles, LANES), F32), vec, vec, full_block,
         ],
-        [stage, halo, wide, (6 * tiles, LANES), (5, tiles, LANES), (5, tiles + SUB, LANES), (12, tiles, LANES)],
+        [stage, halo, wide, (6 * tiles, LANES), (5, tiles, LANES), (5, tiles + SUB, LANES), (12, tiles, LANES), (rows * 5 * tiles, LANES), (2 * rows * 5 * tiles, LANES), (6 * tiles, LANES), (4 * tiles, LANES)],
         (pack, peer, in0, flow, source_term, volume, send),
     )
     in1 = exchange(out1)
-    work = [stage, halo, wide, vector, wide]
+    work = [stage, halo, wide, vector, wide, (rows * BLOCK * tiles, LANES), (2 * rows * BLOCK * tiles, LANES)]
     fixed = (volume, face, link, order, last, diag, send)
     image, mimage, out2 = run(
         functools.partial(first_kernel, shifts=shifts), [vec, vec, full_block], work, (in1, predir, source) + fixed
@@ -681,11 +729,11 @@
     in4 = exchange(out4)
     field, premid, middle, second, out5 = run(
         functools.partial(fourth_kernel, shifts=shifts),
-        [vec, vec, vec, vec, halo_block],
+        [vec, vec, vec, vec, sum_block],
         work[1:],
         (in4, scales, ghosts, field, residual, preres, predir, image, mimage) + fixed[:5],
     )
-    in5 = exchange(out5)
+    in5 = lax.all_to_all(out5, "cells", 0, 0)
     out = (flow_state.shape, F32)
     field, residual = run(last_kernel, [out, out], [(2,) + vector], (in5, field, premid, middle, second))
     return (field, residual)

time: 107 us -> 87.2 us (0.81)
  Pallas kernels: 33.4 us -> 14.9 us
  blocking collectives: 66.6 us -> 50.2 us
  waiting for transfers between devices: 0.01 us -> 7.89 us
  starting transfers between devices: 0.56 us -> 7.64 us
    pallas_call x7, Pallas kernels: 33.4 us -> 14.9 us  [run(): pl.pallas_call(kernel, out_shape=[jax.ShapeDtypeStruct(shape, dtype) for...]
    all_to_all x6 -> x5, blocking collectives: 66.6 us -> 50.2 us  [the longest x4 39.9 us: exchange(): return lax.all_to_all(block, ('cells', 'faces'), 0, 0)]
    all_to_all x0 -> x1, starting transfers between devices: none -> 7.33 us  [exchange(): return lax.all_to_all(block, ('cells', 'faces'), 0, 0)]
    all_to_all x0 -> x1, waiting for transfers between devices: none -> 6.7 us  [exchange(): return lax.all_to_all(block, ('cells', 'faces'), 0, 0)]
    ppermute x1, waiting for transfers between devices: 0.01 us -> 1.19 us  [body(): peer = lax.ppermute(pack, 'faces', [(0, 1), (1, 0)])]
  transfers between devices with their start and end apart: 1 -> 2, of which waited for: 0 -> 2; matrix products, arithmetic and copies ran while one was open for 0% -> 0% of each run, Pallas kernels for 0% -> 0%
where the time goes in v2:
time: 87.2 us; the launch traced here: 86.7 us
  blocking collectives  50.2 us (58%)
  Pallas kernels  14.9 us (17%)
  waiting for transfers between devices  7.89 us (9%)
  starting transfers between devices  7.64 us (9%)
  local copies, waits for them, and re-layouts  4.78 us (5%)
  between operations  1.32 us (2%)
    all_to_all x4, blocking collectives, exchange(): return lax.all_to_all(block, ('cells', 'faces'), 0, 0)  39.9 us
    pallas_call x7, Pallas kernels, run(): pl.pallas_call(kernel, out_shape=[jax.ShapeDtypeStruct(shape, dtype) for...  14.9 us
    all_to_all x1, blocking collectives, body(): in5 = lax.all_to_all(out5, 'cells', 0, 0)  10.3 us
    all_to_all x1, starting transfers between devices, exchange(): return lax.all_to_all(block, ('cells', 'faces'), 0, 0)  7.33 us
    all_to_all x1, waiting for transfers between devices, exchange(): return lax.all_to_all(block, ('cells', 'faces'), 0, 0)  6.7 us
    unnamed x16, local copies, waits for them, and re-layouts  4.78 us
  transfers between devices with their start and end apart: 2, of which 2 were waited for; matrix products, arithmetic and copies ran while one was open for 0% of the time, Pallas kernels for 0%

profile of v2, /device:TPU:0, one launch (start us, length us, event | category | flops | bytes accessed | tf_op | source)
XLA Modules:
  0.0 86.7 jit_solution(16436855232486184379)
XLA Ops:
  1.3 0.0 copy-start.7
  1.3 0.6 copy-done.7
  1.9 0.0 copy-start.1
  1.9 0.9 %copy-done.1 = f32[3,12288]{1,0:T(4,128)S(1)} copy-done((f32[3,12288]{1,0:T(4,128)S(1)}, f32[3,12288]{1,0:T(4,128)}, u32[]{:S(2)}) %copy-start.1) | copy-done | bytes 147480
  2.9 0.0 copy-start.3
  2.9 0.9 %copy-done.3 = f32[4,8192]{1,0:T(4,128)S(1)} copy-done((f32[4,8192]{1,0:T(4,128)S(1)}, f32[4,8192]{1,0:T(4,128)}, u32[]{:S(2)}) %copy-start.3) | copy-done | bytes 131096
  3.8 0.0 copy-start.4
  3.8 0.8 copy-done.4
  4.6 0.0 copy-start.5
  4.6 0.8 copy-done.5
  5.4 0.0 copy-start.6
  5.4 0.7 copy-done.6
  6.1 1.7 %shard_map.104 = (f32[4,96,128]{2,1,0:T(8,128)S(1)}, f32[32,8,128]{2,1,0:T(8,128)}, f32[4,64,128]{2,1,0:T(8,128)S(1)}, s32[2,8,128]{2,1,0:T(8,128)S(1)}) custom-call(s32[1]{0:T(128)S(6)} %copy.11.count_ref, s32[6]{0:T(128)S(1)} %copy-done.7, f32[3,12288]{1,0:T(4,128)S(1)} %copy-done.1, s32[96,128]{1,0:T(8,128)S(1)} %bitcast.8, s32[96,128]{1,0:T(8,128)S(1)} %bitcast.9, ...), custom_call_target="tpu_custom_call" | custom-call | tf_op jit(solution)/shard_map/pallas_call | solution.py:640
  7.8 0.0 copy-start
  7.8 0.0 copy-start.2
  7.8 7.3 %all-to-all-start = ((f32[32,8,128]{2,1,0:T(8,128)}), f32[32,8,128]{2,1,0:T(8,128)S(1)}, u32[]{:S(2)}, u32[]{:S(2)}) async-start(f32[32,8,128]{2,1,0:T(8,128)} %get-tuple-element.38), calls=%async_computation | async-start | bytes 262144 | tf_op jit(solution)/shard_map/all_to_all | solution.py:651
  15.1 0.3 collective-permute-start
  15.4 1.2 %collective-permute-done.peer_ref = f32[4,96,128]{2,1,0:T(8,128)S(1)} collective-permute-done((f32[4,96,128]{2,1,0:T(8,128)S(1)}, f32[4,96,128]{2,1,0:T(8,128)S(1)}, u32[]{:S(2)}, u32[]{:S(2)}) %collective-permute-start) | collective-permute-done | bytes 196640 | tf_op jit(solution)/shard_map/ppermute | solution.py:698
  16.6 6.7 %all-to-all-done.in_ref = f32[32,8,128]{2,1,0:T(8,128)S(1)} async-done(((f32[32,8,128]{2,1,0:T(8,128)}), f32[32,8,128]{2,1,0:T(8,128)S(1)}, u32[]{:S(2)}, u32[]{:S(2)}) %all-to-all-start) | async-done | bytes 131104 | tf_op jit(solution)/shard_map/all_to_all | solution.py:651
  23.3 0.0 copy-done
  23.3 0.0 copy-done.2
  23.3 3.5 %shard_map.105 = (f32[5,3,64,128]{3,2,1,0:T(8,128)S(1)}, s32[2,3,64,128]{3,2,1,0:T(8,128)S(1)}, s32[2,3,64,128]{3,2,1,0:T(8,128)S(1)}, s32[3,3,64,128]{3,2,1,0:T...) custom-call(f32[4,96,128]{2,1,0:T(8,128)S(1)} %get-tuple-element.37., ...), custom_call_target="tpu_custom_call" | custom-call | tf_op jit(solution)/shard_map/pallas_call | solution.py:640
  26.8 10.0 %all_to_all.30.in_ref.in1_ref = f32[32,8,128]{2,1,0:T(8,128)S(1)} all-to-all(f32[32,8,128]{2,1,0:T(8,128)S(1)} %get-tuple-element.41), channel_id=1, replica_groups=mesh['cells'=16,'faces'=2] {'cells','faces'}, dimensions={0} | all-to-all | bytes 262144 | tf_op jit(solution)/shard_map/all_to_all | solution.py:651
  36.8 2.1 %shard_map.106 = (f32[4,64,128]{2,1,0:T(8,128)S(1)}, f32[4,64,128]{2,1,0:T(8,128)S(1)}, f32[32,8,128]{2,1,0:T(8,128)S(1)}) custom-call(f32[32,8,128]{2,1,0:T(8,128)S(1)} %all_to_all.30.in_ref.in1_ref, f32[4,64,128]{2,1,0:T(8,128)S(1)} %get-tuple-element.42.pre_ref, f32[4,64,128]{2,1,0:T(8,128)S(1)} %get-tuple-element.43.source_ref, f32[64,128]{1,0:T(8,128)S(1)} %bitcast.4, ...), custom_call_target="tpu_custom_call" | custom-call | tf_op jit(solution)/shard_map/pallas_call | solution.py:640
  38.9 10.0 %all_to_all.31.in2_ref = f32[32,8,128]{2,1,0:T(8,128)S(1)} all-to-all(f32[32,8,128]{2,1,0:T(8,128)S(1)} %get-tuple-element.49), channel_id=1, replica_groups=mesh['cells'=16,'faces'=2] {'cells','faces'}, dimensions={0} | all-to-all | bytes 262144 | tf_op jit(solution)/shard_map/all_to_all | solution.py:651
  48.9 2.3 %shard_map.107 = (f32[4,64,128]{2,1,0:T(8,128)S(1)}, f32[4,64,128]{2,1,0:T(8,128)S(1)}, f32[4,64,128]{2,1,0:T(8,128)S(1)}, f32[4,64,128]{2,1,0:T(8,128)S(1)}, f3...) custom-call(f32[32,8,128]{2,1,0:T(8,128)S(1)} %all_to_all.30.in_ref.in1_ref, f32[32,8,128]{2,1,0:T(8,128)S(1)} %all_to_all.31.in2_ref, ...), custom_call_target="tpu_custom_call" | custom-call | tf_op jit(solution)/shard_map/pallas_call | solution.py:640
  51.1 10.0 %all_to_all.32.in3_ref = f32[32,8,128]{2,1,0:T(8,128)S(1)} all-to-all(f32[32,8,128]{2,1,0:T(8,128)S(1)} %get-tuple-element.52), channel_id=1, replica_groups=mesh['cells'=16,'faces'=2] {'cells','faces'}, dimensions={0} | all-to-all | bytes 262144 | tf_op jit(solution)/shard_map/all_to_all | solution.py:651
  61.1 2.3 %shard_map.108 = (f32[4,64,128]{2,1,0:T(8,128)S(1)}, f32[4,64,128]{2,1,0:T(8,128)S(1)}, f32[4,64,128]{2,1,0:T(8,128)S(1)}, f32[4,64,128]{2,1,0:T(8,128)S(1)}, f3...) custom-call(f32[32,8,128]{2,1,0:T(8,128)S(1)} %all_to_all.30.in_ref., ...), custom_call_target="tpu_custom_call" | custom-call | tf_op jit(solution)/shard_map/pallas_call | solution.py:640
  63.4 10.0 %all_to_all.33.in4_ref = f32[32,8,128]{2,1,0:T(8,128)S(1)} all-to-all(f32[32,8,128]{2,1,0:T(8,128)S(1)} %get-tuple-element.58), channel_id=1, replica_groups=mesh['cells'=16,'faces'=2] {'cells','faces'}, dimensions={0} | all-to-all | bytes 262144 | tf_op jit(solution)/shard_map/all_to_all | solution.py:651
  73.4 2.0 %shard_map.109 = (f32[4,64,128]{2,1,0:T(8,128)S(1)}, f32[4,64,128]{2,1,0:T(8,128)S(1)}, f32[4,64,128]{2,1,0:T(8,128)S(1)}, f32[4,64,128]{2,1,0:T(8,128)S(1)}, f32[16,8,128]{2,1,0:T(8,128)S(1)}) custom-call(f32[32,8,128]{2,1,0:T(8,128)S(1)} %all_to_all.33.in4_ref, f32[8,128]{1,0:T(8,128)S(1)} %get-tuple-element.59.scale_ref, ...), custom_call_target="tpu_custom_call" | custom-call | tf_op jit(solution)/shard_map/pallas_call | solution.py:640
  75.4 10.3 %all_to_all.34.in_ref = f32[16,8,128]{2,1,0:T(8,128)S(1)} all-to-all(f32[16,8,128]{2,1,0:T(8,128)S(1)} %get-tuple-element.67), channel_id=1, replica_groups=mesh['cells'=16,'faces'=2] {'cells'}, dimensions={0} | all-to-all | bytes 131072 | tf_op jit(solution)/shard_map/all_to_all | solution.py:736
  85.7 1.0 %shard_map.110 = (f32[4,8192]{1,0:T(4,128)}, f32[4,8192]{1,0:T(4,128)}) custom-call(f32[16,8,128]{2,1,0:T(8,128)S(1)} %all_to_all.34.in_ref, f32[4,64,128]{2,1,0:T(8,128)S(1)} %get-tuple-element.68.field_ref, f32[4,64,128]{2,1,0:T(8,128)S(1)} %get-tuple-element.69.premid_ref, f32[4,64,128]{2,1,0:T(8,128)S(1)} %get-tuple-element.70.middle_ref, ...), custom_call_target="tpu_custom_call" | custom-call | tf_op jit(solution)/shard_map/pallas_call | solution.py:640
Async XLA Ops:
  1.3 0.7 copy-start.7
  1.9 0.9 %copy-start.1 = (f32[3,12288]{1,0:T(4,128)S(1)}, f32[3,12288]{1,0:T(4,128)}, u32[]{:S(2)}) copy-start(f32[3,12288]{1,0:T(4,128)} %normal_ref.1) | copy-start | bytes 442372
  2.9 0.9 %copy-start.3 = (f32[4,8192]{1,0:T(4,128)S(1)}, f32[4,8192]{1,0:T(4,128)}, u32[]{:S(2)}) copy-start(f32[4,8192]{1,0:T(4,128)} %flow_ref.1) | copy-start | bytes 393220
  3.8 0.8 copy-start.4
  4.6 0.8 copy-start.5
  5.4 0.7 copy-start.6
  7.8 15.5 %copy-start = (f32[8192]{0:T(1024)S(1)}, f32[8192]{0:T(1024)}, u32[]{:S(2)}) copy-start(f32[8192]{0:T(1024)} %param.11) | copy-start | bytes 98308
  7.8 15.5 %copy-start.2 = (f32[4,8192]{1,0:T(4,128)S(1)}, f32[4,8192]{1,0:T(4,128)}, u32[]{:S(2)}) copy-start(f32[4,8192]{1,0:T(4,128)} %source_ref.1) | copy-start | bytes 393220
  7.8 15.5 %all-to-all-start = ((f32[32,8,128]{2,1,0:T(8,128)}), f32[32,8,128]{2,1,0:T(8,128)S(1)}, u32[]{:S(2)}, u32[]{:S(2)}) async-start(f32[32,8,128]{2,1,0:T(8,128)} %get-tuple-element.38), calls=%async_computation | async-start | bytes 262144 | tf_op jit(solution)/shard_map/all_to_all | solution.py:651
  15.1 1.5 %collective-permute-start = (f32[4,96,128]{2,1,0:T(8,128)S(1)}, f32[4,96,128]{2,1,0:T(8,128)S(1)}, u32[]{:S(2)}, u32[]{:S(2)}) collective-permute-start(f32[4,96,128]{2,1,0:T(8,128)S(1)} %get-tuple-element.37.mine_ref), channel_id=1, source_target_pairs={{0,1},{1,0},{2,3},{3,2},{4,5},{5,4},{6,7},{7,6},{8,9},{9,8},{10,11... | collective-permute-start | bytes 589832 | tf_op jit(solution)/shard_map/ppermute | solution.py:698

commit v3 on v2

--- a/solution.py
+++ b/solution.py
@@ -65,15 +65,23 @@
     return slice(g * SUB, g * SUB + SUB)
 
 
-def listed(cell_ref, send_ref):
+def listed(row_of_tile, tiles, send_ref):
     row_at, lane_at = send_ref[0], send_ref[1]
     found = [jnp.zeros((SUB, LANES), F32) for _ in range(BLOCK)]
-    for t in range(cell_ref.shape[1]):
+    for t in range(tiles):
         here = row_at == t
         for c in range(BLOCK):
-            row = jnp.broadcast_to(cell_ref[c, t : t + 1, :], (SUB, LANES))
+            row = jnp.broadcast_to(row_of_tile(c, t), (SUB, LANES))
             found[c] = jnp.where(here, pick(row, lane_at), found[c])
     return found
+
+
+def tiled_rows(ref):
+    return lambda c, t: ref[c, t : t + 1, :]
+
+
+def flat_rows(ref):
+    return lambda c, t: ref[c : c + 1, t * LANES : (t + 1) * LANES]
 
 
 def send_halo(found, stage_ref, out_ref, each):
@@ -161,89 +169,110 @@
     tiles = here_ref.shape[1]
     rows = order_ref.shape[1]
     each = rows * parts
+    sides = 1 if beside_ref is None else 2
     matrix = prefix_matrix()
     for g in in_groups(tiles):
-        for side in range(2):
+        for side in range(sides):
             for r in range(rows):
                 order = order_ref[side, r, rows8(g), :]
                 for c in range(parts):
                     source = flux_ref[block_at(g * each + r * parts + c), :]
-                    sort_ref[block_at((g * 2 + side) * each + r * parts + c), :] = pick(source, order)
+                    sort_ref[block_at((g * sides + side) * each + r * parts + c), :] = pick(source, order)
     for g in in_groups(tiles):
-        at = slice(g * 2 * each * SUB, (g + 1) * 2 * each * SUB)
+        at = slice(g * sides * each * SUB, (g + 1) * sides * each * SUB)
         sort_ref[at, :] = prefix_sums(sort_ref[at, :], matrix)
     lane = lane_ids()
     for g in in_groups(tiles):
         totals = []
-        for side, of in ((0, 0), (1, 1), (1, 2)):
+        for side, of in ((0, 0), (1, 1), (1, 2))[: 2 * sides - 1]:
             acc = None
             for r in range(rows):
                 last = last_ref[of, r, rows8(g), :]
                 some = last >= 0
                 at = last & (LANES - 1)
                 got = [
-                    jnp.where(some, pick(sort_ref[block_at((g * 2 + side) * each + r * parts + c), :], at), 0.0)
+                    jnp.where(some, pick(sort_ref[block_at((g * sides + side) * each + r * parts + c), :], at), 0.0)
                     for c in range(parts)
                 ]
                 acc = got if acc is None else [a + b for a, b in zip(acc, got)]
             totals.append(acc)
         for c in range(parts):
+            if sides == 1:
+                here_ref[c, rows8(g), :] = totals[0][c]
+                continue
             owned, near, far = totals[0][c], totals[1][c], totals[2][c]
             here_ref[c, rows8(g), :] = owned + near if signs[c] > 0 else owned - near
             beside_ref[c, g * SUB + 1 : g * SUB + 1 + SUB, :] = jnp.where(lane == LANES - 1, near, far)
-            sort_ref[block_at(g * 2 * each + c), :] = far
+            sort_ref[block_at(g * sides * each + c), :] = far
     for g in in_groups(tiles):
         for c in range(parts):
             both = here_ref[c, rows8(g), :]
             here_ref[c, rows8(g), :] = both - jnp.where(lane == 0, 0.0, pltpu.roll(both, 1, 1))
-            at = slice(g * SUB + 1, g * SUB + 1 + SUB)
-            before = pltpu.roll(beside_ref[c, at, :], 1, 1)
-            beside_ref[c, at, :] = sort_ref[block_at(g * 2 * each + c), :] - before
+            if sides == 2:
+                at = slice(g * SUB + 1, g * SUB + 1 + SUB)
+                before = pltpu.roll(beside_ref[c, at, :], 1, 1)
+                beside_ref[c, at, :] = sort_ref[block_at(g * sides * each + c), :] - before
+    if sides == 2:
+        for c in range(parts):
+            beside_ref[c, 0:1, :] = beside_ref[c, tiles : tiles + 1, :]
+
+
+def local_values(wide_ref, link_ref, g, r, parts):
+    owner, code = link_ref[0, r, rows8(g), :], link_ref[1, r, rows8(g), :]
+    at = code & (LANES - 1)
+    source = code >> 7
+    own = [wide_ref[c, rows8(g), :] for c in range(parts)]
+    left = [pick(v, owner) for v in own]
+    right = [jnp.where(source == 0, pick(v, at), 0.0) for v in own]
     for c in range(parts):
-        beside_ref[c, 0:1, :] = beside_ref[c, tiles : tiles + 1, :]
-
-
-def face_values(wide_ref, halo_ref, owner, code, g, lists, parts):
+        other = wide_ref[c, g * SUB + 1 : g * SUB + 1 + SUB, :]
+        right[c] = jnp.where(source == 1, pick(other, at), right[c])
+    return left, right
+
+
+def halo_values(right, halo_ref, link_ref, g, r, lists):
     span = halo_ref.shape[0] // SUB
-    halves = SUB // BLOCK
+    code = link_ref[1, r, rows8(g), :]
     at = code & (LANES - 1)
     source = code >> 7
     first = (g * SUB) % lists
-    own = [wide_ref[c, rows8(g), :] for c in range(parts)]
-    left = [pick(v, owner) for v in own]
-    right = [pick(v, at) for v in own]
-    masks = [source == i for i in range(1, 2 + halves)]
+    right = list(right)
+    for h in range(SUB // BLOCK):
+        for c in range(len(right)):
+            base = (h * BLOCK + c) * span + first
+            right[c] = jnp.where(source == 2 + h, pick(halo_ref[base : base + SUB, :], at), right[c])
+    return right
+
+
+def widen(wide_ref, tiles, parts=BLOCK):
     for c in range(parts):
-        others = [wide_ref[c, g * SUB + 1 : g * SUB + 1 + SUB, :]]
-        for h in range(halves):
-            base = (h * BLOCK + c) * span + first
-            others.append(halo_ref[base : base + SUB, :])
-        for mask, other in zip(masks, others):
-            right[c] = jnp.where(mask, pick(other, at), right[c])
-    return left, right
-
-
-def widen(wide_ref, tiles):
-    for c in range(BLOCK):
         wide_ref[c, tiles : tiles + 1, :] = wide_ref[c, 0:1, :]
 
 
-def face_part(wide_ref, halo_ref, face_ref, link_ref, tables, here_ref, beside_ref, flux_ref, sort_ref, lists):
-    tiles = here_ref.shape[1]
-    rows = face_ref.shape[1]
-    for g in in_groups(tiles):
+def face_terms(normal_ref, pair_ref, g, r):
+    normal = [normal_ref[i, r, rows8(g), :] for i in range(3)]
+    return normal, pair_ref[0, r, rows8(g), :], pair_ref[1, r, rows8(g), :]
+
+
+def put_flux(flux_ref, first, normal, speed, wave, both, gap):
+    for i in range(3):
+        flux_ref[block_at(first + i), :] = speed * both[i] + normal[i] * both[3] + wave * gap[i]
+    last = normal[0] * both[0] + normal[1] * both[1] + normal[2] * both[2] + wave * gap[3]
+    flux_ref[block_at(first + 3), :] = last
+
+
+def face_part(wide_ref, halo_ref, faces, here_ref, beside_ref, flux_ref, sort_ref, lists):
+    normal_ref, pair_ref, link_ref, order_ref, last_ref = faces
+    rows = link_ref.shape[1]
+    for g in in_groups(here_ref.shape[1]):
         for r in range(rows):
-            owner, code = link_ref[0, r, rows8(g), :], link_ref[1, r, rows8(g), :]
-            left, right = face_values(wide_ref, halo_ref, owner, code, g, lists, BLOCK)
-            speed, n0, n1, n2, wave = [face_ref[i, r, rows8(g), :] for i in range(5)]
+            left, right = local_values(wide_ref, link_ref, g, r, BLOCK)
+            right = halo_values(right, halo_ref, link_ref, g, r, lists)
+            normal, speed, wave = face_terms(normal_ref, pair_ref, g, r)
             both = [a + b for a, b in zip(left, right)]
             gap = [a - b for a, b in zip(left, right)]
-            normal = (n0, n1, n2)
-            flux = [speed * both[i] + normal[i] * both[3] + wave * gap[i] for i in range(3)]
-            flux.append(n0 * both[0] + n1 * both[1] + n2 * both[2] + wave * gap[3])
-            for c in range(BLOCK):
-                flux_ref[block_at((g * rows + r) * BLOCK + c), :] = flux[c]
-    to_cells(flux_ref, *tables, here_ref, beside_ref, sort_ref, (-1,) * BLOCK)
+            put_flux(flux_ref, (g * rows + r) * BLOCK, normal, speed, wave, both, gap)
+    to_cells(flux_ref, order_ref, last_ref, here_ref, beside_ref, sort_ref, (-1,) * BLOCK)
 
 
 def precondition(vector, diag_ref, g):
@@ -281,13 +310,42 @@
 
 
 def start_kernel(
-    count_ref, used_ref, normal_ref, owner_ref, neighbour_ref, flow_ref, list_ref,
-    pack_ref, out_ref, flow_out, send_ref,
-    stage_ref, *, cells_here,
+    used_any, flow_any, list_any, normal_any, owner_any, neighbour_any, source_any,
+    out_ref, send_ref, flow_ref, normal_ref, owner_ref, neighbour_ref, source_ref,
+    stage_ref, list_ref, used_ref, sems,
 ):
+    pairs = (
+        (used_any, used_ref), (flow_any, flow_ref), (list_any, list_ref), (normal_any, normal_ref),
+        (owner_any, owner_ref), (neighbour_any, neighbour_ref), (source_any, source_ref),
+    )
+    copies = [pltpu.make_async_copy(a, b, sems.at[i]) for i, (a, b) in enumerate(pairs)]
+    for copy in copies:
+        copy.start()
     lists, width = list_ref.shape
     each = lists // 2
     halves = width // LANES
+    sub = sub_ids()
+    core = lax.axis_index("faces")
+    used = jnp.zeros((SUB, LANES), I32)
+    for copy in copies[:3]:
+        copy.wait()
+    for j in range(each):
+        for h in range(halves):
+            i = j * halves + h
+            rows = [list_ref[k : k + 1, h * LANES : (h + 1) * LANES] for k in (j, each + j)]
+            stage_ref[i : i + 1, :] = jnp.where(core == 0, *rows).astype(F32)
+            used = jnp.where(sub == i, used_ref[core * each + j] - h * LANES, used)
+    cells = stage_ref[0:SUB, :].astype(I32)
+    alive = (lane_ids() < used) & (sub < each * halves)
+    send_ref[0] = jnp.where(alive, cells >> 7, -1)
+    send_ref[1] = jnp.where(alive, cells & (LANES - 1), 0)
+    tiles = flow_ref.shape[1] // LANES
+    send_halo(listed(flat_rows(flow_ref), tiles, send_ref), stage_ref, out_ref, each)
+    for copy in copies[3:]:
+        copy.wait()
+
+
+def pack_kernel(count_ref, normal_ref, owner_ref, neighbour_ref, pack_ref, *, lists, width, cells_here):
     tiles = cells_here // LANES
     pairs = tiles // 2
     shape = (pairs, LANES)
@@ -307,24 +365,7 @@
         code = jnp.where(neighbour < cells_here, near, far)
         pack_ref[3, at, :] = (owner * 512 + code).astype(F32)
         for c in range(3):
-            pack_ref[c, at, :] = jnp.where(live, pack_ref[c, at, :], 0.0)
-    for t in range(tiles):
-        for c in range(BLOCK):
-            flow_out[c, t : t + 1, :] = flow_ref[c : c + 1, t * LANES : (t + 1) * LANES]
-    sub = sub_ids()
-    core = lax.axis_index("faces")
-    used = jnp.zeros((SUB, LANES), I32)
-    for j in range(each):
-        for h in range(halves):
-            i = j * halves + h
-            rows = [list_ref[k : k + 1, h * LANES : (h + 1) * LANES] for k in (j, each + j)]
-            stage_ref[i : i + 1, :] = jnp.where(core == 0, *rows).astype(F32)
-            used = jnp.where(sub == i, used_ref[core * each + j] - h * LANES, used)
-    cells = stage_ref[0:SUB, :].astype(I32)
-    alive = (lane_ids() < used) & (sub < each * halves)
-    send_ref[0] = jnp.where(alive, cells >> 7, -1)
-    send_ref[1] = jnp.where(alive, cells & (LANES - 1), 0)
-    send_halo(listed(flow_out, send_ref), stage_ref, out_ref, each)
+            pack_ref[c, at, :] = jnp.where(live, 0.5 * pack_ref[c, at, :], 0.0)
 
 
 def sorted_columns(x):
@@ -395,17 +436,13 @@
             upper_ref[at, :] = jnp.transpose(jnp.concatenate(counts_below(x, LANES), axis=0))
 
 
-def setup_kernel(
-    mine_ref, peer_ref, in_ref, flow_ref, source_ref, volume_ref, send_ref,
-    face_ref, link_ref, order_ref, last_ref, diag_ref, source_out, pre_ref, out_ref,
-    stage_ref, halo_ref, wide_ref, key_ref, here_ref, beside_ref, tile_ref, flux_ref, sort_ref, lower_ref, upper_ref, *, shifts,
+def table_kernel(
+    mine_ref, peer_ref, flow_ref,
+    normal_ref, link_ref, order_ref, last_ref, lean_ref, coupling_ref,
+    wide_ref, key_ref, beside_ref, joint_ref, flux_ref, sort_ref, lower_ref, upper_ref,
 ):
-    lists = len(shifts)
-    tiles = volume_ref.shape[0]
+    tiles = normal_ref.shape[2]
     pairs = tiles // 2
-    for t in range(tiles):
-        for c in range(BLOCK):
-            source_out[c, t : t + 1, :] = source_ref[c : c + 1, t * LANES : (t + 1) * LANES]
     swapped = lax.axis_index("faces") == 1
     lane = lane_ids((pairs, LANES))
     half = LANES // 2
@@ -419,12 +456,13 @@
         even = (a0, b0, jnp.where(lane < half, a1, pltpu.roll(b1, half, 1)))
         odd = (a2, b2, jnp.where(lane < half, pltpu.roll(a1, half, 1), b1))
         for r in range(3):
-            tile_ref[i * 3 + r, pl.ds(0, pairs, stride=2), :] = even[r]
-            tile_ref[i * 3 + r, pl.ds(1, pairs, stride=2), :] = odd[r]
+            target = normal_ref.at[i, r] if i < 3 else joint_ref.at[r]
+            target[pl.ds(0, pairs, stride=2), :] = even[r]
+            target[pl.ds(1, pairs, stride=2), :] = odd[r]
     lane = lane_ids()
     for r in range(3):
         for g in in_groups(tiles):
-            joint = tile_ref[9 + r, rows8(g), :].astype(I32)
+            joint = joint_ref[r, rows8(g), :].astype(I32)
             owner, code = joint >> 9, joint & 511
             link_ref[0, r, rows8(g), :] = owner
             link_ref[1, r, rows8(g), :] = code
@@ -446,39 +484,58 @@
                 (lower_ref[at : at + SUB, :], lower_ref[near : near + SUB, :], upper_ref[near - skip : near - skip + SUB, :])
             ):
                 last_ref[i, r, rows8(g), :] = count.astype(I32) - 1
+    for t in range(tiles):
+        for c in range(3):
+            wide_ref[c, t : t + 1, :] = flow_ref[c : c + 1, t * LANES : (t + 1) * LANES]
+    widen(wide_ref, tiles, 3)
     for g in in_groups(tiles):
-        put(wide_ref, g, cell(flow_ref, g))
-    widen(wide_ref, tiles)
+        for r in range(3):
+            left, right = local_values(wide_ref, link_ref, g, r, 3)
+            lean, size = zero(), zero()
+            for i in range(3):
+                normal = normal_ref[i, r, rows8(g), :]
+                lean = lean + normal * (left[i] + right[i])
+                size = size + normal * normal
+                flux_ref[block_at((g * 3 + r) * 3 + i), :] = normal
+            lean_ref[0, r, rows8(g), :] = lean
+            lean_ref[1, r, rows8(g), :] = 2.0 * jnp.sqrt(size)
+    to_cells(flux_ref, order_ref, last_ref, coupling_ref, beside_ref, sort_ref, (-1, -1, -1))
+    for g in in_groups(tiles):
+        for i in range(3):
+            coupling_ref[i, rows8(g), :] = coupling_ref[i, rows8(g), :] - beside_ref[i, rows8(g), :]
+
+
+def setup_kernel(
+    in_ref, source_ref, volume_ref, normal_ref, link_ref, order_ref, last_ref, lean_ref, coupling_ref, send_ref,
+    pair_ref, diag_ref, source_out, pre_ref, out_ref,
+    stage_ref, halo_ref, here_ref, beside_ref, flux_ref, sort_ref, *, shifts,
+):
+    tiles = volume_ref.shape[0]
     lay_halo(got_halo(in_ref, shifts), halo_ref)
     for g in in_groups(tiles):
         for r in range(3):
-            owner, code = link_ref[0, r, rows8(g), :], link_ref[1, r, rows8(g), :]
-            left, right = face_values(wide_ref, halo_ref, owner, code, g, lists, 3)
-            normal = [tile_ref[i * 3 + r, rows8(g), :] for i in range(3)]
-            speed = zero()
-            size = zero()
+            right = halo_values([zero() for _ in range(3)], halo_ref, link_ref, g, r, len(shifts))
+            speed = lean_ref[0, r, rows8(g), :]
             for i in range(3):
-                speed = speed + normal[i] * (left[i] + right[i])
-                size = size + normal[i] * normal[i]
-            speed = 0.5 * speed
-            wave = jnp.abs(speed) + 2.0 * jnp.sqrt(size)
-            term = [0.5 * speed] + [0.5 * n for n in normal] + [0.5 * wave]
-            for i in range(5):
-                face_ref[i, r, rows8(g), :] = term[i]
-                flux_ref[block_at((g * 3 + r) * 5 + i), :] = term[i]
-    to_cells(flux_ref, order_ref, last_ref, here_ref, beside_ref, sort_ref, (-1, -1, -1, -1, 1))
+                speed = speed + normal_ref[i, r, rows8(g), :] * right[i]
+            wave = 0.5 * jnp.abs(speed) + lean_ref[1, r, rows8(g), :]
+            for i, term in enumerate((0.5 * speed, wave)):
+                pair_ref[i, r, rows8(g), :] = term
+                flux_ref[block_at((g * 3 + r) * 2 + i), :] = term
+    to_cells(flux_ref, order_ref, last_ref, here_ref, beside_ref, sort_ref, (-1, 1))
+    for t in range(tiles):
+        for c in range(BLOCK):
+            source_out[c, t : t + 1, :] = source_ref[c : c + 1, t * LANES : (t + 1) * LANES]
     for g in in_groups(tiles):
-        volume = volume_ref[rows8(g), :]
-        own = [here_ref[i, rows8(g), :] for i in range(5)]
-        other = [beside_ref[i, rows8(g), :] for i in range(5)]
-        speed, n0, n1, n2 = [own[i] - other[i] for i in range(4)]
-        pressure_diag = volume + (own[4] + other[4])
+        n0, n1, n2 = [coupling_ref[i, rows8(g), :] for i in range(3)]
+        speed = here_ref[0, rows8(g), :] - beside_ref[0, rows8(g), :]
+        pressure_diag = volume_ref[rows8(g), :] + (here_ref[1, rows8(g), :] + beside_ref[1, rows8(g), :])
         inverse = 1.0 / (pressure_diag + speed)
         schur = pressure_diag - (n0 * n0 + n1 * n1 + n2 * n2) * inverse
         for i, value in enumerate((inverse, n0, n1, n2, 1.0 / schur)):
             diag_ref[i, rows8(g), :] = value
         put(pre_ref, g, precondition(cell(source_out, g), diag_ref, g))
-    send_halo(listed(pre_ref, send_ref), stage_ref, out_ref, len(shifts) // 2)
+    send_halo(listed(tiled_rows(pre_ref), tiles, send_ref), stage_ref, out_ref, len(shifts) // 2)
 
 
 def combine(scales, vectors):
@@ -493,7 +550,7 @@
 
 
 def first_kernel(
-    in_ref, pre_ref, source_ref, volume_ref, face_ref, link_ref, order_ref, last_ref, diag_ref, send_ref,
+    in_ref, pre_ref, source_ref, volume_ref, normal_ref, pair_ref, link_ref, order_ref, last_ref, diag_ref, send_ref,
     image_ref, mimage_ref, out_ref,
     stage_ref, halo_ref, wide_ref, here_ref, beside_ref, flux_ref, sort_ref, *, shifts,
 ):
@@ -503,7 +560,8 @@
         put(wide_ref, g, cell(pre_ref, g))
     widen(wide_ref, tiles)
     lay_halo(got_halo(in_ref, shifts), halo_ref)
-    face_part(wide_ref, halo_ref, face_ref, link_ref, (order_ref, last_ref), here_ref, beside_ref, flux_ref, sort_ref, len(shifts))
+    faces = (normal_ref, pair_ref, link_ref, order_ref, last_ref)
+    face_part(wide_ref, halo_ref, faces, here_ref, beside_ref, flux_ref, sort_ref, len(shifts))
     product, rho = zero(), zero()
     for g in groups:
         image = applied(g, volume_ref, wide_ref, here_ref, beside_ref)
@@ -513,12 +571,12 @@
         put(image_ref, g, image)
         put(mimage_ref, g, precondition(image, diag_ref, g))
     send_sums((product, rho), out_ref)
-    send_halo(listed(mimage_ref, send_ref), stage_ref, out_ref, len(shifts) // 2)
+    send_halo(listed(tiled_rows(mimage_ref), tiles, send_ref), stage_ref, out_ref, len(shifts) // 2)
 
 
 def second_kernel(
     in1_ref, in2_ref, pre_ref, mimage_ref, image_ref, source_ref,
-    volume_ref, face_ref, link_ref, order_ref, last_ref, diag_ref, send_ref,
+    volume_ref, normal_ref, pair_ref, link_ref, order_ref, last_ref, diag_ref, send_ref,
     middle_ref, premid_ref, second_ref, msecond_ref, scale_ref, out_ref,
     stage_ref, halo_ref, wide_ref, here_ref, beside_ref, flux_ref, sort_ref, *, shifts,
 ):
@@ -535,7 +593,8 @@
         put(premid_ref, g, premid)
     widen(wide_ref, tiles)
     lay_halo(combine((None, -alpha), (got_halo(in1_ref, shifts), got_halo(in2_ref, shifts))), halo_ref)
-    face_part(wide_ref, halo_ref, face_ref, link_ref, (order_ref, last_ref), here_ref, beside_ref, flux_ref, sort_ref, len(shifts))
+    faces = (normal_ref, pair_ref, link_ref, order_ref, last_ref)
+    face_part(wide_ref, halo_ref, faces, here_ref, beside_ref, flux_ref, sort_ref, len(shifts))
     products = [zero() for _ in range(4)]
     for g in groups:
         second = applied(g, volume_ref, wide_ref, here_ref, beside_ref)
@@ -547,12 +606,12 @@
         for i, (a, b) in enumerate(((second, middle), (second, second), (source, middle), (source, second))):
             products[i] = added(products[i], a, b)
     send_sums(products, out_ref)
-    send_halo(listed(msecond_ref, send_ref), stage_ref, out_ref, len(shifts) // 2)
+    send_halo(listed(tiled_rows(msecond_ref), tiles, send_ref), stage_ref, out_ref, len(shifts) // 2)
 
 
 def third_kernel(
     in1_ref, in2_ref, in3_ref, scale_ref, pre_ref, mimage_ref, premid_ref, msecond_ref, middle_ref, second_ref, source_ref,
-    volume_ref, face_ref, link_ref, order_ref, last_ref, diag_ref, send_ref,
+    volume_ref, normal_ref, pair_ref, link_ref, order_ref, last_ref, diag_ref, send_ref,
     field_ref, residual_ref, preres_ref, predir_ref, image_ref, mimage_out, scale_out, ghost_ref, out_ref,
     stage_ref, halo_ref, wide_ref, here_ref, beside_ref, flux_ref, sort_ref, *, shifts,
 ):
@@ -580,7 +639,8 @@
     for k in range(len(shifts)):
         ghost_ref[k] = preres[k]
     lay_halo(combine((None, beta, drop), (preres, ghost1, ghost2)), halo_ref)
-    face_part(wide_ref, halo_ref, face_ref, link_ref, (order_ref, last_ref), here_ref, beside_ref, flux_ref, sort_ref, len(shifts))
+    faces = (normal_ref, pair_ref, link_ref, order_ref, last_ref)
+    face_part(wide_ref, halo_ref, faces, here_ref, beside_ref, flux_ref, sort_ref, len(shifts))
     product = zero()
     for g in groups:
         image = applied(g, volume_ref, wide_ref, here_ref, beside_ref)
@@ -588,12 +648,12 @@
         put(image_ref, g, image)
         put(mimage_out, g, precondition(image, diag_ref, g))
     send_sums((product,), out_ref)
-    send_halo(listed(mimage_out, send_ref), stage_ref, out_ref, len(shifts) // 2)
+    send_halo(listed(tiled_rows(mimage_out), tiles, send_ref), stage_ref, out_ref, len(shifts) // 2)
 
 
 def fourth_kernel(
     in4_ref, scale_ref, ghost_ref, field_ref, residual_ref, preres_ref, predir_ref, image_ref, mimage_ref,
-    volume_ref, face_ref, link_ref, order_ref, last_ref,
+    volume_ref, normal_ref, pair_ref, link_ref, order_ref, last_ref,
     field_out, premid_ref, middle_ref, second_ref, out_ref,
     halo_ref, wide_ref, here_ref, beside_ref, flux_ref, sort_ref, *, shifts,
 ):
@@ -609,7 +669,8 @@
     widen(wide_ref, tiles)
     ghosts = [ghost_ref[k] for k in range(len(shifts))]
     lay_halo(combine((None, -alpha), (ghosts, got_halo(in4_ref, shifts))), halo_ref)
-    face_part(wide_ref, halo_ref, face_ref, link_ref, (order_ref, last_ref), here_ref, beside_ref, flux_ref, sort_ref, len(shifts))
+    faces = (normal_ref, pair_ref, link_ref, order_ref, last_ref)
+    face_part(wide_ref, halo_ref, faces, here_ref, beside_ref, flux_ref, sort_ref, len(shifts))
     cross, square = zero(), zero()
     for g in groups:
         second = applied(g, volume_ref, wide_ref, here_ref, beside_ref)
@@ -634,15 +695,18 @@
                     out[c : c + 1, t * LANES : (t + 1) * LANES] = stage_ref[i, c, t : t + 1, :]
 
 
-def run(kernel, outs, scratch, args, scalars=0):
+def run(kernel, outs, scratch, args, scalars=0, away=0):
     vmem = pl.BlockSpec(memory_space=pltpu.VMEM)
     smem = pl.BlockSpec(memory_space=pltpu.SMEM)
+    hbm = pl.BlockSpec(memory_space=pltpu.HBM)
+    far = range(scalars, scalars + away)
+    args = [pltpu.with_memory_space_constraint(a, pltpu.HBM) if i in far else a for i, a in enumerate(args)]
     return pl.pallas_call(
         kernel,
         out_shape=[jax.ShapeDtypeStruct(shape, dtype) for shape, dtype in outs],
-        in_specs=[smem] * scalars + [vmem] * (len(args) - scalars),
+        in_specs=[smem] * scalars + [hbm] * away + [vmem] * (len(args) - scalars - away),
         out_specs=[vmem] * len(outs),
-        scratch_shapes=[pltpu.VMEM(shape, F32) for shape in scratch],
+        scratch_shapes=[pltpu.VMEM(shape, F32) if isinstance(shape, tuple) else shape for shape in scratch],
         compiler_params=pltpu.CompilerParams(vmem_limit_bytes=24 << 20),
     )(*args)
 
@@ -679,36 +743,59 @@
     scale = ((SUB, LANES), F32)
     sum_block = ((count, SUB, LANES), F32)
     full_block = ((2 * count, SUB, LANES), F32)
-    wide = (BLOCK, tiles + SUB, LANES)
+    flat_vec = (flow_state.shape, F32)
     stage = (SUB * SUB, LANES)
     halo = (SUB * span, LANES)
     flat = face_owner.shape[0] // LANES
     volume = volume_rate.reshape(tiles, LANES)
 
-    pack, out0, flow, send = run(
-        functools.partial(start_kernel, cells_here=cells_here),
-        [((4, flat, LANES), F32), full_block, vec, ((2, SUB, LANES), I32)],
-        [stage],
+    def wide(parts):
+        return (parts, tiles + SUB, LANES)
+
+    def blocks(parts):
+        return (rows * parts * tiles, LANES)
+
+    ints = ((flat, LANES), I32)
+    out0, send, flow, slopes, owner, neighbour, source = run(
+        start_kernel,
+        [full_block, ((2, SUB, LANES), I32), flat_vec, (face_normal.shape, F32), ints, ints, flat_vec],
+        [stage, pltpu.VMEM(send_list.shape, I32), pltpu.SMEM((lists,), I32), pltpu.SemaphoreType.DMA((7,))],
         (
-            face_count, halo_count, face_normal, face_owner.reshape(flat, LANES),
-            face_neighbour.reshape(flat, LANES), flow_state, send_list,
+            halo_count, flow_state, send_list, face_normal,
+            face_owner.reshape(flat, LANES), face_neighbour.reshape(flat, LANES), source_term,
         ),
-        scalars=2,
+        away=7,
+    )
+    in0 = exchange(out0)
+    (pack,) = run(
+        functools.partial(pack_kernel, lists=lists, width=width, cells_here=cells_here),
+        [((4, flat, LANES), F32)],
+        [],
+        (face_count, slopes, owner, neighbour),
+        scalars=1,
     )
     peer = lax.ppermute(pack, "faces", [(0, 1), (1, 0)])
-    in0 = exchange(out0)
-    face, link, order, last, diag, source, predir, out1 = run(
+    normal, link, order, last, lean, coupling = run(
+        table_kernel,
+        [
+            ((3,) + faces, F32), ((2,) + faces, I32), ((2,) + faces, I32), ((3,) + faces, I32),
+            ((2,) + faces, F32), ((3, tiles, LANES), F32),
+        ],
+        [
+            wide(3), (6 * tiles, LANES), wide(3), faces,
+            blocks(3), blocks(6), (6 * tiles, LANES), (4 * tiles, LANES),
+        ],
+        (pack, peer, flow),
+    )
+    pair, diag, source, predir, out1 = run(
         functools.partial(setup_kernel, shifts=shifts),
-        [
-            ((5,) + faces, F32), ((2,) + faces, I32), ((2,) + faces, I32), ((3,) + faces, I32),
-            ((5, tiles, LANES), F32), vec, vec, full_block,
-        ],
-        [stage, halo, wide, (6 * tiles, LANES), (5, tiles, LANES), (5, tiles + SUB, LANES), (12, tiles, LANES), (rows * 5 * tiles, LANES), (2 * rows * 5 * tiles, LANES), (6 * tiles, LANES), (4 * tiles, LANES)],
-        (pack, peer, in0, flow, source_term, volume, send),
+        [((2,) + faces, F32), ((5, tiles, LANES), F32), vec, vec, full_block],
+        [stage, halo, (2, tiles, LANES), wide(2), blocks(2), blocks(4)],
+        (in0, source, volume, normal, link, order, last, lean, coupling, send),
     )
     in1 = exchange(out1)
-    work = [stage, halo, wide, vector, wide, (rows * BLOCK * tiles, LANES), (2 * rows * BLOCK * tiles, LANES)]
-    fixed = (volume, face, link, order, last, diag, send)
+    work = [stage, halo, wide(BLOCK), vector, wide(BLOCK), blocks(BLOCK), blocks(2 * BLOCK)]
+    fixed = (volume, normal, pair, link, order, last, diag, send)
     image, mimage, out2 = run(
         functools.partial(first_kernel, shifts=shifts), [vec, vec, full_block], work, (in1, predir, source) + fixed
     )
@@ -731,11 +818,10 @@
         functools.partial(fourth_kernel, shifts=shifts),
         [vec, vec, vec, vec, sum_block],
         work[1:],
-        (in4, scales, ghosts, field, residual, preres, predir, image, mimage) + fixed[:5],
+        (in4, scales, ghosts, field, residual, preres, predir, image, mimage) + fixed[:6],
     )
     in5 = lax.all_to_all(out5, "cells", 0, 0)
-    out = (flow_state.shape, F32)
-    field, residual = run(last_kernel, [out, out], [(2,) + vector], (in5, field, premid, middle, second))
+    field, residual = run(last_kernel, [flat_vec, flat_vec], [(2,) + vector], (in5, field, premid, middle, second))
     return (field, residual)
 
 

time: 87.2 us -> 80.4 us (0.922)
  local copies, waits for them, and re-layouts: 4.78 us -> 0.01 us
  waiting for transfers between devices: 7.89 us -> 4.32 us
  Pallas kernels: 14.9 us -> 15.9 us
    unnamed x16 -> x2, local copies, waits for them, and re-layouts: 4.78 us -> 0.01 us
    all_to_all x1, waiting for transfers between devices: 6.7 us -> 3.13 us  [exchange(): return lax.all_to_all(block, ('cells', 'faces'), 0, 0)]
    pallas_call x7 -> x9, Pallas kernels: 14.9 us -> 15.9 us  [run(): pl.pallas_call(kernel, out_shape=[jax.ShapeDtypeStruct(shape, dtype) for...]
  transfers between devices with their start and end apart: 2 -> 2, of which waited for: 2 -> 2; matrix products, arithmetic and copies ran while one was open for 0% -> 0% of each run, Pallas kernels for 0% -> 4%
where the time goes in v3:
time: 80.4 us; the launch traced here: 80.1 us
  blocking collectives  51 us (63%)
  Pallas kernels  15.9 us (20%)
  starting transfers between devices  7.65 us (10%)
  waiting for transfers between devices  4.32 us (5%)
  between operations  1.33 us (2%)
    all_to_all x4, blocking collectives, exchange(): return lax.all_to_all(block, ('cells', 'faces'), 0, 0)  40.7 us
    pallas_call x9, Pallas kernels, run(): pl.pallas_call(kernel, out_shape=[jax.ShapeDtypeStruct(shape, dtype) for...  15.9 us
    all_to_all x1, blocking collectives, body(): in5 = lax.all_to_all(out5, 'cells', 0, 0)  10.3 us
    all_to_all x1, starting transfers between devices, exchange(): return lax.all_to_all(block, ('cells', 'faces'), 0, 0)  7.33 us
    all_to_all x1, waiting for transfers between devices, exchange(): return lax.all_to_all(block, ('cells', 'faces'), 0, 0)  3.13 us
  transfers between devices with their start and end apart: 2, of which 2 were waited for; matrix products, arithmetic and copies ran while one was open for 0% of the time, Pallas kernels for 4%

profile of v3, /device:TPU:0, one launch (start us, length us, event | category | flops | bytes accessed | tf_op | source)
XLA Modules:
  0.0 80.1 jit_solution(8732130700579389632)
XLA Ops:
  0.6 2.0 %shard_map.104 = (f32[32,8,128]{2,1,0:T(8,128)}, s32[2,8,128]{2,1,0:T(8,128)S(1)}, f32[4,8192]{1,0:T(4,128)S(1)}, f32[3,12288]{1,0:T(4,128)S(1)}, s32[96,128]{1,...) custom-call(s32[6]{0:T(128)} %used_any.1, f32[4,8192]{1,0:T(4,128)} %flow_any.1, s32[6,256]{1,0:T(8,128)} %list_any.1, ...), custom_call_target="tpu_custom_call" | custom-call | tf_op jit(solution)/shard_map/pallas_call | solution.py:704
  2.6 7.3 %all-to-all-start = ((f32[32,8,128]{2,1,0:T(8,128)}), f32[32,8,128]{2,1,0:T(8,128)S(1)}, u32[]{:S(2)}, u32[]{:S(2)}) async-start(f32[32,8,128]{2,1,0:T(8,128)} %get-tuple-element.43), calls=%async_computation | async-start | bytes 262144 | tf_op jit(solution)/shard_map/all_to_all | solution.py:715
  10.6 0.2 shard_map.105.mine_ref
  10.8 0.3 collective-permute-start
  11.1 1.2 %collective-permute-done.peer_ref = f32[4,96,128]{2,1,0:T(8,128)S(1)} collective-permute-done((f32[4,96,128]{2,1,0:T(8,128)S(1)}, f32[4,96,128]{2,1,0:T(8,128)S(1)}, u32[]{:S(2)}, u32[]{:S(2)}) %collective-permute-start) | collective-permute-done | bytes 196640 | tf_op jit(solution)/shard_map/ppermute | solution.py:777
  12.3 0.0 copy-start
  12.3 2.7 %shard_map.106 = (f32[3,3,64,128]{3,2,1,0:T(8,128)S(1)}, s32[2,3,64,128]{3,2,1,0:T(8,128)S(1)}, s32[2,3,64,128]{3,2,1,0:T(8,128)S(1)}, s32[3,3,64,128]{3,2,1,0:T...) custom-call(f32[4,96,128]{2,1,0:T(8,128)S(1)} %shard_map.105.mine_ref, ...), custom_call_target="tpu_custom_call" | custom-call | tf_op jit(solution)/shard_map/pallas_call | solution.py:704
  15.1 3.1 %all-to-all-done.in_ref = f32[32,8,128]{2,1,0:T(8,128)S(1)} async-done(((f32[32,8,128]{2,1,0:T(8,128)}), f32[32,8,128]{2,1,0:T(8,128)S(1)}, u32[]{:S(2)}, u32[]{:S(2)}) %all-to-all-start) | async-done | bytes 131104 | tf_op jit(solution)/shard_map/all_to_all | solution.py:715
  18.2 0.0 copy-done
  18.2 1.4 %shard_map.107 = (f32[2,3,64,128]{3,2,1,0:T(8,128)S(1)}, f32[5,64,128]{2,1,0:T(8,128)S(1)}, f32[4,64,128]{2,1,0:T(8,128)S(1)}, f32[4,64,128]{2,1,0:T(8,128)S(1)}, f32[32,8,128]{2,1,0:T(8,128)S(1)}) custom-call(f32[32,8,128]{2,1,0:T(8,128)S(1)} %all-to-all-done.in_ref, f32[4,8192]{1,0:T(4,128)S(1)} %get-tuple-element.44.source_ref, f32[64,128]{1,0:T(8,128)S(1)} %bitcast.3, ...), custom_call_target="tpu_custom_call" | custom-call | tf_op jit(solution)/shard_map/pallas_call | solution.py:704
  19.6 10.7 %all_to_all.30.in_ref.in1_ref = f32[32,8,128]{2,1,0:T(8,128)S(1)} all-to-all(f32[32,8,128]{2,1,0:T(8,128)S(1)} %get-tuple-element.56), channel_id=1, replica_groups=mesh['cells'=16,'faces'=2] {'cells','faces'}, dimensions={0} | all-to-all | bytes 262144 | tf_op jit(solution)/shard_map/all_to_all | solution.py:715
  30.3 2.1 %shard_map.108 = (f32[4,64,128]{2,1,0:T(8,128)S(1)}, f32[4,64,128]{2,1,0:T(8,128)S(1)}, f32[32,8,128]{2,1,0:T(8,128)S(1)}) custom-call(f32[32,8,128]{2,1,0:T(8,128)S(1)} %all_to_all.30.in_ref.in1_ref, f32[4,64,128]{2,1,0:T(8,128)S(1)} %get-tuple-element.57.pre_ref, f32[4,64,128]{2,1,0:T(8,128)S(1)} %get-tuple-element.58.source_ref, f32[64,128]{1,0:T(8,128)S(1)} %bitcast.4, ...), custom_call_target="tpu_custom_call" | custom-call | tf_op jit(solution)/shard_map/pallas_call | solution.py:704
  32.4 10.0 %all_to_all.31.in2_ref = f32[32,8,128]{2,1,0:T(8,128)S(1)} all-to-all(f32[32,8,128]{2,1,0:T(8,128)S(1)} %get-tuple-element.61), channel_id=1, replica_groups=mesh['cells'=16,'faces'=2] {'cells','faces'}, dimensions={0} | all-to-all | bytes 262144 | tf_op jit(solution)/shard_map/all_to_all | solution.py:715
  42.4 2.2 %shard_map.109 = (f32[4,64,128]{2,1,0:T(8,128)S(1)}, f32[4,64,128]{2,1,0:T(8,128)S(1)}, f32[4,64,128]{2,1,0:T(8,128)S(1)}, f32[4,64,128]{2,1,0:T(8,128)S(1)}, f3...) custom-call(f32[32,8,128]{2,1,0:T(8,128)S(1)} %all_to_all.30.in_ref.in1_ref, f32[32,8,128]{2,1,0:T(8,128)S(1)} %all_to_all.31.in2_ref, ...), custom_call_target="tpu_custom_call" | custom-call | tf_op jit(solution)/shard_map/pallas_call | solution.py:704
  44.6 10.0 %all_to_all.32.in3_ref = f32[32,8,128]{2,1,0:T(8,128)S(1)} all-to-all(f32[32,8,128]{2,1,0:T(8,128)S(1)} %get-tuple-element.64), channel_id=1, replica_groups=mesh['cells'=16,'faces'=2] {'cells','faces'}, dimensions={0} | all-to-all | bytes 262144 | tf_op jit(solution)/shard_map/all_to_all | solution.py:715
  54.6 2.3 %shard_map.110 = (f32[4,64,128]{2,1,0:T(8,128)S(1)}, f32[4,64,128]{2,1,0:T(8,128)S(1)}, f32[4,64,128]{2,1,0:T(8,128)S(1)}, f32[4,64,128]{2,1,0:T(8,128)S(1)}, f3...) custom-call(f32[32,8,128]{2,1,0:T(8,128)S(1)} %all_to_all.30.in_ref., ...), custom_call_target="tpu_custom_call" | custom-call | tf_op jit(solution)/shard_map/pallas_call | solution.py:704
  56.9 10.0 %all_to_all.33.in4_ref = f32[32,8,128]{2,1,0:T(8,128)S(1)} all-to-all(f32[32,8,128]{2,1,0:T(8,128)S(1)} %get-tuple-element.70), channel_id=1, replica_groups=mesh['cells'=16,'faces'=2] {'cells','faces'}, dimensions={0} | all-to-all | bytes 262144 | tf_op jit(solution)/shard_map/all_to_all | solution.py:715
  66.8 2.0 %shard_map.111 = (f32[4,64,128]{2,1,0:T(8,128)S(1)}, f32[4,64,128]{2,1,0:T(8,128)S(1)}, f32[4,64,128]{2,1,0:T(8,128)S(1)}, f32[4,64,128]{2,1,0:T(8,128)S(1)}, f32[16,8,128]{2,1,0:T(8,128)S(1)}) custom-call(f32[32,8,128]{2,1,0:T(8,128)S(1)} %all_to_all.33.in4_ref, f32[8,128]{1,0:T(8,128)S(1)} %get-tuple-element.71.scale_ref, ...), custom_call_target="tpu_custom_call" | custom-call | tf_op jit(solution)/shard_map/pallas_call | solution.py:704
  68.8 10.3 %all_to_all.34.in_ref = f32[16,8,128]{2,1,0:T(8,128)S(1)} all-to-all(f32[16,8,128]{2,1,0:T(8,128)S(1)} %get-tuple-element.79), channel_id=1, replica_groups=mesh['cells'=16,'faces'=2] {'cells'}, dimensions={0} | all-to-all | bytes 131072 | tf_op jit(solution)/shard_map/all_to_all | solution.py:823
  79.1 1.0 %shard_map.112 = (f32[4,8192]{1,0:T(4,128)}, f32[4,8192]{1,0:T(4,128)}) custom-call(f32[16,8,128]{2,1,0:T(8,128)S(1)} %all_to_all.34.in_ref, f32[4,64,128]{2,1,0:T(8,128)S(1)} %get-tuple-element.80.field_ref, f32[4,64,128]{2,1,0:T(8,128)S(1)} %get-tuple-element.81.premid_ref, f32[4,64,128]{2,1,0:T(8,128)S(1)} %get-tuple-element.82.middle_ref, ...), custom_call_target="tpu_custom_call" | custom-call | tf_op jit(solution)/shard_map/pallas_call | solution.py:704
Async XLA Ops:
  2.6 15.5 %all-to-all-start = ((f32[32,8,128]{2,1,0:T(8,128)}), f32[32,8,128]{2,1,0:T(8,128)S(1)}, u32[]{:S(2)}, u32[]{:S(2)}) async-start(f32[32,8,128]{2,1,0:T(8,128)} %get-tuple-element.43), calls=%async_computation | async-start | bytes 262144 | tf_op jit(solution)/shard_map/all_to_all | solution.py:715
  10.8 1.5 %collective-permute-start = (f32[4,96,128]{2,1,0:T(8,128)S(1)}, f32[4,96,128]{2,1,0:T(8,128)S(1)}, u32[]{:S(2)}, u32[]{:S(2)}) collective-permute-start(f32[4,96,128]{2,1,0:T(8,128)S(1)} %shard_map.105.mine_ref), channel_id=1, source_target_pairs={{0,1},{1,0},{2,3},{3,2},{4,5},{5,4},{6,7},{7,6},{8,9},{9,8},{10,11... | collective-permute-start | bytes 589832 | tf_op jit(solution)/shard_map/ppermute | solution.py:777
  12.3 5.9 %copy-start = (f32[8192]{0:T(1024)S(1)}, f32[8192]{0:T(1024)}, u32[]{:S(2)}) copy-start(f32[8192]{0:T(1024)} %param.11) | copy-start | bytes 98308

commit v4 on v3

--- a/solution.py
+++ b/solution.py
@@ -310,9 +310,9 @@
 
 
 def start_kernel(
-    used_any, flow_any, list_any, normal_any, owner_any, neighbour_any, source_any,
-    out_ref, send_ref, flow_ref, normal_ref, owner_ref, neighbour_ref, source_ref,
-    stage_ref, list_ref, used_ref, sems,
+    count_ref, used_any, flow_any, list_any, normal_any, owner_any, neighbour_any, source_any,
+    pack_ref, out_ref, send_ref, flow_ref, source_ref,
+    stage_ref, list_ref, used_ref, normal_ref, owner_ref, neighbour_ref, sems,
 ):
     pairs = (
         (used_any, used_ref), (flow_any, flow_ref), (list_any, list_ref), (normal_any, normal_ref),
@@ -343,9 +343,10 @@
     send_halo(listed(flat_rows(flow_ref), tiles, send_ref), stage_ref, out_ref, each)
     for copy in copies[3:]:
         copy.wait()
-
-
-def pack_kernel(count_ref, normal_ref, owner_ref, neighbour_ref, pack_ref, *, lists, width, cells_here):
+    pack_faces(count_ref, normal_ref, owner_ref, neighbour_ref, pack_ref, lists, width, tiles * LANES)
+
+
+def pack_faces(count_ref, normal_ref, owner_ref, neighbour_ref, pack_ref, lists, width, cells_here):
     tiles = cells_here // LANES
     pairs = tiles // 2
     shape = (pairs, LANES)
@@ -549,21 +550,30 @@
     return out
 
 
-def first_kernel(
-    in_ref, pre_ref, source_ref, volume_ref, normal_ref, pair_ref, link_ref, order_ref, last_ref, diag_ref, send_ref,
-    image_ref, mimage_ref, out_ref,
-    stage_ref, halo_ref, wide_ref, here_ref, beside_ref, flux_ref, sort_ref, *, shifts,
-):
-    tiles = volume_ref.shape[0]
-    groups = in_groups(tiles)
-    for g in groups:
-        put(wide_ref, g, cell(pre_ref, g))
+def apply_faces(in_ref, vector_ref, faces, here_ref, beside_ref, wide_ref, halo_ref, flux_ref, sort_ref, shifts):
+    tiles = here_ref.shape[1]
+    for g in in_groups(tiles):
+        put(wide_ref, g, cell(vector_ref, g))
     widen(wide_ref, tiles)
     lay_halo(got_halo(in_ref, shifts), halo_ref)
-    faces = (normal_ref, pair_ref, link_ref, order_ref, last_ref)
     face_part(wide_ref, halo_ref, faces, here_ref, beside_ref, flux_ref, sort_ref, len(shifts))
+
+
+def flatten(out_ref, ref, g):
+    for t in range(g * SUB, g * SUB + SUB):
+        for c in range(BLOCK):
+            out_ref[c : c + 1, t * LANES : (t + 1) * LANES] = ref[c, t : t + 1, :]
+
+
+def first_kernel(
+    in_ref, vector_ref, source_ref, diag_ref, send_ref, volume_ref, *refs, shifts,
+):
+    faces, (image_ref, mimage_ref, out_ref), (stage_ref, *work) = refs[:5], refs[5:8], refs[8:]
+    here_ref, beside_ref, wide_ref = work[:3]
+    tiles = here_ref.shape[1]
+    apply_faces(in_ref, vector_ref, faces, *work, shifts)
     product, rho = zero(), zero()
-    for g in groups:
+    for g in in_groups(tiles):
         image = applied(g, volume_ref, wide_ref, here_ref, beside_ref)
         source = cell(source_ref, g)
         product = added(product, source, image)
@@ -575,33 +585,27 @@
 
 
 def second_kernel(
-    in1_ref, in2_ref, pre_ref, mimage_ref, image_ref, source_ref,
-    volume_ref, normal_ref, pair_ref, link_ref, order_ref, last_ref, diag_ref, send_ref,
-    middle_ref, premid_ref, second_ref, msecond_ref, scale_ref, out_ref,
-    stage_ref, halo_ref, wide_ref, here_ref, beside_ref, flux_ref, sort_ref, *, shifts,
+    in_ref, vector_ref, source_ref, image_ref, diag_ref, send_ref, volume_ref, *refs, shifts,
 ):
-    tiles = volume_ref.shape[0]
-    groups = in_groups(tiles)
-    sums = got_sums(in2_ref, len(shifts) // 2)
+    faces, outs, (stage_ref, *work) = refs[:5], refs[5:11], refs[11:]
+    aimage_ref, second_ref, msecond_ref, middle_ref, scale_ref, out_ref = outs
+    here_ref, beside_ref, wide_ref = work[:3]
+    tiles = here_ref.shape[1]
+    sums = got_sums(in_ref, len(shifts) // 2)
     rho = spread(sums, 1)
     alpha = rho / spread(sums, 0)
     scale_ref[0:1, :] = alpha[0:1, :]
     scale_ref[1:2, :] = rho[0:1, :]
-    for g in groups:
-        premid = combine((None, -alpha), (cell(pre_ref, g), cell(mimage_ref, g)))
-        put(wide_ref, g, premid)
-        put(premid_ref, g, premid)
-    widen(wide_ref, tiles)
-    lay_halo(combine((None, -alpha), (got_halo(in1_ref, shifts), got_halo(in2_ref, shifts))), halo_ref)
-    faces = (normal_ref, pair_ref, link_ref, order_ref, last_ref)
-    face_part(wide_ref, halo_ref, faces, here_ref, beside_ref, flux_ref, sort_ref, len(shifts))
+    apply_faces(in_ref, vector_ref, faces, *work, shifts)
     products = [zero() for _ in range(4)]
-    for g in groups:
-        second = applied(g, volume_ref, wide_ref, here_ref, beside_ref)
-        source = cell(source_ref, g)
-        middle = combine((None, -alpha), (source, cell(image_ref, g)))
+    for g in in_groups(tiles):
+        image, source = cell(image_ref, g), cell(source_ref, g)
+        aimage = applied(g, volume_ref, wide_ref, here_ref, beside_ref)
+        second = combine((None, -alpha), (image, aimage))
+        middle = combine((None, -alpha), (source, image))
+        put(aimage_ref, g, aimage)
+        put(second_ref, g, second)
         put(middle_ref, g, middle)
-        put(second_ref, g, second)
         put(msecond_ref, g, precondition(second, diag_ref, g))
         for i, (a, b) in enumerate(((second, middle), (second, second), (source, middle), (source, second))):
             products[i] = added(products[i], a, b)
@@ -610,89 +614,72 @@
 
 
 def third_kernel(
-    in1_ref, in2_ref, in3_ref, scale_ref, pre_ref, mimage_ref, premid_ref, msecond_ref, middle_ref, second_ref, source_ref,
-    volume_ref, normal_ref, pair_ref, link_ref, order_ref, last_ref, diag_ref, send_ref,
-    field_ref, residual_ref, preres_ref, predir_ref, image_ref, mimage_out, scale_out, ghost_ref, out_ref,
-    stage_ref, halo_ref, wide_ref, here_ref, beside_ref, flux_ref, sort_ref, *, shifts,
+    in_ref, vector_ref, source_ref, image_ref, aimage_ref, second_ref, old_ref, diag_ref, send_ref, volume_ref, *refs, shifts,
 ):
-    tiles = volume_ref.shape[0]
-    groups = in_groups(tiles)
-    sums = got_sums(in3_ref, len(shifts) // 2)
-    alpha, rho = row_of(scale_ref, 0), row_of(scale_ref, 1)
+    faces, outs, (stage_ref, *work) = refs[:5], refs[5:10], refs[10:]
+    apreres_ref, next_ref, mnext_ref, scale_ref, out_ref = outs
+    here_ref, beside_ref, wide_ref = work[:3]
+    tiles = here_ref.shape[1]
+    sums = got_sums(in_ref, len(shifts) // 2)
+    alpha, rho = row_of(old_ref, 0), row_of(old_ref, 1)
     omega = spread(sums, 0) / spread(sums, 1)
     rho_next = spread(sums, 2) - omega * spread(sums, 3)
     beta = rho_next / rho * (alpha / omega)
-    scale_out[0:1, :] = rho_next[0:1, :]
+    for i, value in enumerate((alpha, rho_next, omega, beta)):
+        scale_ref[i : i + 1, :] = value[0:1, :]
+    apply_faces(in_ref, vector_ref, faces, *work, shifts)
     drop = -beta * omega
-    for g in groups:
-        predir, mimage, premid = cell(pre_ref, g), cell(mimage_ref, g), cell(premid_ref, g)
-        put(field_ref, g, combine((alpha, omega), (predir, premid)))
-        put(residual_ref, g, combine((None, -omega), (cell(middle_ref, g), cell(second_ref, g))))
+    product = zero()
+    for g in in_groups(tiles):
+        asecond = applied(g, volume_ref, wide_ref, here_ref, beside_ref)
+        apreres = combine((None, -omega), (cell(second_ref, g), asecond))
+        image = combine((None, beta, drop), (apreres, cell(image_ref, g), cell(aimage_ref, g)))
+        product = added(product, cell(source_ref, g), image)
+        put(apreres_ref, g, apreres)
+        put(next_ref, g, image)
+        put(mnext_ref, g, precondition(image, diag_ref, g))
+    send_sums((product,), out_ref)
+    send_halo(listed(tiled_rows(mnext_ref), tiles, send_ref), stage_ref, out_ref, len(shifts) // 2)
+
+
+def fourth_kernel(
+    in_ref, vector_ref, apreres_ref, image_ref, middle_ref, second_ref, pre_ref, mimage_ref, msecond_ref, old_ref,
+    volume_ref, *refs, shifts,
+):
+    faces, outs, (stage_ref, *work) = refs[:5], refs[5:10], refs[10:]
+    field_out, premid_out, middle_out, second_out, out_ref = outs
+    here_ref, beside_ref, wide_ref = work[:3]
+    tiles = here_ref.shape[1]
+    alpha2 = row_of(old_ref, 1) / spread(got_sums(in_ref, len(shifts) // 2), 0)
+    alpha, omega, beta = [row_of(old_ref, i) for i in (0, 2, 3)]
+    apply_faces(in_ref, vector_ref, faces, *work, shifts)
+    cross, square = zero(), zero()
+    for g in in_groups(tiles):
+        pre, mimage = cell(pre_ref, g), cell(mimage_ref, g)
+        premid = combine((None, -alpha), (pre, mimage))
         preres = combine((None, -omega), (premid, cell(msecond_ref, g)))
-        put(preres_ref, g, preres)
-        predir = combine((None, beta, drop), (preres, predir, mimage))
-        put(predir_ref, g, predir)
-        put(wide_ref, g, predir)
-    widen(wide_ref, tiles)
-    ghost1, ghost2, ghost3 = [got_halo(ref, shifts) for ref in (in1_ref, in2_ref, in3_ref)]
-    preres = combine((None, -alpha, -omega), (ghost1, ghost2, ghost3))
-    for k in range(len(shifts)):
-        ghost_ref[k] = preres[k]
-    lay_halo(combine((None, beta, drop), (preres, ghost1, ghost2)), halo_ref)
-    faces = (normal_ref, pair_ref, link_ref, order_ref, last_ref)
-    face_part(wide_ref, halo_ref, faces, here_ref, beside_ref, flux_ref, sort_ref, len(shifts))
-    product = zero()
-    for g in groups:
-        image = applied(g, volume_ref, wide_ref, here_ref, beside_ref)
-        product = added(product, cell(source_ref, g), image)
-        put(image_ref, g, image)
-        put(mimage_out, g, precondition(image, diag_ref, g))
-    send_sums((product,), out_ref)
-    send_halo(listed(tiled_rows(mimage_out), tiles, send_ref), stage_ref, out_ref, len(shifts) // 2)
-
-
-def fourth_kernel(
-    in4_ref, scale_ref, ghost_ref, field_ref, residual_ref, preres_ref, predir_ref, image_ref, mimage_ref,
-    volume_ref, normal_ref, pair_ref, link_ref, order_ref, last_ref,
-    field_out, premid_ref, middle_ref, second_ref, out_ref,
-    halo_ref, wide_ref, here_ref, beside_ref, flux_ref, sort_ref, *, shifts,
-):
-    tiles = volume_ref.shape[0]
-    groups = in_groups(tiles)
-    alpha = row_of(scale_ref, 0) / spread(got_sums(in4_ref, len(shifts) // 2), 0)
-    for g in groups:
-        premid = combine((None, -alpha), (cell(preres_ref, g), cell(mimage_ref, g)))
-        put(wide_ref, g, premid)
-        put(premid_ref, g, premid)
-        put(field_out, g, combine((None, alpha), (cell(field_ref, g), cell(predir_ref, g))))
-        put(middle_ref, g, combine((None, -alpha), (cell(residual_ref, g), cell(image_ref, g))))
-    widen(wide_ref, tiles)
-    ghosts = [ghost_ref[k] for k in range(len(shifts))]
-    lay_halo(combine((None, -alpha), (ghosts, got_halo(in4_ref, shifts))), halo_ref)
-    faces = (normal_ref, pair_ref, link_ref, order_ref, last_ref)
-    face_part(wide_ref, halo_ref, faces, here_ref, beside_ref, flux_ref, sort_ref, len(shifts))
-    cross, square = zero(), zero()
-    for g in groups:
-        second = applied(g, volume_ref, wide_ref, here_ref, beside_ref)
-        put(second_ref, g, second)
-        cross = added(cross, second, cell(middle_ref, g))
+        predir = combine((None, beta, -beta * omega), (preres, pre, mimage))
+        put(stage_ref.at[0], g, combine((alpha, omega, alpha2), (pre, premid, predir)))
+        put(stage_ref.at[1], g, combine((None, -alpha2), (preres, cell(vector_ref, g))))
+        flatten(field_out, stage_ref.at[0], g)
+        flatten(premid_out, stage_ref.at[1], g)
+        aimage = applied(g, volume_ref, wide_ref, here_ref, beside_ref)
+        second = combine((None, -alpha2), (cell(apreres_ref, g), aimage))
+        middle = combine((None, -omega, -alpha2), (cell(middle_ref, g), cell(second_ref, g), cell(image_ref, g)))
+        put(stage_ref.at[2], g, second)
+        put(stage_ref.at[3], g, middle)
+        flatten(second_out, stage_ref.at[2], g)
+        flatten(middle_out, stage_ref.at[3], g)
+        cross = added(cross, second, middle)
         square = added(square, second, second)
     send_sums((cross, square), out_ref)
 
 
-def last_kernel(in_ref, field_ref, premid_ref, middle_ref, second_ref, field_out, residual_out, stage_ref):
-    tiles = field_ref.shape[1]
-    sums = total_of([in_ref[d] for d in range(in_ref.shape[0])])
-    omega = spread(sums, 0) / spread(sums, 1)
-    for g in in_groups(tiles):
-        field = combine((None, omega), (cell(field_ref, g), cell(premid_ref, g)))
-        residual = combine((None, -omega), (cell(middle_ref, g), cell(second_ref, g)))
-        put(stage_ref.at[0], g, field)
-        put(stage_ref.at[1], g, residual)
-        for i, out in enumerate((field_out, residual_out)):
-            for t in range(g * SUB, g * SUB + SUB):
-                for c in range(BLOCK):
-                    out[c : c + 1, t * LANES : (t + 1) * LANES] = stage_ref[i, c, t : t + 1, :]
+def last_kernel(in_ref, field_ref, premid_ref, middle_ref, second_ref, field_out, residual_out):
+    sums = total_of([in_ref[d] for d in range(0, in_ref.shape[0], lax.axis_size("faces"))])
+    omega = sums[0:1, :] / sums[1:2, :]
+    field_out[...] = field_ref[...] + omega * premid_ref[...]
+    residual_out[...] = middle_ref[...] - omega * second_ref[...]
 
 
 def run(kernel, outs, scratch, args, scalars=0, away=0):
@@ -741,7 +728,6 @@
     vec = (vector, F32)
     faces = (rows, tiles, LANES)
     scale = ((SUB, LANES), F32)
-    sum_block = ((count, SUB, LANES), F32)
     full_block = ((2 * count, SUB, LANES), F32)
     flat_vec = (flow_state.shape, F32)
     stage = (SUB * SUB, LANES)
@@ -755,25 +741,22 @@
     def blocks(parts):
         return (rows * parts * tiles, LANES)
 
-    ints = ((flat, LANES), I32)
-    out0, send, flow, slopes, owner, neighbour, source = run(
+    ints = pltpu.VMEM((flat, LANES), I32)
+    pack, out0, send, flow, source = run(
         start_kernel,
-        [full_block, ((2, SUB, LANES), I32), flat_vec, (face_normal.shape, F32), ints, ints, flat_vec],
-        [stage, pltpu.VMEM(send_list.shape, I32), pltpu.SMEM((lists,), I32), pltpu.SemaphoreType.DMA((7,))],
+        [((4, flat, LANES), F32), full_block, ((2, SUB, LANES), I32), flat_vec, flat_vec],
+        [
+            stage, pltpu.VMEM(send_list.shape, I32), pltpu.SMEM((lists,), I32),
+            face_normal.shape, ints, ints, pltpu.SemaphoreType.DMA((7,)),
+        ],
         (
-            halo_count, flow_state, send_list, face_normal,
+            face_count, halo_count, flow_state, send_list, face_normal,
             face_owner.reshape(flat, LANES), face_neighbour.reshape(flat, LANES), source_term,
         ),
+        scalars=1,
         away=7,
     )
     in0 = exchange(out0)
-    (pack,) = run(
-        functools.partial(pack_kernel, lists=lists, width=width, cells_here=cells_here),
-        [((4, flat, LANES), F32)],
-        [],
-        (face_count, slopes, owner, neighbour),
-        scalars=1,
-    )
     peer = lax.ppermute(pack, "faces", [(0, 1), (1, 0)])
     normal, link, order, last, lean, coupling = run(
         table_kernel,
@@ -793,35 +776,33 @@
         [stage, halo, (2, tiles, LANES), wide(2), blocks(2), blocks(4)],
         (in0, source, volume, normal, link, order, last, lean, coupling, send),
     )
+    tables = (volume, normal, pair, link, order, last)
+    scratch = [vector, wide(BLOCK), wide(BLOCK), halo, blocks(BLOCK), blocks(2 * BLOCK)]
+
+    def step(kernel, outs, args, stage=stage):
+        return run(functools.partial(kernel, shifts=shifts), outs, [stage] + scratch, args + tables)
+
     in1 = exchange(out1)
-    work = [stage, halo, wide(BLOCK), vector, wide(BLOCK), blocks(BLOCK), blocks(2 * BLOCK)]
-    fixed = (volume, normal, pair, link, order, last, diag, send)
-    image, mimage, out2 = run(
-        functools.partial(first_kernel, shifts=shifts), [vec, vec, full_block], work, (in1, predir, source) + fixed
-    )
+    image, mimage, out2 = step(first_kernel, [vec, vec, full_block], (in1, predir, source, diag, send))
     in2 = exchange(out2)
-    middle, premid, second, msecond, scales, out3 = run(
-        functools.partial(second_kernel, shifts=shifts),
-        [vec, vec, vec, vec, scale, full_block],
-        work,
-        (in1, in2, predir, mimage, image, source) + fixed,
+    aimage, second, msecond, middle, scales, out3 = step(
+        second_kernel, [vec, vec, vec, vec, scale, full_block], (in2, mimage, source, image, diag, send)
     )
     in3 = exchange(out3)
-    field, residual, preres, predir, image, mimage, scales, ghosts, out4 = run(
-        functools.partial(third_kernel, shifts=shifts),
-        [vec, vec, vec, vec, vec, vec, scale, ((lists, SUB, LANES), F32), full_block],
-        work,
-        (in1, in2, in3, scales, predir, mimage, premid, msecond, middle, second, source) + fixed,
+    apreres, image, mnext, scales, out4 = step(
+        third_kernel,
+        [vec, vec, vec, scale, full_block],
+        (in3, msecond, source, image, aimage, second, scales, diag, send),
     )
     in4 = exchange(out4)
-    field, premid, middle, second, out5 = run(
-        functools.partial(fourth_kernel, shifts=shifts),
-        [vec, vec, vec, vec, sum_block],
-        work[1:],
-        (in4, scales, ghosts, field, residual, preres, predir, image, mimage) + fixed[:6],
+    field, premid, middle, second, out5 = step(
+        fourth_kernel,
+        [flat_vec] * 4 + [full_block],
+        (in4, mnext, apreres, image, middle, second, predir, mimage, msecond, scales),
+        (4,) + vector,
     )
-    in5 = lax.all_to_all(out5, "cells", 0, 0)
-    field, residual = run(last_kernel, [flat_vec, flat_vec], [(2,) + vector], (in5, field, premid, middle, second))
+    in5 = exchange(out5)
+    field, residual = run(last_kernel, [flat_vec, flat_vec], [], (in5, field, premid, middle, second))
     return (field, residual)
 
 

time: 80.4 us -> 80 us (level)
  blocking collectives: 51 us -> 49.8 us
  waiting for transfers between devices: 4.32 us -> 5.15 us
    all_to_all x1 -> x0, blocking collectives: 10.3 us -> none  [body(): in5 = lax.all_to_all(out5, 'cells', 0, 0)]
    all_to_all x4 -> x5, blocking collectives: 40.7 us -> 49.8 us  [exchange(): return lax.all_to_all(block, ('cells', 'faces'), 0, 0)]
    all_to_all x1, waiting for transfers between devices: 3.13 us -> 3.96 us  [exchange(): return lax.all_to_all(block, ('cells', 'faces'), 0, 0)]
    pallas_call x9 -> x8, Pallas kernels: 15.9 us -> 15.7 us  [run(): pl.pallas_call(kernel, out_shape=[jax.ShapeDtypeStruct(shape, dtype) for...]
  transfers between devices with their start and end apart: 2 -> 2, of which waited for: 2 -> 2; matrix products, arithmetic and copies ran while one was open for 0% -> 0% of each run, Pallas kernels for 4% -> 3%
where the time goes in v4:
time: 80 us; the launch traced here: 79.7 us
  blocking collectives  49.8 us (62%)
  Pallas kernels  15.7 us (20%)
  starting transfers between devices  7.65 us (10%)
  waiting for transfers between devices  5.15 us (6%)
  between operations  1.32 us (2%)
    all_to_all x5, blocking collectives, exchange(): return lax.all_to_all(block, ('cells', 'faces'), 0, 0)  49.8 us
    pallas_call x8, Pallas kernels, run(): pl.pallas_call(kernel, out_shape=[jax.ShapeDtypeStruct(shape, dtype) for...  15.7 us
    all_to_all x1, starting transfers between devices, exchange(): return lax.all_to_all(block, ('cells', 'faces'), 0, 0)  7.33 us
    all_to_all x1, waiting for transfers between devices, exchange(): return lax.all_to_all(block, ('cells', 'faces'), 0, 0)  3.96 us
  transfers between devices with their start and end apart: 2, of which 2 were waited for; matrix products, arithmetic and copies ran while one was open for 0% of the time, Pallas kernels for 3%

profile of v4, /device:TPU:0, one launch (start us, length us, event | category | flops | bytes accessed | tf_op | source)
XLA Modules:
  0.0 79.7 jit_solution(4039048067556509823)
XLA Ops:
  1.3 2.1 %shard_map.104 = (f32[4,96,128]{2,1,0:T(8,128)S(1)}, f32[32,8,128]{2,1,0:T(8,128)}, s32[2,8,128]{2,1,0:T(8,128)S(1)}, f32[4,8192]{1,0:T(4,128)S(1)}, f32[4,8192]{1,0:T(4,128)S(1)}) custom-call(s32[1]{0:T(128)S(6)} %copy.11.count_ref, s32[6]{0:T(128)} %used_any.1, f32[4,8192]{1,0:T(4,128)} %flow_any.1, s32[6,256]{1,0:T(8,128)} %list_any.1, ...), custom_call_target="tpu_custom_call" | custom-call | tf_op jit(solution)/shard_map/pallas_call | solution.py:691
  3.4 7.3 %all-to-all-start = ((f32[32,8,128]{2,1,0:T(8,128)}), f32[32,8,128]{2,1,0:T(8,128)S(1)}, u32[]{:S(2)}, u32[]{:S(2)}) async-start(f32[32,8,128]{2,1,0:T(8,128)} %get-tuple-element.37), calls=%async_computation | async-start | bytes 262144 | tf_op jit(solution)/shard_map/all_to_all | solution.py:702
  10.7 0.3 collective-permute-start
  11.1 1.2 %collective-permute-done.peer_ref = f32[4,96,128]{2,1,0:T(8,128)S(1)} collective-permute-done((f32[4,96,128]{2,1,0:T(8,128)S(1)}, f32[4,96,128]{2,1,0:T(8,128)S(1)}, u32[]{:S(2)}, u32[]{:S(2)}) %collective-permute-start) | collective-permute-done | bytes 196640 | tf_op jit(solution)/shard_map/ppermute | solution.py:760
  12.2 0.0 copy-start
  12.3 2.7 %shard_map.105 = (f32[3,3,64,128]{3,2,1,0:T(8,128)S(1)}, s32[2,3,64,128]{3,2,1,0:T(8,128)S(1)}, s32[2,3,64,128]{3,2,1,0:T(8,128)S(1)}, s32[3,3,64,128]{3,2,1,0:T...) custom-call(f32[4,96,128]{2,1,0:T(8,128)S(1)} %get-tuple-element.39.mine_ref, ...), custom_call_target="tpu_custom_call" | custom-call | tf_op jit(solution)/shard_map/pallas_call | solution.py:691
  15.0 4.0 %all-to-all-done.in_ref = f32[32,8,128]{2,1,0:T(8,128)S(1)} async-done(((f32[32,8,128]{2,1,0:T(8,128)}), f32[32,8,128]{2,1,0:T(8,128)S(1)}, u32[]{:S(2)}, u32[]{:S(2)}) %all-to-all-start) | async-done | bytes 131104 | tf_op jit(solution)/shard_map/all_to_all | solution.py:702
  18.9 0.0 copy-done
  18.9 1.4 %shard_map.106 = (f32[2,3,64,128]{3,2,1,0:T(8,128)S(1)}, f32[5,64,128]{2,1,0:T(8,128)S(1)}, f32[4,64,128]{2,1,0:T(8,128)S(1)}, f32[4,64,128]{2,1,0:T(8,128)S(1)}, f32[32,8,128]{2,1,0:T(8,128)S(1)}) custom-call(f32[32,8,128]{2,1,0:T(8,128)S(1)} %all-to-all-done.in_ref, f32[4,8192]{1,0:T(4,128)S(1)} %get-tuple-element.38.source_ref, f32[64,128]{1,0:T(8,128)S(1)} %bitcast.3, ...), custom_call_target="tpu_custom_call" | custom-call | tf_op jit(solution)/shard_map/pallas_call | solution.py:691
  20.3 10.0 %all_to_all.30.in_ref = f32[32,8,128]{2,1,0:T(8,128)S(1)} all-to-all(f32[32,8,128]{2,1,0:T(8,128)S(1)} %get-tuple-element.48), channel_id=1, replica_groups=mesh['cells'=16,'faces'=2] {'cells','faces'}, dimensions={0} | all-to-all | bytes 262144 | tf_op jit(solution)/shard_map/all_to_all | solution.py:702
  30.3 2.1 %shard_map.107 = (f32[4,64,128]{2,1,0:T(8,128)S(1)}, f32[4,64,128]{2,1,0:T(8,128)S(1)}, f32[32,8,128]{2,1,0:T(8,128)S(1)}) custom-call(f32[32,8,128]{2,1,0:T(8,128)S(1)} %all_to_all.30.in_ref, f32[4,64,128]{2,1,0:T(8,128)S(1)} %get-tuple-element.49.vector_ref.pre_ref, f32[4,64,128]{2,1,0:T(8,128)S(1)} %get-tuple-element.50.source_ref, ...), custom_call_target="tpu_custom_call" | custom-call | tf_op jit(solution)/shard_map/pallas_call | solution.py:691
  32.4 10.0 %all_to_all.31.in_ref = f32[32,8,128]{2,1,0:T(8,128)S(1)} all-to-all(f32[32,8,128]{2,1,0:T(8,128)S(1)} %get-tuple-element.53), channel_id=1, replica_groups=mesh['cells'=16,'faces'=2] {'cells','faces'}, dimensions={0} | all-to-all | bytes 262144 | tf_op jit(solution)/shard_map/all_to_all | solution.py:702
  42.4 2.2 %shard_map.108 = (f32[4,64,128]{2,1,0:T(8,128)S(1)}, f32[4,64,128]{2,1,0:T(8,128)S(1)}, f32[4,64,128]{2,1,0:T(8,128)S(1)}, f32[4,64,128]{2,1,0:T(8,128)S(1)}, f3...) custom-call(f32[32,8,128]{2,1,0:T(8,128)S(1)} %all_to_all.31.in_ref, ...), custom_call_target="tpu_custom_call" | custom-call | tf_op jit(solution)/shard_map/pallas_call | solution.py:691
  44.6 10.0 %all_to_all.32.in_ref = f32[32,8,128]{2,1,0:T(8,128)S(1)} all-to-all(f32[32,8,128]{2,1,0:T(8,128)S(1)} %get-tuple-element.56), channel_id=1, replica_groups=mesh['cells'=16,'faces'=2] {'cells','faces'}, dimensions={0} | all-to-all | bytes 262144 | tf_op jit(solution)/shard_map/all_to_all | solution.py:702
  54.5 2.2 %shard_map.109 = (f32[4,64,128]{2,1,0:T(8,128)S(1)}, f32[4,64,128]{2,1,0:T(8,128)S(1)}, f32[4,64,128]{2,1,0:T(8,128)S(1)}, f32[8,128]{1,0:T(8,128)S(1)}, f32[32,8,128]{2,1,0:T(8,128)S(1)}) custom-call(f32[32,8,128]{2,1,0:T(8,128)S(1)} %all_to_all.32.in_ref, f32[4,64,128]{2,1,0:T(8,128)S(1)} %get-tuple-element.57.vector_ref.msecond_ref, ...), custom_call_target="tpu_custom_call" | custom-call | tf_op jit(solution)/shard_map/pallas_call | solution.py:691
  56.7 10.0 %all_to_all.33.in_ref = f32[32,8,128]{2,1,0:T(8,128)S(1)} all-to-all(f32[32,8,128]{2,1,0:T(8,128)S(1)} %get-tuple-element.61), channel_id=1, replica_groups=mesh['cells'=16,'faces'=2] {'cells','faces'}, dimensions={0} | all-to-all | bytes 262144 | tf_op jit(solution)/shard_map/all_to_all | solution.py:702
  66.7 2.2 %shard_map.110 = (f32[4,8192]{1,0:T(4,128)S(1)}, f32[4,8192]{1,0:T(4,128)S(1)}, f32[4,8192]{1,0:T(4,128)S(1)}, f32[4,8192]{1,0:T(4,128)S(1)}, f32[32,8,128]{2,1,0:T(8,128)S(1)}) custom-call(f32[32,8,128]{2,1,0:T(8,128)S(1)} %all_to_all.33.in_ref, f32[4,64,128]{2,1,0:T(8,128)S(1)} %get-tuple-element.62.vector_ref, ...), custom_call_target="tpu_custom_call" | custom-call | tf_op jit(solution)/shard_map/pallas_call | solution.py:691
  68.9 10.0 %all_to_all.34.in_ref = f32[32,8,128]{2,1,0:T(8,128)S(1)} all-to-all(f32[32,8,128]{2,1,0:T(8,128)S(1)} %get-tuple-element.67), channel_id=1, replica_groups=mesh['cells'=16,'faces'=2] {'cells','faces'}, dimensions={0} | all-to-all | bytes 262144 | tf_op jit(solution)/shard_map/all_to_all | solution.py:702
  78.9 0.8 %shard_map.111 = (f32[4,8192]{1,0:T(4,128)}, f32[4,8192]{1,0:T(4,128)}) custom-call(f32[32,8,128]{2,1,0:T(8,128)S(1)} %all_to_all.34.in_ref, f32[4,8192]{1,0:T(4,128)S(1)} %get-tuple-element.68.field_ref, f32[4,8192]{1,0:T(4,128)S(1)} %get-tuple-element.69.premid_ref, f32[4,8192]{1,0:T(4,128)S(1)} %get-tuple-element.70.middle_ref, ...), custom_call_target="tpu_custom_call" | custom-call | tf_op jit(solution)/shard_map/pallas_call | solution.py:691
Async XLA Ops:
  3.4 15.5 %all-to-all-start = ((f32[32,8,128]{2,1,0:T(8,128)}), f32[32,8,128]{2,1,0:T(8,128)S(1)}, u32[]{:S(2)}, u32[]{:S(2)}) async-start(f32[32,8,128]{2,1,0:T(8,128)} %get-tuple-element.37), calls=%async_computation | async-start | bytes 262144 | tf_op jit(solution)/shard_map/all_to_all | solution.py:702
  10.7 1.5 %collective-permute-start = (f32[4,96,128]{2,1,0:T(8,128)S(1)}, f32[4,96,128]{2,1,0:T(8,128)S(1)}, u32[]{:S(2)}, u32[]{:S(2)}) collective-permute-start(f32[4,96,128]{2,1,0:T(8,128)S(1)} %get-tuple-element.39.mine_ref), channel_id=1, source_target_pairs={{0,1},{1,0},{2,3},{3,2},{4,5},{5,4},{6,7},{7,6},{8,9},{9,8},{10,11... | collective-permute-start | bytes 589832 | tf_op jit(solution)/shard_map/ppermute | solution.py:760
  12.2 6.7 %copy-start = (f32[8192]{0:T(1024)S(1)}, f32[8192]{0:T(1024)}, u32[]{:S(2)}) copy-start(f32[8192]{0:T(1024)} %param.11) | copy-start | bytes 98308

commit v5 on v3

--- a/solution.py
+++ b/solution.py
@@ -65,14 +65,22 @@
     return slice(g * SUB, g * SUB + SUB)
 
 
-def listed(row_of_tile, tiles, send_ref):
-    row_at, lane_at = send_ref[0], send_ref[1]
-    found = [jnp.zeros((SUB, LANES), F32) for _ in range(BLOCK)]
-    for t in range(tiles):
-        here = row_at == t
-        for c in range(BLOCK):
-            row = jnp.broadcast_to(row_of_tile(c, t), (SUB, LANES))
-            found[c] = jnp.where(here, pick(row, lane_at), found[c])
+def listed(row_of_tile, tiles, send_ref, per):
+    packed = send_ref.shape[0] // 2
+    sub = sub_ids()
+    found = []
+    for v in range(packed):
+        row_at, lane_at = send_ref[v], send_ref[packed + v]
+        low, high = [min(n // per, BLOCK - 1) for n in (v * SUB, v * SUB + SUB - 1)]
+        assert high - low <= 1
+        values = jnp.zeros((SUB, LANES), F32)
+        for t in range(tiles):
+            row = jnp.broadcast_to(row_of_tile(low, t), (SUB, LANES))
+            if high > low:
+                other = jnp.broadcast_to(row_of_tile(high, t), (SUB, LANES))
+                row = jnp.where(sub < high * per - v * SUB, row, other)
+            values = jnp.where(row_at == t, pick(row, lane_at), values)
+        found.append(values)
     return found
 
 
@@ -88,13 +96,13 @@
     cores = lax.axis_size("faces")
     count = out_ref.shape[0] // cores
     halves = SUB // BLOCK
-    for c in range(BLOCK):
-        stage_ref[c * SUB : (c + 1) * SUB, :] = found[c]
+    for v, values in enumerate(found):
+        stage_ref[v * SUB : (v + 1) * SUB, :] = values
     sign = 1 - 2 * lax.axis_index("faces")
     for j in range(each):
         place = partition(sign * (j + 1), count)
         for h in range(halves):
-            rows = stage_ref[pl.ds(j * halves + h, BLOCK, stride=SUB), :]
+            rows = stage_ref[pl.ds(j * halves + h, BLOCK, stride=each * halves), :]
             for core in range(cores):
                 out_ref[place * cores + core, h * BLOCK : (h + 1) * BLOCK, :] = rows
 
@@ -310,9 +318,9 @@
 
 
 def start_kernel(
-    used_any, flow_any, list_any, normal_any, owner_any, neighbour_any, source_any,
-    out_ref, send_ref, flow_ref, normal_ref, owner_ref, neighbour_ref, source_ref,
-    stage_ref, list_ref, used_ref, sems,
+    count_ref, used_any, flow_any, list_any, normal_any, owner_any, neighbour_any, source_any,
+    pack_ref, out_ref, send_ref, flow_ref, source_ref,
+    stage_ref, list_ref, used_ref, normal_ref, owner_ref, neighbour_ref, sems,
 ):
     pairs = (
         (used_any, used_ref), (flow_any, flow_ref), (list_any, list_ref), (normal_any, normal_ref),
@@ -326,26 +334,33 @@
     halves = width // LANES
     sub = sub_ids()
     core = lax.axis_index("faces")
-    used = jnp.zeros((SUB, LANES), I32)
+    per = each * halves
+    packed = send_ref.shape[0] // 2
     for copy in copies[:3]:
         copy.wait()
-    for j in range(each):
-        for h in range(halves):
-            i = j * halves + h
-            rows = [list_ref[k : k + 1, h * LANES : (h + 1) * LANES] for k in (j, each + j)]
-            stage_ref[i : i + 1, :] = jnp.where(core == 0, *rows).astype(F32)
-            used = jnp.where(sub == i, used_ref[core * each + j] - h * LANES, used)
-    cells = stage_ref[0:SUB, :].astype(I32)
-    alive = (lane_ids() < used) & (sub < each * halves)
-    send_ref[0] = jnp.where(alive, cells >> 7, -1)
-    send_ref[1] = jnp.where(alive, cells & (LANES - 1), 0)
+    rows = []
+    for i in range(per):
+        j, h = i // halves, i % halves
+        two = [list_ref[k : k + 1, h * LANES : (h + 1) * LANES] for k in (j, each + j)]
+        rows.append(jnp.where(core == 0, *two))
+    for v in range(packed):
+        cells = jnp.zeros((SUB, LANES), I32)
+        used = jnp.zeros((SUB, LANES), I32)
+        for s in range(min(SUB, BLOCK * per - v * SUB)):
+            i = (v * SUB + s) % per
+            cells = jnp.where(sub == s, jnp.broadcast_to(rows[i], (SUB, LANES)), cells)
+            used = jnp.where(sub == s, used_ref[core * each + i // halves] - i % halves * LANES, used)
+        alive = lane_ids() < used
+        send_ref[v] = jnp.where(alive, cells >> 7, -1)
+        send_ref[packed + v] = jnp.where(alive, cells & (LANES - 1), 0)
     tiles = flow_ref.shape[1] // LANES
-    send_halo(listed(flat_rows(flow_ref), tiles, send_ref), stage_ref, out_ref, each)
+    send_halo(listed(flat_rows(flow_ref), tiles, send_ref, per), stage_ref, out_ref, each)
     for copy in copies[3:]:
         copy.wait()
-
-
-def pack_kernel(count_ref, normal_ref, owner_ref, neighbour_ref, pack_ref, *, lists, width, cells_here):
+    pack_faces(count_ref, normal_ref, owner_ref, neighbour_ref, pack_ref, lists, width, tiles * LANES)
+
+
+def pack_faces(count_ref, normal_ref, owner_ref, neighbour_ref, pack_ref, lists, width, cells_here):
     tiles = cells_here // LANES
     pairs = tiles // 2
     shape = (pairs, LANES)
@@ -535,7 +550,7 @@
         for i, value in enumerate((inverse, n0, n1, n2, 1.0 / schur)):
             diag_ref[i, rows8(g), :] = value
         put(pre_ref, g, precondition(cell(source_out, g), diag_ref, g))
-    send_halo(listed(tiled_rows(pre_ref), tiles, send_ref), stage_ref, out_ref, len(shifts) // 2)
+    send_halo(listed(tiled_rows(pre_ref), tiles, send_ref, len(shifts) // 2 * (SUB // BLOCK)), stage_ref, out_ref, len(shifts) // 2)
 
 
 def combine(scales, vectors):
@@ -571,7 +586,7 @@
         put(image_ref, g, image)
         put(mimage_ref, g, precondition(image, diag_ref, g))
     send_sums((product, rho), out_ref)
-    send_halo(listed(tiled_rows(mimage_ref), tiles, send_ref), stage_ref, out_ref, len(shifts) // 2)
+    send_halo(listed(tiled_rows(mimage_ref), tiles, send_ref, len(shifts) // 2 * (SUB // BLOCK)), stage_ref, out_ref, len(shifts) // 2)
 
 
 def second_kernel(
@@ -606,7 +621,7 @@
         for i, (a, b) in enumerate(((second, middle), (second, second), (source, middle), (source, second))):
             products[i] = added(products[i], a, b)
     send_sums(products, out_ref)
-    send_halo(listed(tiled_rows(msecond_ref), tiles, send_ref), stage_ref, out_ref, len(shifts) // 2)
+    send_halo(listed(tiled_rows(msecond_ref), tiles, send_ref, len(shifts) // 2 * (SUB // BLOCK)), stage_ref, out_ref, len(shifts) // 2)
 
 
 def third_kernel(
@@ -648,7 +663,7 @@
         put(image_ref, g, image)
         put(mimage_out, g, precondition(image, diag_ref, g))
     send_sums((product,), out_ref)
-    send_halo(listed(tiled_rows(mimage_out), tiles, send_ref), stage_ref, out_ref, len(shifts) // 2)
+    send_halo(listed(tiled_rows(mimage_out), tiles, send_ref, len(shifts) // 2 * (SUB // BLOCK)), stage_ref, out_ref, len(shifts) // 2)
 
 
 def fourth_kernel(
@@ -682,7 +697,7 @@
 
 def last_kernel(in_ref, field_ref, premid_ref, middle_ref, second_ref, field_out, residual_out, stage_ref):
     tiles = field_ref.shape[1]
-    sums = total_of([in_ref[d] for d in range(in_ref.shape[0])])
+    sums = total_of([in_ref[d] for d in range(0, in_ref.shape[0], lax.axis_size("faces"))])
     omega = spread(sums, 0) / spread(sums, 1)
     for g in in_groups(tiles):
         field = combine((None, omega), (cell(field_ref, g), cell(premid_ref, g)))
@@ -741,7 +756,6 @@
     vec = (vector, F32)
     faces = (rows, tiles, LANES)
     scale = ((SUB, LANES), F32)
-    sum_block = ((count, SUB, LANES), F32)
     full_block = ((2 * count, SUB, LANES), F32)
     flat_vec = (flow_state.shape, F32)
     stage = (SUB * SUB, LANES)
@@ -755,25 +769,23 @@
     def blocks(parts):
         return (rows * parts * tiles, LANES)
 
-    ints = ((flat, LANES), I32)
-    out0, send, flow, slopes, owner, neighbour, source = run(
+    ints = pltpu.VMEM((flat, LANES), I32)
+    packed = -(-BLOCK * (lists // 2) * (width // LANES) // SUB)
+    pack, out0, send, flow, source = run(
         start_kernel,
-        [full_block, ((2, SUB, LANES), I32), flat_vec, (face_normal.shape, F32), ints, ints, flat_vec],
-        [stage, pltpu.VMEM(send_list.shape, I32), pltpu.SMEM((lists,), I32), pltpu.SemaphoreType.DMA((7,))],
+        [((4, flat, LANES), F32), full_block, ((2 * packed, SUB, LANES), I32), flat_vec, flat_vec],
+        [
+            stage, pltpu.VMEM(send_list.shape, I32), pltpu.SMEM((lists,), I32),
+            face_normal.shape, ints, ints, pltpu.SemaphoreType.DMA((7,)),
+        ],
         (
-            halo_count, flow_state, send_list, face_normal,
+            face_count, halo_count, flow_state, send_list, face_normal,
             face_owner.reshape(flat, LANES), face_neighbour.reshape(flat, LANES), source_term,
         ),
+        scalars=1,
         away=7,
     )
     in0 = exchange(out0)
-    (pack,) = run(
-        functools.partial(pack_kernel, lists=lists, width=width, cells_here=cells_here),
-        [((4, flat, LANES), F32)],
-        [],
-        (face_count, slopes, owner, neighbour),
-        scalars=1,
-    )
     peer = lax.ppermute(pack, "faces", [(0, 1), (1, 0)])
     normal, link, order, last, lean, coupling = run(
         table_kernel,
@@ -816,11 +828,11 @@
     in4 = exchange(out4)
     field, premid, middle, second, out5 = run(
         functools.partial(fourth_kernel, shifts=shifts),
-        [vec, vec, vec, vec, sum_block],
+        [vec, vec, vec, vec, full_block],
         work[1:],
         (in4, scales, ghosts, field, residual, preres, predir, image, mimage) + fixed[:6],
     )
-    in5 = lax.all_to_all(out5, "cells", 0, 0)
+    in5 = exchange(out5)
     field, residual = run(last_kernel, [flat_vec, flat_vec], [(2,) + vector], (in5, field, premid, middle, second))
     return (field, residual)
 

time: 80.4 us -> 79.8 us (level)
  blocking collectives: 51 us -> 49.8 us
  waiting for transfers between devices: 4.32 us -> 5.15 us
    all_to_all x1 -> x0, blocking collectives: 10.3 us -> none  [body(): in5 = lax.all_to_all(out5, 'cells', 0, 0)]
    all_to_all x4 -> x5, blocking collectives: 40.7 us -> 49.8 us  [exchange(): return lax.all_to_all(block, ('cells', 'faces'), 0, 0)]
    all_to_all x1, waiting for transfers between devices: 3.13 us -> 3.96 us  [exchange(): return lax.all_to_all(block, ('cells', 'faces'), 0, 0)]
    pallas_call x9 -> x8, Pallas kernels: 15.9 us -> 15.5 us  [run(): pl.pallas_call(kernel, out_shape=[jax.ShapeDtypeStruct(shape, dtype) for...]
  transfers between devices with their start and end apart: 2 -> 2, of which waited for: 2 -> 2; matrix products, arithmetic and copies ran while one was open for 0% -> 0% of each run, Pallas kernels for 4% -> 3%
where the time goes in v5:
time: 79.8 us; the launch traced here: 79.5 us
  blocking collectives  49.8 us (62%)
  Pallas kernels  15.5 us (19%)
  starting transfers between devices  7.65 us (10%)
  waiting for transfers between devices  5.15 us (6%)
  between operations  1.32 us (2%)
    all_to_all x5, blocking collectives, exchange(): return lax.all_to_all(block, ('cells', 'faces'), 0, 0)  49.8 us
    pallas_call x8, Pallas kernels, run(): pl.pallas_call(kernel, out_shape=[jax.ShapeDtypeStruct(shape, dtype) for...  15.5 us
    all_to_all x1, starting transfers between devices, exchange(): return lax.all_to_all(block, ('cells', 'faces'), 0, 0)  7.33 us
    all_to_all x1, waiting for transfers between devices, exchange(): return lax.all_to_all(block, ('cells', 'faces'), 0, 0)  3.96 us
  transfers between devices with their start and end apart: 2, of which 2 were waited for; matrix products, arithmetic and copies ran while one was open for 0% of the time, Pallas kernels for 3%

profile of v5, /device:TPU:0, one launch (start us, length us, event | category | flops | bytes accessed | tf_op | source)
XLA Modules:
  0.0 79.5 jit_solution(11662253225301034726)
XLA Ops:
  1.3 2.1 %shard_map.104 = (f32[4,96,128]{2,1,0:T(8,128)S(1)}, f32[32,8,128]{2,1,0:T(8,128)}, s32[6,8,128]{2,1,0:T(8,128)S(1)}, f32[4,8192]{1,0:T(4,128)S(1)}, f32[4,8192]{1,0:T(4,128)S(1)}) custom-call(s32[1]{0:T(128)S(6)} %copy.11.count_ref, s32[6]{0:T(128)} %used_any.1, f32[4,8192]{1,0:T(4,128)} %flow_any.1, s32[6,256]{1,0:T(8,128)} %list_any.1, ...), custom_call_target="tpu_custom_call" | custom-call | tf_op jit(solution)/shard_map/pallas_call | solution.py:719
  3.3 7.3 %all-to-all-start = ((f32[32,8,128]{2,1,0:T(8,128)}), f32[32,8,128]{2,1,0:T(8,128)S(1)}, u32[]{:S(2)}, u32[]{:S(2)}) async-start(f32[32,8,128]{2,1,0:T(8,128)} %get-tuple-element.41), calls=%async_computation | async-start | bytes 262144 | tf_op jit(solution)/shard_map/all_to_all | solution.py:730
  10.7 0.3 collective-permute-start
  11.0 1.2 %collective-permute-done.peer_ref = f32[4,96,128]{2,1,0:T(8,128)S(1)} collective-permute-done((f32[4,96,128]{2,1,0:T(8,128)S(1)}, f32[4,96,128]{2,1,0:T(8,128)S(1)}, u32[]{:S(2)}, u32[]{:S(2)}) %collective-permute-start) | collective-permute-done | bytes 196640 | tf_op jit(solution)/shard_map/ppermute | solution.py:789
  12.2 0.0 copy-start
  12.2 2.7 %shard_map.105 = (f32[3,3,64,128]{3,2,1,0:T(8,128)S(1)}, s32[2,3,64,128]{3,2,1,0:T(8,128)S(1)}, s32[2,3,64,128]{3,2,1,0:T(8,128)S(1)}, s32[3,3,64,128]{3,2,1,0:T...) custom-call(f32[4,96,128]{2,1,0:T(8,128)S(1)} %get-tuple-element.43.mine_ref, ...), custom_call_target="tpu_custom_call" | custom-call | tf_op jit(solution)/shard_map/pallas_call | solution.py:719
  14.9 4.0 %all-to-all-done.in_ref = f32[32,8,128]{2,1,0:T(8,128)S(1)} async-done(((f32[32,8,128]{2,1,0:T(8,128)}), f32[32,8,128]{2,1,0:T(8,128)S(1)}, u32[]{:S(2)}, u32[]{:S(2)}) %all-to-all-start) | async-done | bytes 131104 | tf_op jit(solution)/shard_map/all_to_all | solution.py:730
  18.9 0.0 copy-done
  18.9 1.3 %shard_map.106 = (f32[2,3,64,128]{3,2,1,0:T(8,128)S(1)}, f32[5,64,128]{2,1,0:T(8,128)S(1)}, f32[4,64,128]{2,1,0:T(8,128)S(1)}, f32[4,64,128]{2,1,0:T(8,128)S(1)}, f32[32,8,128]{2,1,0:T(8,128)S(1)}) custom-call(f32[32,8,128]{2,1,0:T(8,128)S(1)} %all-to-all-done.in_ref, f32[4,8192]{1,0:T(4,128)S(1)} %get-tuple-element.42.source_ref, f32[64,128]{1,0:T(8,128)S(1)} %bitcast.3, ...), custom_call_target="tpu_custom_call" | custom-call | tf_op jit(solution)/shard_map/pallas_call | solution.py:719
  20.2 10.0 %all_to_all.30.in_ref.in1_ref = f32[32,8,128]{2,1,0:T(8,128)S(1)} all-to-all(f32[32,8,128]{2,1,0:T(8,128)S(1)} %get-tuple-element.52), channel_id=1, replica_groups=mesh['cells'=16,'faces'=2] {'cells','faces'}, dimensions={0} | all-to-all | bytes 262144 | tf_op jit(solution)/shard_map/all_to_all | solution.py:730
  30.2 2.0 %shard_map.107 = (f32[4,64,128]{2,1,0:T(8,128)S(1)}, f32[4,64,128]{2,1,0:T(8,128)S(1)}, f32[32,8,128]{2,1,0:T(8,128)S(1)}) custom-call(f32[32,8,128]{2,1,0:T(8,128)S(1)} %all_to_all.30.in_ref.in1_ref, f32[4,64,128]{2,1,0:T(8,128)S(1)} %get-tuple-element.53.pre_ref, f32[4,64,128]{2,1,0:T(8,128)S(1)} %get-tuple-element.54.source_ref, f32[64,128]{1,0:T(8,128)S(1)} %bitcast.4, ...), custom_call_target="tpu_custom_call" | custom-call | tf_op jit(solution)/shard_map/pallas_call | solution.py:719
  32.2 10.0 %all_to_all.31.in2_ref = f32[32,8,128]{2,1,0:T(8,128)S(1)} all-to-all(f32[32,8,128]{2,1,0:T(8,128)S(1)} %get-tuple-element.57), channel_id=1, replica_groups=mesh['cells'=16,'faces'=2] {'cells','faces'}, dimensions={0} | all-to-all | bytes 262144 | tf_op jit(solution)/shard_map/all_to_all | solution.py:730
  42.2 2.2 %shard_map.108 = (f32[4,64,128]{2,1,0:T(8,128)S(1)}, f32[4,64,128]{2,1,0:T(8,128)S(1)}, f32[4,64,128]{2,1,0:T(8,128)S(1)}, f32[4,64,128]{2,1,0:T(8,128)S(1)}, f3...) custom-call(f32[32,8,128]{2,1,0:T(8,128)S(1)} %all_to_all.30.in_ref.in1_ref, f32[32,8,128]{2,1,0:T(8,128)S(1)} %all_to_all.31.in2_ref, ...), custom_call_target="tpu_custom_call" | custom-call | tf_op jit(solution)/shard_map/pallas_call | solution.py:719
  44.4 10.0 %all_to_all.32.in3_ref = f32[32,8,128]{2,1,0:T(8,128)S(1)} all-to-all(f32[32,8,128]{2,1,0:T(8,128)S(1)} %get-tuple-element.60), channel_id=1, replica_groups=mesh['cells'=16,'faces'=2] {'cells','faces'}, dimensions={0} | all-to-all | bytes 262144 | tf_op jit(solution)/shard_map/all_to_all | solution.py:730
  54.3 2.2 %shard_map.109 = (f32[4,64,128]{2,1,0:T(8,128)S(1)}, f32[4,64,128]{2,1,0:T(8,128)S(1)}, f32[4,64,128]{2,1,0:T(8,128)S(1)}, f32[4,64,128]{2,1,0:T(8,128)S(1)}, f3...) custom-call(f32[32,8,128]{2,1,0:T(8,128)S(1)} %all_to_all.30.in_ref., ...), custom_call_target="tpu_custom_call" | custom-call | tf_op jit(solution)/shard_map/pallas_call | solution.py:719
  56.5 10.0 %all_to_all.33.in4_ref = f32[32,8,128]{2,1,0:T(8,128)S(1)} all-to-all(f32[32,8,128]{2,1,0:T(8,128)S(1)} %get-tuple-element.66), channel_id=1, replica_groups=mesh['cells'=16,'faces'=2] {'cells','faces'}, dimensions={0} | all-to-all | bytes 262144 | tf_op jit(solution)/shard_map/all_to_all | solution.py:730
  66.5 2.0 %shard_map.110 = (f32[4,64,128]{2,1,0:T(8,128)S(1)}, f32[4,64,128]{2,1,0:T(8,128)S(1)}, f32[4,64,128]{2,1,0:T(8,128)S(1)}, f32[4,64,128]{2,1,0:T(8,128)S(1)}, f32[32,8,128]{2,1,0:T(8,128)S(1)}) custom-call(f32[32,8,128]{2,1,0:T(8,128)S(1)} %all_to_all.33.in4_ref, f32[8,128]{1,0:T(8,128)S(1)} %get-tuple-element.67.scale_ref, ...), custom_call_target="tpu_custom_call" | custom-call | tf_op jit(solution)/shard_map/pallas_call | solution.py:719
  68.5 10.0 %all_to_all.34.in_ref = f32[32,8,128]{2,1,0:T(8,128)S(1)} all-to-all(f32[32,8,128]{2,1,0:T(8,128)S(1)} %get-tuple-element.75), channel_id=1, replica_groups=mesh['cells'=16,'faces'=2] {'cells','faces'}, dimensions={0} | all-to-all | bytes 262144 | tf_op jit(solution)/shard_map/all_to_all | solution.py:730
  78.5 1.0 %shard_map.111 = (f32[4,8192]{1,0:T(4,128)}, f32[4,8192]{1,0:T(4,128)}) custom-call(f32[32,8,128]{2,1,0:T(8,128)S(1)} %all_to_all.34.in_ref, f32[4,64,128]{2,1,0:T(8,128)S(1)} %get-tuple-element.76.field_ref, f32[4,64,128]{2,1,0:T(8,128)S(1)} %get-tuple-element.77.premid_ref, f32[4,64,128]{2,1,0:T(8,128)S(1)} %get-tuple-element.78.middle_ref, ...), custom_call_target="tpu_custom_call" | custom-call | tf_op jit(solution)/shard_map/pallas_call | solution.py:719
Async XLA Ops:
  3.3 15.5 %all-to-all-start = ((f32[32,8,128]{2,1,0:T(8,128)}), f32[32,8,128]{2,1,0:T(8,128)S(1)}, u32[]{:S(2)}, u32[]{:S(2)}) async-start(f32[32,8,128]{2,1,0:T(8,128)} %get-tuple-element.41), calls=%async_computation | async-start | bytes 262144 | tf_op jit(solution)/shard_map/all_to_all | solution.py:730
  10.7 1.5 %collective-permute-start = (f32[4,96,128]{2,1,0:T(8,128)S(1)}, f32[4,96,128]{2,1,0:T(8,128)S(1)}, u32[]{:S(2)}, u32[]{:S(2)}) collective-permute-start(f32[4,96,128]{2,1,0:T(8,128)S(1)} %get-tuple-element.43.mine_ref), channel_id=1, source_target_pairs={{0,1},{1,0},{2,3},{3,2},{4,5},{5,4},{6,7},{7,6},{8,9},{9,8},{10,11... | collective-permute-start | bytes 589832 | tf_op jit(solution)/shard_map/ppermute | solution.py:789
  12.2 6.7 %copy-start = (f32[8192]{0:T(1024)S(1)}, f32[8192]{0:T(1024)}, u32[]{:S(2)}) copy-start(f32[8192]{0:T(1024)} %param.11) | copy-start | bytes 98308

commit v6 on v5

--- a/solution.py
+++ b/solution.py
@@ -666,13 +666,20 @@
     send_halo(listed(tiled_rows(mimage_out), tiles, send_ref, len(shifts) // 2 * (SUB // BLOCK)), stage_ref, out_ref, len(shifts) // 2)
 
 
+def flatten(out_ref, ref, g):
+    for t in range(g * SUB, g * SUB + SUB):
+        for c in range(BLOCK):
+            out_ref[c : c + 1, t * LANES : (t + 1) * LANES] = ref[c, t : t + 1, :]
+
+
 def fourth_kernel(
     in4_ref, scale_ref, ghost_ref, field_ref, residual_ref, preres_ref, predir_ref, image_ref, mimage_ref,
     volume_ref, normal_ref, pair_ref, link_ref, order_ref, last_ref,
-    field_out, premid_ref, middle_ref, second_ref, out_ref,
-    halo_ref, wide_ref, here_ref, beside_ref, flux_ref, sort_ref, *, shifts,
+    field_flat, premid_flat, middle_flat, second_flat, out_ref,
+    stage_ref, halo_ref, wide_ref, here_ref, beside_ref, flux_ref, sort_ref, *, shifts,
 ):
     tiles = volume_ref.shape[0]
+    field_out, premid_ref, middle_ref, second_ref = [stage_ref.at[i] for i in range(4)]
     groups = in_groups(tiles)
     alpha = row_of(scale_ref, 0) / spread(got_sums(in4_ref, len(shifts) // 2), 0)
     for g in groups:
@@ -681,6 +688,9 @@
         put(premid_ref, g, premid)
         put(field_out, g, combine((None, alpha), (cell(field_ref, g), cell(predir_ref, g))))
         put(middle_ref, g, combine((None, -alpha), (cell(residual_ref, g), cell(image_ref, g))))
+        flatten(field_flat, field_out, g)
+        flatten(premid_flat, premid_ref, g)
+        flatten(middle_flat, middle_ref, g)
     widen(wide_ref, tiles)
     ghosts = [ghost_ref[k] for k in range(len(shifts))]
     lay_halo(combine((None, -alpha), (ghosts, got_halo(in4_ref, shifts))), halo_ref)
@@ -690,24 +700,17 @@
     for g in groups:
         second = applied(g, volume_ref, wide_ref, here_ref, beside_ref)
         put(second_ref, g, second)
+        flatten(second_flat, second_ref, g)
         cross = added(cross, second, cell(middle_ref, g))
         square = added(square, second, second)
     send_sums((cross, square), out_ref)
 
 
-def last_kernel(in_ref, field_ref, premid_ref, middle_ref, second_ref, field_out, residual_out, stage_ref):
-    tiles = field_ref.shape[1]
+def last_kernel(in_ref, field_ref, premid_ref, middle_ref, second_ref, field_out, residual_out):
     sums = total_of([in_ref[d] for d in range(0, in_ref.shape[0], lax.axis_size("faces"))])
-    omega = spread(sums, 0) / spread(sums, 1)
-    for g in in_groups(tiles):
-        field = combine((None, omega), (cell(field_ref, g), cell(premid_ref, g)))
-        residual = combine((None, -omega), (cell(middle_ref, g), cell(second_ref, g)))
-        put(stage_ref.at[0], g, field)
-        put(stage_ref.at[1], g, residual)
-        for i, out in enumerate((field_out, residual_out)):
-            for t in range(g * SUB, g * SUB + SUB):
-                for c in range(BLOCK):
-                    out[c : c + 1, t * LANES : (t + 1) * LANES] = stage_ref[i, c, t : t + 1, :]
+    omega = sums[0:1, :] / sums[1:2, :]
+    field_out[...] = field_ref[...] + omega * premid_ref[...]
+    residual_out[...] = middle_ref[...] - omega * second_ref[...]
 
 
 def run(kernel, outs, scratch, args, scalars=0, away=0):
@@ -828,12 +831,12 @@
     in4 = exchange(out4)
     field, premid, middle, second, out5 = run(
         functools.partial(fourth_kernel, shifts=shifts),
-        [vec, vec, vec, vec, full_block],
-        work[1:],
+        [flat_vec] * 4 + [full_block],
+        [(4,) + vector] + work[1:],
         (in4, scales, ghosts, field, residual, preres, predir, image, mimage) + fixed[:6],
     )
     in5 = exchange(out5)
-    field, residual = run(last_kernel, [flat_vec, flat_vec], [(2,) + vector], (in5, field, premid, middle, second))
+    field, residual = run(last_kernel, [flat_vec, flat_vec], [], (in5, field, premid, middle, second))
     return (field, residual)
 
 

time: 79.8 us -> 79.8 us (level)
  no operation moved by 1% of the time
where the time goes in v6:
time: 79.8 us; the launch traced here: 79.5 us
  blocking collectives  49.8 us (62%)
  Pallas kernels  15.6 us (20%)
  starting transfers between devices  7.65 us (10%)
  waiting for transfers between devices  5.15 us (6%)
  between operations  1.32 us (2%)
    all_to_all x5, blocking collectives, exchange(): return lax.all_to_all(block, ('cells', 'faces'), 0, 0)  49.8 us
    pallas_call x8, Pallas kernels, run(): pl.pallas_call(kernel, out_shape=[jax.ShapeDtypeStruct(shape, dtype) for...  15.6 us
    all_to_all x1, starting transfers between devices, exchange(): return lax.all_to_all(block, ('cells', 'faces'), 0, 0)  7.33 us
    all_to_all x1, waiting for transfers between devices, exchange(): return lax.all_to_all(block, ('cells', 'faces'), 0, 0)  3.96 us
  transfers between devices with their start and end apart: 2, of which 2 were waited for; matrix products, arithmetic and copies ran while one was open for 0% of the time, Pallas kernels for 3%

profile of v6, /device:TPU:0, one launch (start us, length us, event | category | flops | bytes accessed | tf_op | source)
XLA Modules:
  0.0 79.5 jit_solution(3665295954824475151)
XLA Ops:
  1.3 2.1 %shard_map.104 = (f32[4,96,128]{2,1,0:T(8,128)S(1)}, f32[32,8,128]{2,1,0:T(8,128)}, s32[6,8,128]{2,1,0:T(8,128)S(1)}, f32[4,8192]{1,0:T(4,128)S(1)}, f32[4,8192]{1,0:T(4,128)S(1)}) custom-call(s32[1]{0:T(128)S(6)} %copy.11.count_ref, s32[6]{0:T(128)} %used_any.1, f32[4,8192]{1,0:T(4,128)} %flow_any.1, s32[6,256]{1,0:T(8,128)} %list_any.1, ...), custom_call_target="tpu_custom_call" | custom-call | tf_op jit(solution)/shard_map/pallas_call | solution.py:722
  3.3 7.3 %all-to-all-start = ((f32[32,8,128]{2,1,0:T(8,128)}), f32[32,8,128]{2,1,0:T(8,128)S(1)}, u32[]{:S(2)}, u32[]{:S(2)}) async-start(f32[32,8,128]{2,1,0:T(8,128)} %get-tuple-element.41), calls=%async_computation | async-start | bytes 262144 | tf_op jit(solution)/shard_map/all_to_all | solution.py:733
  10.7 0.3 collective-permute-start
  11.0 1.2 %collective-permute-done.peer_ref = f32[4,96,128]{2,1,0:T(8,128)S(1)} collective-permute-done((f32[4,96,128]{2,1,0:T(8,128)S(1)}, f32[4,96,128]{2,1,0:T(8,128)S(1)}, u32[]{:S(2)}, u32[]{:S(2)}) %collective-permute-start) | collective-permute-done | bytes 196640 | tf_op jit(solution)/shard_map/ppermute | solution.py:792
  12.2 0.0 copy-start
  12.2 2.7 %shard_map.105 = (f32[3,3,64,128]{3,2,1,0:T(8,128)S(1)}, s32[2,3,64,128]{3,2,1,0:T(8,128)S(1)}, s32[2,3,64,128]{3,2,1,0:T(8,128)S(1)}, s32[3,3,64,128]{3,2,1,0:T...) custom-call(f32[4,96,128]{2,1,0:T(8,128)S(1)} %get-tuple-element.43.mine_ref, ...), custom_call_target="tpu_custom_call" | custom-call | tf_op jit(solution)/shard_map/pallas_call | solution.py:722
  14.9 4.0 %all-to-all-done.in_ref = f32[32,8,128]{2,1,0:T(8,128)S(1)} async-done(((f32[32,8,128]{2,1,0:T(8,128)}), f32[32,8,128]{2,1,0:T(8,128)S(1)}, u32[]{:S(2)}, u32[]{:S(2)}) %all-to-all-start) | async-done | bytes 131104 | tf_op jit(solution)/shard_map/all_to_all | solution.py:733
  18.9 0.0 copy-done
  18.9 1.3 %shard_map.106 = (f32[2,3,64,128]{3,2,1,0:T(8,128)S(1)}, f32[5,64,128]{2,1,0:T(8,128)S(1)}, f32[4,64,128]{2,1,0:T(8,128)S(1)}, f32[4,64,128]{2,1,0:T(8,128)S(1)}, f32[32,8,128]{2,1,0:T(8,128)S(1)}) custom-call(f32[32,8,128]{2,1,0:T(8,128)S(1)} %all-to-all-done.in_ref, f32[4,8192]{1,0:T(4,128)S(1)} %get-tuple-element.42.source_ref, f32[64,128]{1,0:T(8,128)S(1)} %bitcast.3, ...), custom_call_target="tpu_custom_call" | custom-call | tf_op jit(solution)/shard_map/pallas_call | solution.py:722
  20.2 10.0 %all_to_all.30.in_ref.in1_ref = f32[32,8,128]{2,1,0:T(8,128)S(1)} all-to-all(f32[32,8,128]{2,1,0:T(8,128)S(1)} %get-tuple-element.52), channel_id=1, replica_groups=mesh['cells'=16,'faces'=2] {'cells','faces'}, dimensions={0} | all-to-all | bytes 262144 | tf_op jit(solution)/shard_map/all_to_all | solution.py:733
  30.2 2.0 %shard_map.107 = (f32[4,64,128]{2,1,0:T(8,128)S(1)}, f32[4,64,128]{2,1,0:T(8,128)S(1)}, f32[32,8,128]{2,1,0:T(8,128)S(1)}) custom-call(f32[32,8,128]{2,1,0:T(8,128)S(1)} %all_to_all.30.in_ref.in1_ref, f32[4,64,128]{2,1,0:T(8,128)S(1)} %get-tuple-element.53.pre_ref, f32[4,64,128]{2,1,0:T(8,128)S(1)} %get-tuple-element.54.source_ref, f32[64,128]{1,0:T(8,128)S(1)} %bitcast.4, ...), custom_call_target="tpu_custom_call" | custom-call | tf_op jit(solution)/shard_map/pallas_call | solution.py:722
  32.2 10.0 %all_to_all.31.in2_ref = f32[32,8,128]{2,1,0:T(8,128)S(1)} all-to-all(f32[32,8,128]{2,1,0:T(8,128)S(1)} %get-tuple-element.57), channel_id=1, replica_groups=mesh['cells'=16,'faces'=2] {'cells','faces'}, dimensions={0} | all-to-all | bytes 262144 | tf_op jit(solution)/shard_map/all_to_all | solution.py:733
  42.2 2.2 %shard_map.108 = (f32[4,64,128]{2,1,0:T(8,128)S(1)}, f32[4,64,128]{2,1,0:T(8,128)S(1)}, f32[4,64,128]{2,1,0:T(8,128)S(1)}, f32[4,64,128]{2,1,0:T(8,128)S(1)}, f3...) custom-call(f32[32,8,128]{2,1,0:T(8,128)S(1)} %all_to_all.30.in_ref.in1_ref, f32[32,8,128]{2,1,0:T(8,128)S(1)} %all_to_all.31.in2_ref, ...), custom_call_target="tpu_custom_call" | custom-call | tf_op jit(solution)/shard_map/pallas_call | solution.py:722
  44.4 10.0 %all_to_all.32.in3_ref = f32[32,8,128]{2,1,0:T(8,128)S(1)} all-to-all(f32[32,8,128]{2,1,0:T(8,128)S(1)} %get-tuple-element.60), channel_id=1, replica_groups=mesh['cells'=16,'faces'=2] {'cells','faces'}, dimensions={0} | all-to-all | bytes 262144 | tf_op jit(solution)/shard_map/all_to_all | solution.py:733
  54.3 2.2 %shard_map.109 = (f32[4,64,128]{2,1,0:T(8,128)S(1)}, f32[4,64,128]{2,1,0:T(8,128)S(1)}, f32[4,64,128]{2,1,0:T(8,128)S(1)}, f32[4,64,128]{2,1,0:T(8,128)S(1)}, f3...) custom-call(f32[32,8,128]{2,1,0:T(8,128)S(1)} %all_to_all.30.in_ref., ...), custom_call_target="tpu_custom_call" | custom-call | tf_op jit(solution)/shard_map/pallas_call | solution.py:722
  56.5 10.0 %all_to_all.33.in4_ref = f32[32,8,128]{2,1,0:T(8,128)S(1)} all-to-all(f32[32,8,128]{2,1,0:T(8,128)S(1)} %get-tuple-element.66), channel_id=1, replica_groups=mesh['cells'=16,'faces'=2] {'cells','faces'}, dimensions={0} | all-to-all | bytes 262144 | tf_op jit(solution)/shard_map/all_to_all | solution.py:733
  66.5 2.2 %shard_map.110 = (f32[4,8192]{1,0:T(4,128)S(1)}, f32[4,8192]{1,0:T(4,128)S(1)}, f32[4,8192]{1,0:T(4,128)S(1)}, f32[4,8192]{1,0:T(4,128)S(1)}, f32[32,8,128]{2,1,0:T(8,128)S(1)}) custom-call(f32[32,8,128]{2,1,0:T(8,128)S(1)} %all_to_all.33.in4_ref, f32[8,128]{1,0:T(8,128)S(1)} %get-tuple-element.67.scale_ref, f32[6,8,128]{2,1,0:T(8,128)S(1)} %get-tuple-element.68.ghost_ref, ...), custom_call_target="tpu_custom_call" | custom-call | tf_op jit(solution)/shard_map/pallas_call | solution.py:722
  68.7 10.0 %all_to_all.34.in_ref = f32[32,8,128]{2,1,0:T(8,128)S(1)} all-to-all(f32[32,8,128]{2,1,0:T(8,128)S(1)} %get-tuple-element.75), channel_id=1, replica_groups=mesh['cells'=16,'faces'=2] {'cells','faces'}, dimensions={0} | all-to-all | bytes 262144 | tf_op jit(solution)/shard_map/all_to_all | solution.py:733
  78.7 0.8 %shard_map.111 = (f32[4,8192]{1,0:T(4,128)}, f32[4,8192]{1,0:T(4,128)}) custom-call(f32[32,8,128]{2,1,0:T(8,128)S(1)} %all_to_all.34.in_ref, f32[4,8192]{1,0:T(4,128)S(1)} %get-tuple-element.76.field_ref, f32[4,8192]{1,0:T(4,128)S(1)} %get-tuple-element.77.premid_ref, f32[4,8192]{1,0:T(4,128)S(1)} %get-tuple-element.78.middle_ref, ...), custom_call_target="tpu_custom_call" | custom-call | tf_op jit(solution)/shard_map/pallas_call | solution.py:722
Async XLA Ops:
  3.3 15.5 %all-to-all-start = ((f32[32,8,128]{2,1,0:T(8,128)}), f32[32,8,128]{2,1,0:T(8,128)S(1)}, u32[]{:S(2)}, u32[]{:S(2)}) async-start(f32[32,8,128]{2,1,0:T(8,128)} %get-tuple-element.41), calls=%async_computation | async-start | bytes 262144 | tf_op jit(solution)/shard_map/all_to_all | solution.py:733
  10.7 1.5 %collective-permute-start = (f32[4,96,128]{2,1,0:T(8,128)S(1)}, f32[4,96,128]{2,1,0:T(8,128)S(1)}, u32[]{:S(2)}, u32[]{:S(2)}) collective-permute-start(f32[4,96,128]{2,1,0:T(8,128)S(1)} %get-tuple-element.43.mine_ref), channel_id=1, source_target_pairs={{0,1},{1,0},{2,3},{3,2},{4,5},{5,4},{6,7},{7,6},{8,9},{9,8},{10,11... | collective-permute-start | bytes 589832 | tf_op jit(solution)/shard_map/ppermute | solution.py:792
  12.2 6.7 %copy-start = (f32[8192]{0:T(1024)S(1)}, f32[8192]{0:T(1024)}, u32[]{:S(2)}) copy-start(f32[8192]{0:T(1024)} %param.11) | copy-start | bytes 98308
